TPU v7x, 32 devices: a whole 2x2x4 slice. The times are simulated.
32 devices in a mesh: vid: 4 (over z), th: 4 (over x, core), tw: 2 (over y).
Axes of the slice: x: 2, y: 2, z: 4, core: 2. Of those that a mesh axis runs over, the one named last changes fastest.
Arguments:
- queries: bfloat16 [16, 32, 6, 3072], P('vid', 'th', 'tw'), parts along dimension 0, may hold values from -70 to 70
- video_kv: bfloat16 [2, 16, 32, 6, 3072], P(None, 'vid', 'th', 'tw'), parts along dimension 1, may hold values from -6 to 6
- text_kv: bfloat16 [2, 904, 3072], P(None, 'vid', 'tw'), parts along dimension 1, may hold values from -6 to 6
- time_embed: bfloat16 [2048], P('vid'), parts along dimension 0, may hold values from -6 to 6
- gate_weight: bfloat16 [512, 3072], P(None, 'tw'), may hold values from -0.25 to 0.25
- window_extent: int32 [48, 2], replicated, may hold values from 1 to 3
- tile_valid: int32 [16, 2, 2], P('vid'), parts along dimension 0, may hold values from 2 to 8, as said below
Outputs:
- gated: bfloat16 [16, 32, 6, 3072], P('vid', 'th', 'tw'), parts along dimension 0
There are 4 independent parts, one for each index of `vid`. A program takes and returns all parts, laid end to end along the dimension named above; an argument that names none is the same for every part. Nothing has to cross between parts.
Inputs may be any that keep to these rules, and one draw needn't show every extreme that they name: Tile (i, j) holds tokens in its leading tile_valid[i, j, 0] of 8 rows and leading tile_valid[i, j, 1] of 3 columns; its other slots are padding. Some tile is full in every draw.
All inputs are finite; a program needn't handle non-finite values.
Results may differ from a plain program's by a relative error of at most 0.0063.
Values may be sent and summed in bfloat16 or wider, within the bound.
No kernel may reach another device: no remote copies, remote signals or barrier semaphores. Data moves between devices by JAX's collectives and lax.ppermute only.
A program may use at most 128 MiB of HBM per device.

v0:
```python
import math

import jax
import jax.numpy as jnp
from jax import lax
from jax.sharding import PartitionSpec as P

HEAD_DIM = 64
HALO = 3


NEG = -1e30


def extended(cells, sides, width):
    for axis, dim in sides:
        count = lax.axis_size(axis)
        ends = count - 1
        head = lax.slice_in_dim(cells, 0, width, axis=dim)
        tail = lax.slice_in_dim(cells, cells.shape[dim] - width, cells.shape[dim], axis=dim)
        cells = jnp.concatenate(
            [
                lax.ppermute(tail, axis, [(i, (i + 1) % count) for i in range(ends)]),
                cells,
                lax.ppermute(head, axis, [((i + 1) % count, i) for i in range(ends)]),
            ],
            axis=dim,
        )
    return cells


def key_validity(tile_valid, row_at, col_at, tile_rows, tile_cols):
    tiles_down = tile_valid.shape[0]
    tiles_across = tile_valid.shape[1]
    glob_row = row_at * tile_rows + jnp.arange(tile_rows + 2 * HALO, dtype=jnp.int32) - HALO
    glob_col = col_at * tile_cols + jnp.arange(tile_cols + 2 * HALO, dtype=jnp.int32) - HALO
    tile_row = jnp.floor_divide(glob_row, tile_rows)
    tile_col = jnp.floor_divide(glob_col, tile_cols)
    pick_row = (tile_row[:, None] == jnp.arange(tiles_down, dtype=jnp.int32)[None, :]).astype(
        jnp.float32
    )
    pick_col = (tile_col[:, None] == jnp.arange(tiles_across, dtype=jnp.int32)[None, :]).astype(
        jnp.float32
    )
    table = tile_valid.astype(jnp.float32)
    high = lax.Precision.HIGHEST
    limit_rows = jnp.dot(
        jnp.dot(pick_row, table[..., 0], precision=high), pick_col.T, precision=high
    )
    limit_cols = jnp.dot(
        jnp.dot(pick_row, table[..., 1], precision=high), pick_col.T, precision=high
    )
    local_row = (glob_row - tile_row * tile_rows).astype(jnp.float32)
    local_col = (glob_col - tile_col * tile_cols).astype(jnp.float32)
    return (local_row[:, None] < limit_rows) & (local_col[None, :] < limit_cols)


def video_part(
    query_rows,
    video_keys,
    video_values,
    key_ok,
    window_extent,
    frames,
    tile_rows,
    tile_cols,
    score_scale,
):
    count_q, head_count, head_depth = query_rows.shape
    count_k = video_keys.shape[0]
    span_rows = tile_rows + 2 * HALO
    span_cols = tile_cols + 2 * HALO
    per_turn = math.gcd(head_count, 4)
    query_ids = jnp.arange(count_q, dtype=jnp.int32)
    key_ids = jnp.arange(count_k, dtype=jnp.int32)
    query_row = query_ids // tile_cols % tile_rows
    query_col = query_ids % tile_cols
    key_row = key_ids // span_cols % span_rows
    key_col = key_ids % span_cols
    row_gap = jnp.abs(key_row[None, :] - query_row[:, None] - HALO)
    col_gap = jnp.abs(key_col[None, :] - query_col[:, None] - HALO)
    key_flat = jnp.tile(key_ok.reshape(-1), frames)

    def one_group(turn_index, carry):
        video_out, video_max, video_total = carry
        first_head = jnp.asarray(turn_index, jnp.int32) * per_turn
        query_part = lax.dynamic_slice_in_dim(query_rows, first_head, per_turn, 1)
        key_part = lax.dynamic_slice_in_dim(video_keys, first_head, per_turn, 1)
        value_part = lax.dynamic_slice_in_dim(video_values, first_head, per_turn, 1)
        extents = lax.dynamic_slice_in_dim(window_extent, first_head, per_turn, 0)
        allowed = (
            (row_gap[None] <= extents[:, 0][:, None, None])
            & (col_gap[None] <= extents[:, 1][:, None, None])
            & key_flat[None, None, :]
        )
        scores = (
            jnp.einsum("nhd,khd->hnk", query_part, key_part, preferred_element_type=jnp.float32)
            * score_scale
        )
        scores = jnp.where(allowed, scores, NEG)
        maximum = jnp.max(scores, axis=-1)
        exp_terms = jnp.where(allowed, jnp.exp(scores - maximum[..., None]), 0.0)
        totals = jnp.sum(exp_terms, axis=-1)
        weights = exp_terms.astype(jnp.bfloat16)
        partial_value = jnp.einsum(
            "hnk,khd->nhd", weights, value_part, preferred_element_type=jnp.float32
        )
        video_out = lax.dynamic_update_slice_in_dim(video_out, partial_value, first_head, 1)
        video_max = lax.dynamic_update_slice_in_dim(video_max, maximum, first_head, 0)
        video_total = lax.dynamic_update_slice_in_dim(video_total, totals, first_head, 0)
        return (video_out, video_max, video_total)

    initial = (
        jnp.zeros((count_q, head_count, head_depth), jnp.float32),
        jnp.zeros((head_count, count_q), jnp.float32),
        jnp.zeros((head_count, count_q), jnp.float32),
    )
    return lax.fori_loop(0, head_count // per_turn, one_group, initial)


def text_part(query_rows, text_keys, text_values, score_scale):
    scores = (
        jnp.einsum("nhd,thd->nht", query_rows, text_keys, preferred_element_type=jnp.float32)
        * score_scale
    )
    maximum = jnp.max(scores, axis=-1)
    exp_terms = jnp.exp(scores - maximum[..., None])
    totals = jnp.sum(exp_terms, axis=-1)
    partial_value = jnp.einsum(
        "nht,thd->nhd",
        exp_terms.astype(jnp.bfloat16),
        text_values,
        preferred_element_type=jnp.float32,
    )
    return (partial_value, maximum, totals)


def combine(video_out, video_max, video_total, text_out, text_max, text_total):
    max_v = video_max.T
    total_v = video_total.T
    joint_max = jnp.maximum(max_v, text_max)
    scale_v = jnp.exp(max_v - joint_max)
    scale_t = jnp.exp(text_max - joint_max)
    denom = total_v * scale_v + text_total * scale_t
    return (video_out * scale_v[..., None] + text_out * scale_t[..., None]) / denom[..., None]


def attend_tile(
    query_block,
    kv_block,
    text_keys,
    text_values,
    extents,
    gate_vec,
    key_ok,
    tile_rows,
    tile_cols,
    score_scale,
):
    frames = query_block.shape[0]
    width = query_block.shape[3]
    head_count = width // HEAD_DIM
    query_rows = query_block.reshape(-1, head_count, HEAD_DIM)
    video_keys = kv_block[0].reshape(-1, head_count, HEAD_DIM)
    video_values = kv_block[1].reshape(-1, head_count, HEAD_DIM)
    video_out, video_max, video_total = video_part(
        query_rows,
        video_keys,
        video_values,
        key_ok,
        extents,
        frames,
        tile_rows,
        tile_cols,
        score_scale,
    )
    text_out, text_max, text_total = text_part(query_rows, text_keys, text_values, score_scale)
    attended = combine(video_out, video_max, video_total, text_out, text_max, text_total)
    attended = attended.reshape(frames, tile_rows, tile_cols, width)
    query_ok = key_ok[HALO : HALO + tile_rows, HALO : HALO + tile_cols]
    result = jnp.where(query_ok[None, :, :, None], gate_vec.astype(jnp.float32) * attended, 0.0)
    return result.astype(jnp.bfloat16)


def body(queries, video_kv, text_kv, time_embed, gate_weight, window_extent, tile_valid):
    frames, tile_rows, tile_cols, model_width = queries.shape
    head_count = model_width // HEAD_DIM
    score_scale = HEAD_DIM ** (-0.5)
    text_count = text_kv.shape[1]
    row_at = lax.axis_index("th")
    col_at = lax.axis_index("tw")
    mod_in = jax.nn.silu(time_embed.astype(jnp.float32)).astype(jnp.bfloat16)
    gate_part = jnp.dot(mod_in[None, :], gate_weight, preferred_element_type=jnp.float32)[0].astype(
        jnp.bfloat16
    )
    padded = extended(video_kv, (("th", 2), ("tw", 3)), HALO)
    text_full, gate_full = (
        lax.all_gather(text_kv, "tw", axis=2, tiled=True),
        lax.all_gather(gate_part, "tw", axis=0, tiled=True),
    )
    text_keys = text_full[0].reshape(text_count, head_count, HEAD_DIM)
    text_values = text_full[1].reshape(text_count, head_count, HEAD_DIM)
    key_ok = key_validity(tile_valid, row_at, col_at, tile_rows, tile_cols)
    return attend_tile(
        queries,
        padded,
        text_keys,
        text_values,
        window_extent,
        gate_full,
        key_ok,
        tile_rows,
        tile_cols,
        score_scale,
    )


def solution(mesh):
    placed = (
        P("vid", "th", "tw", None),
        P(None, "vid", "th", "tw", None),
        P(None, "vid", "tw"),
        P("vid"),
        P(None, "tw"),
        P(),
        P("vid", None, None),
    )
    return jax.shard_map(
        body, mesh=mesh, in_specs=placed, out_specs=P("vid", "th", "tw", None), check_vma=False
    )
```

profile of v0, /device:TPU:1, one launch (start us, length us, event | category | flops | bytes accessed | tf_op | source)
XLA Modules:
  0.0 264.3 jit_solution(14702985069549406135)
XLA Ops:
  9.1 4.5 %collective-permute-start = (bf16[2,4,3,3,3072]{4,1,3,2,0:T(4,128)(2,1)S(1)}, bf16[2,4,3,3,3072]{4,1,3,2,0:T(4,128)(2,1)S(1)}, u32[]{:S(2)}, u32[]{:S(2)}) collective-permute-start(bf16[2,4,3,3,3072]{4,1,3,2,0:T(4,128)(2,1)S(1)} %copy.61), channel_id=1, source_target_pairs={{0,2},{2,4},{4,6},{1,3},{3,5},{5,7},{8,10},{10,12},{12,14},{9,11},... | collective-permute-start | bytes 1327112 | tf_op jit(solution)/shard_map/ppermute | solution.py:23
  15.8 3.0 %collective-permute-done = bf16[2,4,3,3,3072]{4,1,3,2,0:T(4,128)(2,1)S(1)} collective-permute-done((bf16[2,4,3,3,3072]{4,1,3,2,0:T(4,128)(2,1)S(1)}, bf16[2,4,3,3,3072]{4,1,3,2,0:T(4,128)(2,1)S(1)}, u32[]{:S(2)}, u32[]{:S(2)}) %collective-permute-start) | collective-permute-done | bytes 442400 | tf_op jit(solution)/shard_map/ppermute | solution.py:23
  19.1 4.4 %collective-permute-done.1 = bf16[2,4,3,3,3072]{4,1,3,2,0:T(4,128)(2,1)S(1)} collective-permute-done((bf16[2,4,3,3,3072]{4,1,3,2,0:T(4,128)(2,1)S(1)}, bf16[2,4,3,3,3072]{4,1,3,2,0:T(4,128)(2,1)S(1)}, u32[]{:S(2)}, u32[]{:S(2)}) %collective-permute-start.1) | collective-permute-done | bytes 442400 | tf_op jit(solution)/shard_map/ppermute | solution.py:25
  24.6 2.7 %pad_maximum_fusion.1 = bf16[2,4,14,3,3072]{4,2,3,1,0:T(8,128)(2,1)} fusion(bf16[2,4,3,3,3072]{4,2,3,1,0:T(4,128)(2,1)S(1)} %copy.48, bf16[2,4,8,3,3072]{4,2,3,1,0:T(8,128)(2,1)S(1)} %copy-done.3, bf16[2,4,3,3,3072]{4,2,3,1,0:T(4,128)(2,1)S(1)} %copy.47), kind=kLoop, calls=%fused_computation.33 | loop fusion | flops 6193152 | bytes 4128768 | tf_op jit(solution)/shard_map/concatenate | solution.py:21
  27.3 4.6 %collective-permute-start.2 = (bf16[2,4,14,3,3072]{4,2,3,1,0:T(8,128)(2,1)}, bf16[2,4,14,3,3072]{4,2,3,1,0:T(8,128)(2,1)}, u32[]{:S(2)}, u32[]{:S(2)}) collective-permute-start(bf16[2,4,14,3,3072]{4,2,3,1,0:T(8,128)(2,1)} %pad_maximum_fusion.1), channel_id=1, source_target_pairs={{0,1},{2,3},{4,5},{6,7},{8,9},{10,11},{12,13},{14,15},{16,17},{18,... | collective-permute-start | bytes 6193160 | tf_op jit(solution)/shard_map/ppermute | solution.py:23
  34.4 2.5 copy.50
  36.9 3.4 %reshape.132 = bf16[96,48,64]{2,1,0:T(8,128)(2,1)} reshape(bf16[4,8,3,3072]{3,2,1,0:T(4,128)(2,1)} %copy.50) | data formatting | bytes 1179648 | tf_op jit(solution)/shard_map/reshape | solution.py:163
  43.1 68.6 %all-gather = bf16[2,1,1536]{2,1,0:T(2,128)(2,1)S(1)} all-gather(bf16[1,1,1536]{2,1,0:T(2,128)(2,1)S(1)} %reshape.134), channel_id=1, replica_groups=mesh['vid'=4,'th'=4,'tw'=2] {'tw'}, dimensions={0}, use_global_device_ids=true | all-gather | bytes 9216 | tf_op jit(solution)/shard_map/all_gather | solution.py:199
  111.8 4.2 %pad_maximum_fusion = bf16[2,4,14,9,3072]{4,2,3,1,0:T(8,128)(2,1)S(1)} fusion(bf16[2,4,14,3,3072]{4,2,3,1,0:T(8,128)(2,1)} %collective-permute-done.3, bf16[2,4,3,3,3072]{4,2,3,1,0:T(4,128)(2,1)} %copy-done.4, bf16[2,4,8,3,3072]{4,2,3,1,0:T(8,128)(2,1)S(1)} %copy-done.3, bf16[2,4,3,3,3072]{4,2,3,1,0:T(4,128)(2,1)S(1)} %copy.47, ...), kind=kLoop, calls=%fused_computation.26 | loop fusion | flops 30965760 | bytes 12386304 | tf_op jit(solution)/shard_map/concatenate | solution.py:21
  116.1 2.6 fusion.58
  118.6 4.5 %copy.49 = bf16[1,4,14,9,3072]{4,3,2,1,0:T(8,128)(2,1)} copy(bf16[1,4,14,9,3072]{4,2,3,1,0:T(8,128)(2,1)S(1)} %get-tuple-element.304) | data formatting | bytes 6193152 | tf_op jit(solution)/shard_map/slice | solution.py:165
  123.1 9.9 %reshape_squeeze.12 = bf16[504,48,64]{2,1,0:T(8,128)(2,1)} reshape(bf16[1,4,14,9,3072]{4,3,2,1,0:T(8,128)(2,1)} %copy.49) | data formatting | bytes 6193152 | tf_op jit(solution)/shard_map/reshape;squeeze | solution.py:165
  132.9 7.6 %copy.53 = bf16[504,48,64]{0,2,1:T(8,128)(2,1)} copy(bf16[504,48,64]{2,1,0:T(8,128)(2,1)} %reshape_squeeze.12) | data formatting | bytes 6193152
  140.5 6.5 %copy.51 = bf16[1,4,14,9,3072]{4,3,2,1,0:T(8,128)(2,1)} copy(bf16[1,4,14,9,3072]{4,2,3,1,0:T(8,128)(2,1)} %get-tuple-element.303) | data formatting | bytes 6193152 | tf_op jit(solution)/shard_map/slice | solution.py:164
  147.0 9.9 %reshape_squeeze.13 = bf16[504,48,64]{2,1,0:T(8,128)(2,1)} reshape(bf16[1,4,14,9,3072]{4,3,2,1,0:T(8,128)(2,1)} %copy.51) | data formatting | bytes 6193152 | tf_op jit(solution)/shard_map/reshape;squeeze | solution.py:164
  156.9 7.7 %copy.55 = bf16[504,48,64]{0,2,1:T(8,128)(2,1)} copy(bf16[504,48,64]{2,1,0:T(8,128)(2,1)} %reshape_squeeze.13) | data formatting | bytes 6193152
  165.9 51.7 %while.18 = (s32[]{:T(128)}, f32[96,48,64]{0,2,1:T(8,128)}, f32[48,96]{1,0:T(8,128)S(1)}, f32[48,96]{1,0:T(8,128)S(1)}, bf16[504,48,64]{0,2,1:T(8,128)(2,1)}, /*...) while((s32[]{:T(128)}, f32[96,48,64]{0,2,1:T(8,128)}, ...), condition=%wide.region_3.4_spmd.clone, body=%wide.region_0.3_spmd.clone.sunk | while | flops 53899012 | bytes 4623533 | solution.py:118
  217.7 9.9 %fusion.59 = (bf16[1,226,3072]{2,0,1:T(2,128)(2,1)}, bf16[1,226,3072]{2,0,1:T(2,128)(2,1)}) fusion(bf16[2,226,3072]{2,0,1:T(2,128)(2,1)} %all-gather.3.cloned.1.call-done), kind=kLoop, calls=%fused_computation.99 | loop fusion | bytes 5554176 | tf_op jit(solution)/shard_map/slice | solution.py:201
  227.6 6.5 %copy.56 = bf16[1,226,3072]{1,2,0:T(8,128)(2,1)S(1)} copy(bf16[1,226,3072]{2,0,1:T(2,128)(2,1)} %get-tuple-element.305) | data formatting | bytes 2777088 | tf_op jit(solution)/shard_map/slice | solution.py:201
  234.1 3.0 %bitcast_reduce_fusion = (f32[96,48]{0,1:T(8,128)S(1)}, f32[48,226,96]{1,2,0:T(8,128)}) fusion(bf16[226,48,64]{0,2,1:T(8,128)(2,1)S(1)} %bitcast.53, bf16[96,48,64]{0,2,1:T(8,128)(2,1)S(1)} %get-tuple-element.465), kind=kOutput, calls=%fused_computation.28 | convolution fusion | flops 135378432 | bytes 6162432 | tf_op jit(solution)/shard_map/nhd,thd->nht/dot_general | solution.py:123
  237.1 6.6 %copy.58 = bf16[1,226,3072]{1,2,0:T(8,128)(2,1)S(1)} copy(bf16[1,226,3072]{2,0,1:T(2,128)(2,1)} %get-tuple-element.306) | data formatting | bytes 2777088 | tf_op jit(solution)/shard_map/slice | solution.py:202
  243.8 3.6 %fusion.20 = f32[96,48]{0,1:T(8,128)S(1)} fusion(f32[48,226,96]{1,2,0:T(8,128)} %get-tuple-element.312, f32[96,48]{0,1:T(8,128)S(1)} %get-tuple-element.311), kind=kLoop, calls=%fused_computation.30 | loop fusion | flops 3119616 | bytes 4202496 | tf_op jit(solution)/shard_map/reduce_sum | solution.py:128
  250.0 3.1 %copy.59 = f32[96,48,64]{2,1,0:T(8,128)} copy(f32[96,48,64]{0,2,1:T(8,128)} %fusion.27) | data formatting | bytes 2359296 | tf_op jit(solution)/shard_map/div | solution.py:145
  253.0 2.9 %reshape.133 = f32[4,8,3,3072]{3,2,1,0:T(4,128)S(1)} reshape(f32[96,48,64]{2,1,0:T(8,128)} %copy.59) | data formatting | bytes 2359296 | tf_op jit(solution)/shard_map/reshape | solution.py:179
  (177 shorter events, 68.4 us)
Async XLA Ops:
  6.5 36.2 %copy-start = (bf16[512,1536]{1,0:T(8,128)(2,1)S(1)}, bf16[512,1536]{1,0:T(8,128)(2,1)}, u32[]{:S(2)}) copy-start(bf16[512,1536]{1,0:T(8,128)(2,1)} %param.13) | copy-start | bytes 4718596
  6.5 18.1 %copy-start.3 = (bf16[2,4,8,3,3072]{4,2,3,1,0:T(8,128)(2,1)S(1)}, bf16[2,4,8,3,3072]{4,2,3,1,0:T(8,128)(2,1)}, u32[]{:S(2)}) copy-start(bf16[2,4,8,3,3072]{4,2,3,1,0:T(8,128)(2,1)} %param.10) | copy-start | bytes 3538948
  6.5 211.1 %all-gather.3.cloned.1.call-start = ((), (), s32[]{:S(2)}) async-start(), calls=%async_computation | async-start | bytes 4165632 | tf_op jit(solution)/shard_map/all_gather | solution.py:198
  9.1 9.7 %collective-permute-start = (bf16[2,4,3,3,3072]{4,1,3,2,0:T(4,128)(2,1)S(1)}, bf16[2,4,3,3,3072]{4,1,3,2,0:T(4,128)(2,1)S(1)}, u32[]{:S(2)}, u32[]{:S(2)}) collective-permute-start(bf16[2,4,3,3,3072]{4,1,3,2,0:T(4,128)(2,1)S(1)} %copy.61), channel_id=1, source_target_pairs={{0,2},{2,4},{4,6},{1,3},{3,5},{5,7},{8,10},{10,12},{12,14},{9,11},... | collective-permute-start | bytes 1327112 | tf_op jit(solution)/shard_map/ppermute | solution.py:23
  13.9 9.6 %collective-permute-start.1 = (bf16[2,4,3,3,3072]{4,1,3,2,0:T(4,128)(2,1)S(1)}, bf16[2,4,3,3,3072]{4,1,3,2,0:T(4,128)(2,1)S(1)}, u32[]{:S(2)}, u32[]{:S(2)}) collective-permute-start(bf16[2,4,3,3,3072]{4,1,3,2,0:T(4,128)(2,1)S(1)} %copy.62), channel_id=1, source_target_pairs={{2,0},{4,2},{6,4},{3,1},{5,3},{7,5},{10,8},{12,10},{14,12},{11,9},... | collective-permute-start | bytes 1327112 | tf_op jit(solution)/shard_map/ppermute | solution.py:25
  23.8 0.8 copy-start.4
  24.6 8.6 %copy-start.8 = (s32[4,2,2]{0,2,1:T(2,128)S(1)}, s32[4,2,2]{0,2,1:T(2,128)}, u32[]{:S(2)}) copy-start(s32[4,2,2]{0,2,1:T(2,128)} %param.15) | copy-start | bytes 196
  27.3 84.5 %collective-permute-start.2 = (bf16[2,4,14,3,3072]{4,2,3,1,0:T(8,128)(2,1)}, bf16[2,4,14,3,3072]{4,2,3,1,0:T(8,128)(2,1)}, u32[]{:S(2)}, u32[]{:S(2)}) collective-permute-start(bf16[2,4,14,3,3072]{4,2,3,1,0:T(8,128)(2,1)} %pad_maximum_fusion.1), channel_id=1, source_target_pairs={{0,1},{2,3},{4,5},{6,7},{8,9},{10,11},{12,13},{14,15},{16,17},{18,... | collective-permute-start | bytes 6193160 | tf_op jit(solution)/shard_map/ppermute | solution.py:23
  31.9 79.9 %collective-permute-start.3 = (bf16[2,4,14,3,3072]{4,2,3,1,0:T(8,128)(2,1)}, bf16[2,4,14,3,3072]{4,2,3,1,0:T(8,128)(2,1)}, u32[]{:S(2)}, u32[]{:S(2)}) collective-permute-start(bf16[2,4,14,3,3072]{4,2,3,1,0:T(8,128)(2,1)} %pad_maximum_fusion.1), channel_id=1, source_target_pairs={{1,0},{3,2},{5,4},{7,6},{9,8},{11,10},{13,12},{15,14},{17,16},{19,... | collective-permute-start | bytes 6193160 | tf_op jit(solution)/shard_map/ppermute | solution.py:25
  33.5 9.3 %copy-start.9 = (bf16[512]{0:T(512)(128)(2,1)S(1)}, bf16[512]{0:T(512)(128)(2,1)}, u32[]{:S(2)}) copy-start(bf16[512]{0:T(512)(128)(2,1)} %param.12) | copy-start | bytes 3076
  156.9 9.1 %copy-start.5 = (bf16[96,48,64]{0,2,1:T(8,128)(2,1)S(1)}, bf16[96,48,64]{0,2,1:T(8,128)(2,1)}, u32[]{:S(2)}) copy-start(bf16[96,48,64]{0,2,1:T(8,128)(2,1)} %copy.54) | copy-start | bytes 1769476
  156.9 9.1 %copy-start.7 = (s32[48,2]{0,1:T(2,128)S(1)}, s32[48,2]{0,1:T(2,128)}, u32[]{:S(2)}) copy-start(s32[48,2]{0,1:T(2,128)} %param.14) | copy-start | bytes 1156
  237.1 10.2 %copy-start.6 = (f32[96,48,64]{0,2,1:T(8,128)S(1)}, f32[96,48,64]{0,2,1:T(8,128)}, u32[]{:S(2)}) copy-start(f32[96,48,64]{0,2,1:T(8,128)} %get-tuple-element.191) | copy-start | bytes 3538948
  243.7 3.8 %copy-start.2 = (f32[48,226,96]{1,2,0:T(8,128)S(1)}, f32[48,226,96]{1,2,0:T(8,128)}, u32[]{:S(2)}) copy-start(f32[48,226,96]{1,2,0:T(8,128)} %get-tuple-element.312) | copy-start | bytes 12496900
  250.0 7.5 %copy-start.1 = (bf16[512,1536]{1,0:T(8,128)(2,1)S(1)}, bf16[512,1536]{1,0:T(8,128)(2,1)}, u32[]{:S(2)}) copy-start(bf16[512,1536]{1,0:T(8,128)(2,1)} %param.13) | copy-start | bytes 4718596
Sparse Core Ops, SparseCore 0:
  33.3 72.7 all-gather.2
where the time goes:
time: 266 us; the launch traced here: 264 us
  local copies, waits for them, and re-layouts  94.2 us (35%)
  blocking collectives  68.6 us (26%)
  matrix products  48.9 us (18%)
  other arithmetic  19 us (7%)
  between operations  13.6 us (5%)
  starting transfers between devices  12.3 us (5%)
  waiting for transfers between devices  7.41 us (3%)
    all_gather x1, blocking collectives, body(): lax.all_gather(gate_part, 'tw', axis=0, tiled=True)  68.6 us
    dot_general x12, matrix products, one_group(): jnp.einsum('hnk,khd->nhd', weights, value_part, preferred_element_type=jn...  24.9 us
    unnamed x27, local copies, waits for them, and re-layouts  21.8 us
    dot_general x12, matrix products, one_group(): jnp.einsum('nhd,khd->hnk', query_part, key_part, preferred_element_type=j...  17.4 us
    slice x2, local copies, waits for them, and re-layouts, body(): text_keys = text_full[0].reshape(text_count, head_count, HEAD_DIM)  16.4 us
    another operation x1, local copies, waits for them, and re-layouts, attend_tile(): video_values = kv_block[1].reshape(-1, head_count, HEAD_DIM)  9.85 us
    another operation x1, local copies, waits for them, and re-layouts, attend_tile(): video_keys = kv_block[0].reshape(-1, head_count, HEAD_DIM)  9.85 us
    ppermute x2, starting transfers between devices, extended(): lax.ppermute(tail, axis, [(i, (i + 1) % count) for i in range(ends)])  9.08 us
  transfers between devices with their start and end apart: 5, of which 2 were waited for; matrix products, arithmetic and copies ran while one was open for 44% of the time, Pallas kernels for 0%

commit v1 on v0

--- a/solution.py
+++ b/solution.py
@@ -1,8 +1,12 @@
 import math
+from functools import partial
 
 import jax
 import jax.numpy as jnp
+import numpy as np
 from jax import lax
+from jax.experimental import pallas as pl
+from jax.experimental.pallas import tpu as pltpu
 from jax.sharding import PartitionSpec as P
 
 HEAD_DIM = 64
@@ -182,7 +186,7 @@
     return result.astype(jnp.bfloat16)
 
 
-def body(queries, video_kv, text_kv, time_embed, gate_weight, window_extent, tile_valid):
+def general_body(queries, video_kv, text_kv, time_embed, gate_weight, window_extent, tile_valid):
     frames, tile_rows, tile_cols, model_width = queries.shape
     head_count = model_width // HEAD_DIM
     score_scale = HEAD_DIM ** (-0.5)
@@ -215,6 +219,390 @@
     )
 
 
+LANES = 128
+CHUNKS = (8, 4)
+UNROLL = 2
+VMEM_LIMIT = 16 * 2**20
+
+
+def pack_kernel(q_ref, kv_ref, *refs, moves):
+    outs, sems = refs[:-1], refs[-1]
+    col_at = lax.axis_index("tw")
+    half = q_ref.shape[2] // 2
+    copies = []
+    for at, (source, first, out, slot, other) in enumerate(moves):
+        to = outs[out].at[slot]
+        side = 1 - col_at if other else col_at
+        lanes = pl.ds(pl.multiple_of(side * half + first, LANES), to.shape[2])
+        ref = q_ref if source == 0 else kv_ref
+        copies.append(pltpu.make_async_copy(ref.at[:, :, lanes], to, sems.at[at]))
+    for copy in copies:
+        copy.start()
+    for copy in copies:
+        copy.wait()
+
+
+def pack(q, kv, shapes, moves, name):
+    return pl.pallas_call(
+        partial(pack_kernel, moves=moves),
+        out_shape=[jax.ShapeDtypeStruct(shape, q.dtype) for shape in shapes],
+        in_specs=[pl.BlockSpec(memory_space=pltpu.HBM)] * 2,
+        out_specs=[pl.BlockSpec(memory_space=pltpu.VMEM)] * len(shapes),
+        scratch_shapes=[pltpu.SemaphoreType.DMA((len(moves),))],
+        compiler_params=pltpu.CompilerParams(vmem_limit_bytes=VMEM_LIMIT),
+        name=name,
+    )(q, kv)
+
+
+def cut_edges(select_ref, keys_values, bottom_ref, top_ref):
+    edge = bottom_ref.shape[1]
+    for part in (0, 1):
+        rows = lax.dot_general(
+            select_ref[...],
+            keys_values[part],
+            (((1,), (0,)), ((), ())),
+            preferred_element_type=jnp.float32,
+        ).astype(jnp.bfloat16)
+        bottom_ref[part] = rows[:edge]
+        top_ref[part] = rows[edge:]
+
+
+def edges_kernel(select_ref, peer_ref, *refs):
+    bottom_ref, top_ref = refs[-2:]
+    cut_edges(select_ref, (peer_ref[1], peer_ref[2]), bottom_ref, top_ref)
+
+
+def prepare_kernel(
+    valid_ref,
+    select_ref,
+    key_ref,
+    query_ref,
+    time_ref,
+    weight_ref,
+    kv_ref,
+    bottom_ref,
+    top_ref,
+    bias_ref,
+    gate_ref,
+    ok_ref,
+    *,
+    tile_cols,
+    tiles_down,
+):
+    row_at = lax.axis_index("th")
+    col_at = lax.axis_index("tw")
+    cut_edges(select_ref, (kv_ref[0], kv_ref[1]), bottom_ref, top_ref)
+    key_row, key_local, key_col, key_block = (key_ref[i : i + 1] for i in range(4))
+    query_row, query_col, query_peer = (query_ref[:, i : i + 1] for i in range(3))
+    key_peer = key_block % 2
+    row_limit = jnp.zeros_like(key_row)
+    col_limit = jnp.zeros_like(key_row)
+    query_limits = []
+    for at, step in enumerate((0, -1, 1)):
+        tile_row = row_at + step
+        inside = (tile_row >= 0) & (tile_row < tiles_down)
+        tile_row = jnp.clip(tile_row, 0, tiles_down - 1)
+        for peer in (0, 1):
+            side = 1 - col_at if peer else col_at
+            rows = jnp.where(inside, valid_ref[side, 0, tile_row], 0)
+            cols = valid_ref[side, 1, tile_row]
+            block = 2 * at + peer
+            row_limit = jnp.where(key_block == block, rows, row_limit)
+            col_limit = jnp.where(key_block == block, cols, col_limit)
+            if step == 0:
+                query_limits.append((rows, cols))
+    key_ok = (key_local < row_limit) & (key_col < col_limit)
+    key_at = key_col + tile_cols * jnp.where(key_peer > 0, 1 - col_at, col_at)
+    query_at = query_col + tile_cols * jnp.where(query_peer > 0, 1 - col_at, col_at)
+    row_gap = jnp.abs(query_row - key_row)
+    col_gap = jnp.where(key_ok, jnp.abs(query_at - key_at), 2 * HALO + 1)
+    for rows in range(HALO):
+        for cols in range(HALO):
+            near = (row_gap <= rows + 1) & (col_gap <= cols + 1)
+            bias_ref[rows * HALO + cols] = jnp.where(near, 0.0, NEG)
+    row_limit = jnp.where(query_peer > 0, query_limits[1][0], query_limits[0][0])
+    col_limit = jnp.where(query_peer > 0, query_limits[1][1], query_limits[0][1])
+    query_ok = (query_row < row_limit) & (query_col < col_limit)
+    ok_ref[...] = jnp.broadcast_to(jnp.where(query_ok, 1.0, 0.0), ok_ref.shape)
+    step = time_ref[...].astype(jnp.float32)
+    step = (step / (1.0 + jnp.exp(-step))).astype(jnp.bfloat16)
+    gate = jnp.dot(step, weight_ref[...], preferred_element_type=jnp.float32)
+    gate = gate.astype(jnp.bfloat16).astype(jnp.float32)
+    for pair in range(gate_ref.shape[0]):
+        gate_ref[pair] = gate[0:1, pair * LANES : (pair + 1) * LANES]
+
+
+def attend_kernel(
+    extent_ref,
+    mine_q_ref,
+    mine_kv_ref,
+    peer_ref,
+    above_mine_ref,
+    below_mine_ref,
+    above_peer_ref,
+    below_peer_ref,
+    text_ref,
+    bias_ref,
+    gate_ref,
+    ok_ref,
+    own_out_ref,
+    peer_out_ref,
+    key_ref,
+    value_ref,
+    *,
+    first_pair,
+    pairs,
+    unroll,
+    text_count,
+    score_scale,
+):
+    count = mine_q_ref.shape[1]
+    edge = above_mine_ref.shape[1]
+    near = 2 * count + 4 * edge
+    first_head = lax.axis_index("tw") * (2 * gate_ref.shape[0])
+    left = lax.broadcasted_iota(jnp.int32, (1, LANES), 1) < HEAD_DIM
+    zero = jnp.zeros((), jnp.bfloat16)
+    one = jnp.ones((), jnp.bfloat16)
+    text_rows = text_ref.shape[1]
+    text_bias = jnp.where(
+        lax.broadcasted_iota(jnp.int32, (1, text_rows), 1) < text_count, 0.0, NEG
+    )
+
+    def one_pair(turn, slot):
+        here = pl.ds(pl.multiple_of(turn * LANES, LANES), LANES)
+        whole = pl.ds(pl.multiple_of((first_pair + turn) * LANES, LANES), LANES)
+        for part, into in ((0, key_ref.at[slot]), (1, value_ref.at[slot])):
+            into[0:count] = mine_kv_ref[part, :, whole]
+            into[count : 2 * count] = peer_ref[1 + part, :, here]
+            at = 2 * count
+            for ref, lanes in (
+                (above_mine_ref, whole),
+                (above_peer_ref, here),
+                (below_mine_ref, whole),
+                (below_peer_ref, here),
+            ):
+                into[at : at + edge] = ref[part, :, lanes]
+                at += edge
+            into[near:] = text_ref[part, :, whole]
+        queries = jnp.concatenate([mine_q_ref[0, :, whole], peer_ref[0, :, here]], 0)
+        queries = queries * jnp.asarray(score_scale, jnp.bfloat16)
+        queries = jnp.concatenate([jnp.where(left, queries, zero), jnp.where(left, zero, queries)], 0)
+        both = lax.dot_general(
+            queries, key_ref[slot], (((1,), (1,)), ((), ())), preferred_element_type=jnp.float32
+        )
+        values = value_ref[slot]
+        outs = []
+        for side in (0, 1):
+            head = first_head + 2 * (first_pair + turn) + side
+            reach_rows = jnp.clip(extent_ref[0, head], 1, HALO) - 1
+            reach_cols = jnp.clip(extent_ref[1, head], 1, HALO) - 1
+            bias = bias_ref[reach_rows * HALO + reach_cols]
+            scores = both[2 * count * side : 2 * count * (side + 1)]
+            scores = jnp.concatenate([scores[:, :near] + bias, scores[:, near:] + text_bias], 1)
+            top = jnp.max(scores, axis=-1, keepdims=True)
+            weights = jnp.exp(scores - top).astype(jnp.bfloat16)
+            summed = jnp.where(left, values, one) if side == 0 else jnp.where(left, one, values)
+            outs.append(
+                lax.dot_general(
+                    weights, summed, (((1,), (0,)), ((), ())), preferred_element_type=jnp.float32
+                )
+            )
+        total = pltpu.roll(jnp.where(left, outs[1], outs[0]), HEAD_DIM, 1)
+        attended = jnp.where(left, outs[0], outs[1]) / total
+        gated = jnp.where(ok_ref[...] > 0.0, attended * gate_ref[first_pair + turn], 0.0)
+        gated = gated.astype(jnp.bfloat16)
+        own_out_ref[:, here] = gated[:count]
+        peer_out_ref[:, here] = gated[count:]
+
+    def some_pairs(turn, carry):
+        for slot in range(unroll):
+            one_pair(turn * unroll + slot, slot)
+        return carry
+
+    lax.fori_loop(0, pairs // unroll, some_pairs, 0)
+
+
+def place_kernel(*refs, moves):
+    ins, out_ref, sems = refs[:-2], refs[-2], refs[-1]
+    col_at = lax.axis_index("tw")
+    half = out_ref.shape[1] // 2
+    copies = []
+    for at, (source, first, other) in enumerate(moves):
+        side = 1 - col_at if other else col_at
+        ref = ins[source]
+        lanes = pl.ds(pl.multiple_of(side * half + first, LANES), ref.shape[1])
+        copies.append(pltpu.make_async_copy(ref, out_ref.at[:, lanes], sems.at[at]))
+    for copy in copies:
+        copy.start()
+    for copy in copies:
+        copy.wait()
+
+
+def place(pieces, base, shape, moves, name):
+    vmem = pl.BlockSpec(memory_space=pltpu.VMEM)
+    hbm = pl.BlockSpec(memory_space=pltpu.HBM)
+    rest = () if base is None else (base,)
+    return pl.pallas_call(
+        partial(place_kernel, moves=moves),
+        out_shape=jax.ShapeDtypeStruct(shape, jnp.bfloat16),
+        in_specs=[vmem] * len(pieces) + [hbm] * len(rest),
+        out_specs=hbm,
+        scratch_shapes=[pltpu.SemaphoreType.DMA((len(moves),))],
+        input_output_aliases={} if base is None else {len(pieces): 0},
+        compiler_params=pltpu.CompilerParams(vmem_limit_bytes=VMEM_LIMIT),
+        name=name,
+    )(*pieces, *rest)
+
+
+def places(frames, tile_rows, tile_cols, edge_rows):
+    keys = []
+    for at, (step, low, high) in enumerate(
+        ((0, 0, tile_rows), (-1, tile_rows - edge_rows, tile_rows), (1, 0, edge_rows))
+    ):
+        shape = (frames, tile_cols, high - low)
+        row = np.broadcast_to(np.arange(low, high), shape).reshape(-1)
+        col = np.broadcast_to(np.arange(tile_cols)[:, None], shape).reshape(-1)
+        for peer in (0, 1):
+            keys.append(np.stack([row + step * tile_rows, row, col, 0 * row + 2 * at + peer]))
+    query = np.concatenate(keys[:2], 1)[[0, 2, 3]]
+    keys = np.concatenate(keys, 1)
+    keys = np.concatenate([keys, 0 * keys]).astype(np.int32)
+    query = np.concatenate([query, np.zeros((5, query.shape[1]))]).T.astype(np.int32)
+    groups = np.arange(frames * tile_cols)[:, None] * tile_rows
+    rows = np.arange(edge_rows)[None, :]
+    chosen = np.concatenate(
+        [(groups + tile_rows - edge_rows + rows).reshape(-1), (groups + rows).reshape(-1)]
+    )
+    select = (chosen[:, None] == np.arange(frames * tile_cols * tile_rows)[None, :]).astype(
+        jnp.bfloat16
+    )
+    return keys, query, select
+
+
+def swapped_body(queries, video_kv, text_kv, time_embed, gate_weight, window_extent, tile_valid):
+    frames, tile_rows, tile_cols, model_width = queries.shape
+    half = model_width // 2
+    count = frames * tile_rows * tile_cols
+    edge_rows = HALO + HALO % 2
+    edge = frames * tile_cols * edge_rows
+    near = 2 * count + 4 * edge
+    text_count = text_kv.shape[1]
+    text_rows = -(-text_count // LANES) * LANES
+    tiles_down = lax.axis_size("th")
+    swap = [(0, 1), (1, 0)]
+    down = [(i, i + 1) for i in range(tiles_down - 1)]
+    up = [(i + 1, i) for i in range(tiles_down - 1)]
+    vmem = pl.BlockSpec(memory_space=pltpu.VMEM)
+    smem = pl.BlockSpec(memory_space=pltpu.SMEM)
+    params = pltpu.CompilerParams(vmem_limit_bytes=VMEM_LIMIT)
+    key_places, query_places, select = places(frames, tile_rows, tile_cols, edge_rows)
+    q = jnp.transpose(queries, (0, 2, 1, 3)).reshape(1, count, model_width)
+    kv = jnp.transpose(video_kv, (0, 1, 3, 2, 4)).reshape(2, count, model_width)
+    total_pairs = half // LANES
+    pieces = []
+    first = 0
+    for share in CHUNKS:
+        pairs = share * total_pairs // sum(CHUNKS)
+        pieces.append((first, pairs))
+        first += pairs
+    head, tail = slice(0, 1), slice(1, 3)
+    arrived = []
+    for at, (first, pairs) in enumerate(pieces):
+        low = first * LANES
+        shapes = [(3, count, pairs * LANES)]
+        moves = [(0, low, 0, head, True), (1, low, 0, tail, True)]
+        last = at == len(pieces) - 1
+        if last:
+            shapes += [(1, count, half), (2, count, half)]
+            moves += [(0, 0, 1, slice(0, 1), False), (1, 0, 2, slice(0, 2), False)]
+        packed = pack(q, kv, shapes, tuple(moves), "pack")
+        arrived.append(lax.ppermute(packed[0], "tw", swap))
+        if last:
+            mine_q, mine_kv = packed[1:]
+    edge_shape = jax.ShapeDtypeStruct((2, edge, half), jnp.bfloat16)
+    bottom, top, bias, gate, query_ok = pl.pallas_call(
+        partial(prepare_kernel, tile_cols=tile_cols, tiles_down=tiles_down),
+        out_shape=[
+            edge_shape,
+            edge_shape,
+            jax.ShapeDtypeStruct((HALO * HALO, 2 * count, near), jnp.float32),
+            jax.ShapeDtypeStruct((total_pairs, 1, LANES), jnp.float32),
+            jax.ShapeDtypeStruct((2 * count, LANES), jnp.float32),
+        ],
+        in_specs=[smem] + [vmem] * 6,
+        out_specs=[vmem] * 5,
+        compiler_params=params,
+        name="prepare",
+    )(
+        jnp.transpose(tile_valid.reshape(tiles_down, 2, 2), (1, 2, 0)),
+        select,
+        key_places,
+        query_places,
+        time_embed.reshape(1, -1),
+        gate_weight,
+        mine_kv,
+    )
+    above_mine = lax.ppermute(bottom, "th", down)
+    below_mine = lax.ppermute(top, "th", up)
+    text = jnp.pad(text_kv, ((0, 0), (0, text_rows - text_count), (0, 0)))
+    extents = window_extent.T
+    owned, returned = [], []
+    for (first, pairs), peer in zip(pieces, arrived):
+        width = pairs * LANES
+        edge_shape = jax.ShapeDtypeStruct((2, edge, width), jnp.bfloat16)
+        bottom, top = pl.pallas_call(
+            edges_kernel,
+            out_shape=[edge_shape] * 2,
+            in_specs=[vmem] * 2 + [pl.BlockSpec(memory_space=pl.ANY)],
+            out_specs=[vmem] * 2,
+            compiler_params=params,
+            name="edges",
+        )(select, peer, text)
+        above_peer = lax.ppermute(bottom, "th", down)
+        below_peer = lax.ppermute(top, "th", up)
+        unroll = math.gcd(pairs, UNROLL)
+        own_out, peer_out = pl.pallas_call(
+            partial(
+                attend_kernel,
+                first_pair=first,
+                pairs=pairs,
+                unroll=unroll,
+                text_count=text_count,
+                score_scale=HEAD_DIM ** (-0.5),
+            ),
+            out_shape=[jax.ShapeDtypeStruct((count, width), jnp.bfloat16)] * 2,
+            in_specs=[smem] + [vmem] * 11,
+            out_specs=[vmem] * 2,
+            scratch_shapes=[pltpu.VMEM((unroll, near + text_rows, LANES), jnp.bfloat16)] * 2,
+            compiler_params=params,
+            name="attend",
+        )(
+            extents,
+            mine_q,
+            mine_kv,
+            peer,
+            above_mine,
+            below_mine,
+            above_peer,
+            below_peer,
+            text,
+            bias,
+            gate,
+            query_ok,
+        )
+        owned.append(own_out)
+        returned.append(lax.ppermute(peer_out, "tw", swap))
+    starts = [first * LANES for first, _ in pieces]
+    early = owned + returned[:-1]
+    moves = [(i, low, False) for i, low in enumerate(starts)]
+    moves += [(len(owned) + i, low, True) for i, low in enumerate(starts[:-1])]
+    result = place(early, None, (count, model_width), tuple(moves), "place")
+    moves = ((0, starts[-1], True),)
+    result = place(returned[-1:], result, (count, model_width), moves, "place_last")
+    result = result.reshape(frames, tile_cols, tile_rows, model_width)
+    return jnp.transpose(result, (0, 2, 1, 3))
+
+
 def solution(mesh):
     placed = (
         P("vid", "th", "tw", None),
@@ -225,6 +613,7 @@
         P(),
         P("vid", None, None),
     )
+    body = swapped_body if mesh.shape["tw"] == 2 else general_body
     return jax.shard_map(
         body, mesh=mesh, in_specs=placed, out_specs=P("vid", "th", "tw", None), check_vma=False
     )

time: 266 us -> 51.4 us (0.19)
  local copies, waits for them, and re-layouts: 94.2 us -> 2.62 us
  blocking collectives: 68.6 us -> 0 us
  matrix products: 48.9 us -> 0 us
  other arithmetic: 19 us -> 0 us
  between operations: 13.6 us -> 0.24 us
  Pallas kernels: 0 us -> 12.7 us
  starting transfers between devices: 12.3 us -> 23.2 us
  waiting for transfers between devices: 7.41 us -> 12.3 us
    all_gather x1 -> x0, blocking collectives: 68.6 us -> none  [body(): lax.all_gather(gate_part, 'tw', axis=0, tiled=True)]
    dot_general x31 -> x0, matrix products: 48.9 us -> none  [the longest x12 24.9 us: one_group(): jnp.einsum('hnk,khd->nhd', weights, value_part, preferred_element_type=jn...]
    slice x9 -> x0, local copies, waits for them, and re-layouts: 38.9 us -> none  [the longest x2 16.4 us: body(): text_keys = text_full[0].reshape(text_count, head_count, HEAD_DIM)]
    another operation x17 -> x0, local copies, waits for them, and re-layouts: 19.9 us -> none  [the longest x1 9.85 us: attend_tile(): video_values = kv_block[1].reshape(-1, head_count, HEAD_DIM)]
    unnamed x27 -> x21, local copies, waits for them, and re-layouts: 21.8 us -> 2.51 us
    pallas_call x0 -> x9, Pallas kernels: none -> 12.7 us  [the longest x2 9.19 us: swapped_body(): pl.pallas_call(partial(attend_kernel, first_pair=first, pairs=pairs, unro...]
    ppermute x4 -> x10, starting transfers between devices: 12.3 us -> 23.2 us  [the longest x2 9.24 us: swapped_body(): above_peer = lax.ppermute(bottom, 'th', down)]
    reduce_sum x13 -> x0, other arithmetic: 8.9 us -> none  [the longest x12 5.34 us: one_group(): totals = jnp.sum(exp_terms, axis=-1)]
  transfers between devices with their start and end apart: 5 -> 10, of which waited for: 2 -> 4; matrix products, arithmetic and copies ran while one was open for 44% -> 0% of each run, Pallas kernels for 0% -> 23%
where the time goes in v1:
time: 51.4 us; the launch traced here: 51.1 us
  starting transfers between devices  23.2 us (45%)
  Pallas kernels  12.7 us (25%)
  waiting for transfers between devices  12.3 us (24%)
  local copies, waits for them, and re-layouts  2.62 us (5%)
    ppermute x2, starting transfers between devices, swapped_body(): above_peer = lax.ppermute(bottom, 'th', down)  9.24 us
    pallas_call x2, Pallas kernels, swapped_body(): pl.pallas_call(partial(attend_kernel, first_pair=first, pairs=pairs, unro...  9.19 us
    ppermute x2, waiting for transfers between devices, swapped_body(): below_peer = lax.ppermute(top, 'th', up)  5.17 us
    ppermute x2, waiting for transfers between devices, swapped_body(): arrived.append(lax.ppermute(packed[0], 'tw', swap))  4.71 us
    ppermute x1, starting transfers between devices, swapped_body(): above_mine = lax.ppermute(bottom, 'th', down)  4.43 us
    ppermute x2, starting transfers between devices, swapped_body(): below_peer = lax.ppermute(top, 'th', up)  3.83 us
    unnamed x21, local copies, waits for them, and re-layouts  2.51 us
    ppermute x2, waiting for transfers between devices, swapped_body(): returned.append(lax.ppermute(peer_out, 'tw', swap))  2.44 us
  transfers between devices with their start and end apart: 10, of which 4 were waited for; matrix products, arithmetic and copies ran while one was open for 0% of the time, Pallas kernels for 23%

profile of v1, /device:TPU:1, one launch (start us, length us, event | category | flops | bytes accessed | tf_op | source)
XLA Modules:
  0.0 51.1 jit_solution(18346044536602214753)
XLA Ops:
  0.0 1.3 %copy-done = bf16[2,4,8,3,3072]{4,2,3,1,0:T(8,128)(2,1)S(1)} copy-done((bf16[2,4,8,3,3072]{4,2,3,1,0:T(8,128)(2,1)S(1)}, bf16[2,4,8,3,3072]{4,2,3,1,0:T(8,128)(2,1)}, u32[]{:S(2)}) %copy-start) | copy-done | bytes 1179672
  1.3 1.1 %copy-done.1 = bf16[4,8,3,3072]{3,1,2,0:T(8,128)(2,1)S(1)} copy-done((bf16[4,8,3,3072]{3,1,2,0:T(8,128)(2,1)S(1)}, bf16[4,8,3,3072]{3,1,2,0:T(8,128)(2,1)}, u32[]{:S(2)}) %copy-start.1) | copy-done | bytes 589848
  2.5 2.1 %collective-permute-start.6 = (bf16[3,96,1024]{2,1,0:T(8,128)(2,1)S(1)}, bf16[3,96,1024]{2,1,0:T(8,128)(2,1)S(1)}, u32[]{:S(2)}, u32[]{:S(2)}) collective-permute-start(bf16[3,96,1024]{2,1,0:T(8,128)(2,1)S(1)} %pack.3), channel_id=1, source_target_pairs={{0,1},{1,0},{2,3},{3,2},{4,5},{5,4},{6,7},{7,6},{8,9},{9,8},{10,11... | collective-permute-start | bytes 1769480 | tf_op jit(solution)/shard_map/ppermute | solution.py:519
  4.6 0.2 pack.2
  4.9 1.3 %prepare.1 = (bf16[2,48,1536]{2,1,0:T(8,128)(2,1)S(1)}, bf16[2,48,1536]{2,1,0:T(8,128)(2,1)S(1)}, f32[9,192,384]{2,1,0:T(8,128)S(1)}, f32[12,1,128]{2,1,0:T(1,128)S(1)}, f32[192,128]{1,0:T(8,128)S(1)}) custom-call(s32[2,2,4]{2,1,0:T(2,128)S(1)} %bitcast.17, bf16[96,96]{1,0:T(8,128)(2,1)S(1)} %copy-done.3, s32[8,384]{1,0:T(8,128)S(1)} %copy-done.5, ...), custom_call_target="tpu_custom_call" | custom-call | tf_op jit(solution)/shard_map/prepare/pallas_call | solution.py:523
  6.3 4.4 %collective-permute-start.1 = (bf16[2,48,1536]{2,1,0:T(8,128)(2,1)S(1)}, bf16[2,48,1536]{2,1,0:T(8,128)(2,1)S(1)}, u32[]{:S(2)}, u32[]{:S(2)}) collective-permute-start(bf16[2,48,1536]{2,1,0:T(8,128)(2,1)S(1)} %get-tuple-element.24), channel_id=1, source_target_pairs={{0,2},{2,4},{4,6},{1,3},{3,5},{5,7},{8,10},{10,12},{12,14},{9,11},... | collective-permute-start | bytes 884744 | tf_op jit(solution)/shard_map/ppermute | solution.py:545
  10.7 1.9 %collective-permute-start.2 = (bf16[2,48,1536]{2,1,0:T(8,128)(2,1)S(1)}, bf16[2,48,1536]{2,1,0:T(8,128)(2,1)S(1)}, u32[]{:S(2)}, u32[]{:S(2)}) collective-permute-start(bf16[2,48,1536]{2,1,0:T(8,128)(2,1)S(1)} %get-tuple-element.25), channel_id=1, source_target_pairs={{2,0},{4,2},{6,4},{3,1},{5,3},{7,5},{10,8},{12,10},{14,12},{11,9},... | collective-permute-start | bytes 884744 | tf_op jit(solution)/shard_map/ppermute | solution.py:546
  12.6 0.1 copy.12
  12.9 4.7 %collective-permute-done.6.peer_ref = bf16[3,96,1024]{2,1,0:T(8,128)(2,1)S(1)} collective-permute-done((bf16[3,96,1024]{2,1,0:T(8,128)(2,1)S(1)}, bf16[3,96,1024]{2,1,0:T(8,128)(2,1)S(1)}, u32[]{:S(2)}, u32[]{:S(2)}) %collective-permute-start.6) | collective-permute-done | bytes 589856 | tf_op jit(solution)/shard_map/ppermute | solution.py:519
  17.6 0.3 edges.3
  17.9 5.6 %collective-permute-start.7 = (bf16[2,48,1024]{2,1,0:T(8,128)(2,1)S(1)}, bf16[2,48,1024]{2,1,0:T(8,128)(2,1)S(1)}, u32[]{:S(2)}, u32[]{:S(2)}) collective-permute-start(bf16[2,48,1024]{2,1,0:T(8,128)(2,1)S(1)} %get-tuple-element.32), channel_id=1, source_target_pairs={{0,2},{2,4},{4,6},{1,3},{3,5},{5,7},{8,10},{10,12},{12,14},{9,11},... | collective-permute-start | bytes 589832 | tf_op jit(solution)/shard_map/ppermute | solution.py:561
  23.5 1.9 %collective-permute-start.8 = (bf16[2,48,1024]{2,1,0:T(8,128)(2,1)S(1)}, bf16[2,48,1024]{2,1,0:T(8,128)(2,1)S(1)}, u32[]{:S(2)}, u32[]{:S(2)}) collective-permute-start(bf16[2,48,1024]{2,1,0:T(8,128)(2,1)S(1)} %get-tuple-element.33), channel_id=1, source_target_pairs={{2,0},{4,2},{6,4},{3,1},{5,3},{7,5},{10,8},{12,10},{14,12},{11,9},... | collective-permute-start | bytes 589832 | tf_op jit(solution)/shard_map/ppermute | solution.py:562
  25.4 0.2 edges.2
  25.6 3.6 %collective-permute-start.3 = (bf16[2,48,512]{2,1,0:T(8,128)(2,1)S(1)}, bf16[2,48,512]{2,1,0:T(8,128)(2,1)S(1)}, u32[]{:S(2)}, u32[]{:S(2)}) collective-permute-start(bf16[2,48,512]{2,1,0:T(8,128)(2,1)S(1)} %get-tuple-element.26), channel_id=1, source_target_pairs={{0,2},{2,4},{4,6},{1,3},{3,5},{5,7},{8,10},{10,12},{12,14},{9,11},... | collective-permute-start | bytes 294920 | tf_op jit(solution)/shard_map/ppermute | solution.py:561
  29.3 1.2 %collective-permute-done.8.below_peer_ref = bf16[2,48,1024]{2,1,0:T(8,128)(2,1)S(1)} collective-permute-done((bf16[2,48,1024]{2,1,0:T(8,128)(2,1)S(1)}, bf16[2,48,1024]{2,1,0:T(8,128)(2,1)S(1)}, u32[]{:S(2)}, u32[]{:S(2)}) %collective-permute-start.8) | collective-permute-done | bytes 196640 | tf_op jit(solution)/shard_map/ppermute | solution.py:562
  30.5 6.0 %attend.3 = (bf16[96,1024]{1,0:T(8,128)(2,1)S(1)}, bf16[96,1024]{1,0:T(8,128)(2,1)S(1)}) custom-call(s32[2,48]{1,0:T(2,128)S(1)} %bitcast.15, bf16[1,96,1536]{2,1,0:T(8,128)(2,1)S(1)} %get-tuple-element.21.mine_q_ref, bf16[2,96,1536]{2,1,0:T(8,128)(2,1)S(1)} %get-tuple-element.22.kv_ref.mine_kv_ref, ...), custom_call_target="tpu_custom_call" | custom-call | tf_op jit(solution)/shard_map/attend/pallas_call | solution.py:564
  36.5 1.3 %collective-permute-start.9 = (bf16[96,1024]{1,0:T(8,128)(2,1)S(1)}, bf16[96,1024]{1,0:T(8,128)(2,1)S(1)}, u32[]{:S(2)}, u32[]{:S(2)}) collective-permute-start(bf16[96,1024]{1,0:T(8,128)(2,1)S(1)} %get-tuple-element.36), channel_id=1, source_target_pairs={{0,1},{1,0},{2,3},{3,2},{4,5},{5,4},{6,7},{7,6},{8,9},{9,8},{10,11... | collective-permute-start | bytes 589832 | tf_op jit(solution)/shard_map/ppermute | solution.py:594
  37.8 1.9 %collective-permute-start.4 = (bf16[2,48,512]{2,1,0:T(8,128)(2,1)S(1)}, bf16[2,48,512]{2,1,0:T(8,128)(2,1)S(1)}, u32[]{:S(2)}, u32[]{:S(2)}) collective-permute-start(bf16[2,48,512]{2,1,0:T(8,128)(2,1)S(1)} %get-tuple-element.27), channel_id=1, source_target_pairs={{2,0},{4,2},{6,4},{3,1},{5,3},{7,5},{10,8},{12,10},{14,12},{11,9},... | collective-permute-start | bytes 294920 | tf_op jit(solution)/shard_map/ppermute | solution.py:562
  39.7 4.0 %collective-permute-done.4.below_peer_ref = bf16[2,48,512]{2,1,0:T(8,128)(2,1)S(1)} collective-permute-done((bf16[2,48,512]{2,1,0:T(8,128)(2,1)S(1)}, bf16[2,48,512]{2,1,0:T(8,128)(2,1)S(1)}, u32[]{:S(2)}, u32[]{:S(2)}) %collective-permute-start.4) | collective-permute-done | bytes 98336 | tf_op jit(solution)/shard_map/ppermute | solution.py:562
  43.7 3.2 %attend.2 = (bf16[96,512]{1,0:T(8,128)(2,1)S(1)}, bf16[96,512]{1,0:T(8,128)(2,1)S(1)}) custom-call(s32[2,48]{1,0:T(2,128)S(1)} %bitcast.16, bf16[1,96,1536]{2,1,0:T(8,128)(2,1)S(1)} %get-tuple-element.21.mine_q_ref, bf16[2,96,1536]{2,1,0:T(8,128)(2,1)S(1)} %get-tuple-element.22.kv_ref.mine_kv_ref, bf16[3,96,512]{2,1,0:T(8,128)(2,1)S(1)} %collective-permute-done.peer_ref, ...), custom_call_target="tpu_custom_call" | custom-call | tf_op jit(solution)/shard_map/attend/pallas_call | solution.py:564
  46.9 0.3 collective-permute-start.5
  47.2 0.8 %place.1.refs_1_ = bf16[96,3072]{1,0:T(8,128)(2,1)} custom-call(bf16[96,1024]{1,0:T(8,128)(2,1)S(1)} %get-tuple-element.34.refs_0_, bf16[96,512]{1,0:T(8,128)(2,1)S(1)} %get-tuple-element.35.refs_1_, bf16[96,1024]{1,0:T(8,128)(2,1)S(1)} %collective-permute-done.9.refs_2_), custom_call_target="tpu_custom_call" | custom-call | tf_op jit(solution)/shard_map/place/pallas_call | solution.py:445
  48.0 2.4 %collective-permute-done.5.refs_0_ = bf16[96,512]{1,0:T(8,128)(2,1)S(1)} collective-permute-done((bf16[96,512]{1,0:T(8,128)(2,1)S(1)}, bf16[96,512]{1,0:T(8,128)(2,1)S(1)}, u32[]{:S(2)}, u32[]{:S(2)}) %collective-permute-start.5) | collective-permute-done | bytes 98336 | tf_op jit(solution)/shard_map/ppermute | solution.py:594
  50.5 0.6 %place_last.1 = bf16[96,3072]{1,0:T(8,128)(2,1)} custom-call(bf16[96,512]{1,0:T(8,128)(2,1)S(1)} %collective-permute-done.5.refs_0_, bf16[96,3072]{1,0:T(8,128)(2,1)} %place.1.refs_1_), custom_call_target="tpu_custom_call", output_to_operand_aliasing={{}: (1, {})} | custom-call | tf_op jit(solution)/shard_map/place_last/pallas_call | solution.py:445
  (28 shorter events, 0.4 us)
Async XLA Ops:
  0.0 1.3 %copy-start = (bf16[2,4,8,3,3072]{4,2,3,1,0:T(8,128)(2,1)S(1)}, bf16[2,4,8,3,3072]{4,2,3,1,0:T(8,128)(2,1)}, u32[]{:S(2)}) copy-start(bf16[2,4,8,3,3072]{4,2,3,1,0:T(8,128)(2,1)} %param.11) | copy-start | bytes 3538948
  1.3 1.1 %copy-start.1 = (bf16[4,8,3,3072]{3,1,2,0:T(8,128)(2,1)S(1)}, bf16[4,8,3,3072]{3,1,2,0:T(8,128)(2,1)}, u32[]{:S(2)}) copy-start(bf16[4,8,3,3072]{3,1,2,0:T(8,128)(2,1)} %param.10) | copy-start | bytes 1769476
  2.3 2.5 %copy-start.9 = (bf16[512]{0:T(512)(128)(2,1)S(1)}, bf16[512]{0:T(512)(128)(2,1)}, u32[]{:S(2)}) copy-start(bf16[512]{0:T(512)(128)(2,1)} %param.13) | copy-start | bytes 3076
  2.3 2.5 %copy-start.2 = (bf16[512,1536]{1,0:T(8,128)(2,1)S(1)}, bf16[512,1536]{1,0:T(8,128)(2,1)}, u32[]{:S(2)}) copy-start(bf16[512,1536]{1,0:T(8,128)(2,1)} %weight_ref.1) | copy-start | bytes 4718596
  2.3 2.6 %copy-start.3 = (bf16[96,96]{1,0:T(8,128)(2,1)S(1)}, bf16[96,96]{1,0:T(8,128)(2,1)}, u32[]{:S(2)}) copy-start(bf16[96,96]{1,0:T(8,128)(2,1)} %constant.9.clone.select_ref) | copy-start | bytes 55300
  2.3 2.6 %copy-start.4 = (s32[192,8]{1,0:T(8,128)S(1)}, s32[192,8]{1,0:T(8,128)}, u32[]{:S(2)}) copy-start(s32[192,8]{1,0:T(8,128)} %constant.11.clone.query_ref) | copy-start | bytes 18436
  2.3 2.6 %copy-start.5 = (s32[8,384]{1,0:T(8,128)S(1)}, s32[8,384]{1,0:T(8,128)}, u32[]{:S(2)}) copy-start(s32[8,384]{1,0:T(8,128)} %constant.10.clone.key_ref) | copy-start | bytes 36868
  2.4 2.6 %copy-start.7 = (s32[4,2,2]{0,2,1:T(2,128)S(1)}, s32[4,2,2]{0,2,1:T(2,128)}, u32[]{:S(2)}) copy-start(s32[4,2,2]{0,2,1:T(2,128)} %param.16) | copy-start | bytes 196
  2.5 15.2 %collective-permute-start.6 = (bf16[3,96,1024]{2,1,0:T(8,128)(2,1)S(1)}, bf16[3,96,1024]{2,1,0:T(8,128)(2,1)S(1)}, u32[]{:S(2)}, u32[]{:S(2)}) collective-permute-start(bf16[3,96,1024]{2,1,0:T(8,128)(2,1)S(1)} %pack.3), channel_id=1, source_target_pairs={{0,1},{1,0},{2,3},{3,2},{4,5},{5,4},{6,7},{7,6},{8,9},{9,8},{10,11... | collective-permute-start | bytes 1769480 | tf_op jit(solution)/shard_map/ppermute | solution.py:519
  4.8 7.9 %copy-start.8 = (bf16[2,226,1536]{2,0,1:T(2,128)(2,1)S(1)}, bf16[2,226,1536]{2,0,1:T(2,128)(2,1)}, u32[]{:S(2)}) copy-start(bf16[2,226,1536]{2,0,1:T(2,128)(2,1)} %param.12) | copy-start | bytes 4165636
  4.8 20.6 %collective-permute-start = (bf16[3,96,512]{2,1,0:T(8,128)(2,1)S(1)}, bf16[3,96,512]{2,1,0:T(8,128)(2,1)S(1)}, u32[]{:S(2)}, u32[]{:S(2)}) collective-permute-start(bf16[3,96,512]{2,1,0:T(8,128)(2,1)S(1)} %get-tuple-element.23), channel_id=1, source_target_pairs={{0,1},{1,0},{2,3},{3,2},{4,5},{5,4},{6,7},{7,6},{8,9},{9,8},{10,11... | collective-permute-start | bytes 884744 | tf_op jit(solution)/shard_map/ppermute | solution.py:519
  6.3 23.0 %collective-permute-start.1 = (bf16[2,48,1536]{2,1,0:T(8,128)(2,1)S(1)}, bf16[2,48,1536]{2,1,0:T(8,128)(2,1)S(1)}, u32[]{:S(2)}, u32[]{:S(2)}) collective-permute-start(bf16[2,48,1536]{2,1,0:T(8,128)(2,1)S(1)} %get-tuple-element.24), channel_id=1, source_target_pairs={{0,2},{2,4},{4,6},{1,3},{3,5},{5,7},{8,10},{10,12},{12,14},{9,11},... | collective-permute-start | bytes 884744 | tf_op jit(solution)/shard_map/ppermute | solution.py:545
  10.7 18.6 %collective-permute-start.2 = (bf16[2,48,1536]{2,1,0:T(8,128)(2,1)S(1)}, bf16[2,48,1536]{2,1,0:T(8,128)(2,1)S(1)}, u32[]{:S(2)}, u32[]{:S(2)}) collective-permute-start(bf16[2,48,1536]{2,1,0:T(8,128)(2,1)S(1)} %get-tuple-element.25), channel_id=1, source_target_pairs={{2,0},{4,2},{6,4},{3,1},{5,3},{7,5},{10,8},{12,10},{14,12},{11,9},... | collective-permute-start | bytes 884744 | tf_op jit(solution)/shard_map/ppermute | solution.py:546
  12.9 17.6 %copy-start.6 = (s32[48,2]{0,1:T(2,128)S(1)}, s32[48,2]{0,1:T(2,128)}, u32[]{:S(2)}) copy-start(s32[48,2]{0,1:T(2,128)} %param.15) | copy-start | bytes 1156
  17.9 11.4 %collective-permute-start.7 = (bf16[2,48,1024]{2,1,0:T(8,128)(2,1)S(1)}, bf16[2,48,1024]{2,1,0:T(8,128)(2,1)S(1)}, u32[]{:S(2)}, u32[]{:S(2)}) collective-permute-start(bf16[2,48,1024]{2,1,0:T(8,128)(2,1)S(1)} %get-tuple-element.32), channel_id=1, source_target_pairs={{0,2},{2,4},{4,6},{1,3},{3,5},{5,7},{8,10},{10,12},{12,14},{9,11},... | collective-permute-start | bytes 589832 | tf_op jit(solution)/shard_map/ppermute | solution.py:561
  23.5 7.0 %collective-permute-start.8 = (bf16[2,48,1024]{2,1,0:T(8,128)(2,1)S(1)}, bf16[2,48,1024]{2,1,0:T(8,128)(2,1)S(1)}, u32[]{:S(2)}, u32[]{:S(2)}) collective-permute-start(bf16[2,48,1024]{2,1,0:T(8,128)(2,1)S(1)} %get-tuple-element.33), channel_id=1, source_target_pairs={{2,0},{4,2},{6,4},{3,1},{5,3},{7,5},{10,8},{12,10},{14,12},{11,9},... | collective-permute-start | bytes 589832 | tf_op jit(solution)/shard_map/ppermute | solution.py:562
  25.6 14.1 %collective-permute-start.3 = (bf16[2,48,512]{2,1,0:T(8,128)(2,1)S(1)}, bf16[2,48,512]{2,1,0:T(8,128)(2,1)S(1)}, u32[]{:S(2)}, u32[]{:S(2)}) collective-permute-start(bf16[2,48,512]{2,1,0:T(8,128)(2,1)S(1)} %get-tuple-element.26), channel_id=1, source_target_pairs={{0,2},{2,4},{4,6},{1,3},{3,5},{5,7},{8,10},{10,12},{12,14},{9,11},... | collective-permute-start | bytes 294920 | tf_op jit(solution)/shard_map/ppermute | solution.py:561
  36.5 10.8 %collective-permute-start.9 = (bf16[96,1024]{1,0:T(8,128)(2,1)S(1)}, bf16[96,1024]{1,0:T(8,128)(2,1)S(1)}, u32[]{:S(2)}, u32[]{:S(2)}) collective-permute-start(bf16[96,1024]{1,0:T(8,128)(2,1)S(1)} %get-tuple-element.36), channel_id=1, source_target_pairs={{0,1},{1,0},{2,3},{3,2},{4,5},{5,4},{6,7},{7,6},{8,9},{9,8},{10,11... | collective-permute-start | bytes 589832 | tf_op jit(solution)/shard_map/ppermute | solution.py:594
  37.8 5.9 %collective-permute-start.4 = (bf16[2,48,512]{2,1,0:T(8,128)(2,1)S(1)}, bf16[2,48,512]{2,1,0:T(8,128)(2,1)S(1)}, u32[]{:S(2)}, u32[]{:S(2)}) collective-permute-start(bf16[2,48,512]{2,1,0:T(8,128)(2,1)S(1)} %get-tuple-element.27), channel_id=1, source_target_pairs={{2,0},{4,2},{6,4},{3,1},{5,3},{7,5},{10,8},{12,10},{14,12},{11,9},... | collective-permute-start | bytes 294920 | tf_op jit(solution)/shard_map/ppermute | solution.py:562
  46.9 3.5 %collective-permute-start.5 = (bf16[96,512]{1,0:T(8,128)(2,1)S(1)}, bf16[96,512]{1,0:T(8,128)(2,1)S(1)}, u32[]{:S(2)}, u32[]{:S(2)}) collective-permute-start(bf16[96,512]{1,0:T(8,128)(2,1)S(1)} %get-tuple-element.31), channel_id=1, source_target_pairs={{0,1},{1,0},{2,3},{3,2},{4,5},{5,4},{6,7},{7,6},{8,9},{9,8},{10,11... | collective-permute-start | bytes 294920 | tf_op jit(solution)/shard_map/ppermute | solution.py:594

commit v2 on v1

--- a/solution.py
+++ b/solution.py
@@ -8,6 +8,7 @@
 from jax.experimental import pallas as pl
 from jax.experimental.pallas import tpu as pltpu
 from jax.sharding import PartitionSpec as P
+
 
 HEAD_DIM = 64
 HALO = 3
@@ -187,7 +188,7 @@
 
 
 def general_body(queries, video_kv, text_kv, time_embed, gate_weight, window_extent, tile_valid):
-    frames, tile_rows, tile_cols, model_width = queries.shape
+    _, tile_rows, tile_cols, model_width = queries.shape
     head_count = model_width // HEAD_DIM
     score_scale = HEAD_DIM ** (-0.5)
     text_count = text_kv.shape[1]
@@ -220,8 +221,8 @@
 
 
 LANES = 128
-CHUNKS = (8, 4)
-UNROLL = 2
+CHUNKS = (7, 5)
+UNROLL = 4
 VMEM_LIMIT = 16 * 2**20
 
 
@@ -242,7 +243,7 @@
         copy.wait()
 
 
-def pack(q, kv, shapes, moves, name):
+def pack(q, kv, shapes, moves):
     return pl.pallas_call(
         partial(pack_kernel, moves=moves),
         out_shape=[jax.ShapeDtypeStruct(shape, q.dtype) for shape in shapes],
@@ -250,7 +251,6 @@
         out_specs=[pl.BlockSpec(memory_space=pltpu.VMEM)] * len(shapes),
         scratch_shapes=[pltpu.SemaphoreType.DMA((len(moves),))],
         compiler_params=pltpu.CompilerParams(vmem_limit_bytes=VMEM_LIMIT),
-        name=name,
     )(q, kv)
 
 
@@ -268,20 +268,37 @@
 
 
 def edges_kernel(select_ref, peer_ref, *refs):
-    bottom_ref, top_ref = refs[-2:]
-    cut_edges(select_ref, (peer_ref[1], peer_ref[2]), bottom_ref, top_ref)
+    cut_edges(select_ref, (peer_ref[1], peer_ref[2]), *refs[-2:])
+
+
+def own_edges_kernel(select_ref, mine_ref, other_ref, bottom_ref, top_ref):
+    half = mine_ref.shape[2]
+    for ref, skip, low, high in (
+        (mine_ref, 0, 0, half),
+        (other_ref, 1, half, bottom_ref.shape[2]),
+    ):
+        cut_edges(
+            select_ref,
+            (ref[skip], ref[skip + 1]),
+            bottom_ref.at[:, :, low:high],
+            top_ref.at[:, :, low:high],
+        )
+
+
+def join_kernel(above_ref, below_ref, out_ref):
+    edge = above_ref.shape[1]
+    skip = above_ref.shape[2] - out_ref.shape[2]
+    for part in (0, 1):
+        out_ref[part, :edge] = above_ref[part, :, skip:]
+        out_ref[part, edge:] = below_ref[part, :, skip:]
 
 
 def prepare_kernel(
     valid_ref,
-    select_ref,
     key_ref,
     query_ref,
     time_ref,
     weight_ref,
-    kv_ref,
-    bottom_ref,
-    top_ref,
     bias_ref,
     gate_ref,
     ok_ref,
@@ -291,7 +308,6 @@
 ):
     row_at = lax.axis_index("th")
     col_at = lax.axis_index("tw")
-    cut_edges(select_ref, (kv_ref[0], kv_ref[1]), bottom_ref, top_ref)
     key_row, key_local, key_col, key_block = (key_ref[i : i + 1] for i in range(4))
     query_row, query_col, query_peer = (query_ref[:, i : i + 1] for i in range(3))
     key_peer = key_block % 2
@@ -339,59 +355,61 @@
     peer_ref,
     above_mine_ref,
     below_mine_ref,
-    above_peer_ref,
-    below_peer_ref,
     text_ref,
     bias_ref,
     gate_ref,
     ok_ref,
-    own_out_ref,
-    peer_out_ref,
-    key_ref,
-    value_ref,
-    *,
+    *refs,
     first_pair,
     pairs,
     unroll,
     text_count,
     score_scale,
 ):
+    *edges, own_out_ref, peer_out_ref, key_ref, value_ref = refs
+    above_peer, below_peer = edges[0], edges[-1]
     count = mine_q_ref.shape[1]
     edge = above_mine_ref.shape[1]
     near = 2 * count + 4 * edge
     first_head = lax.axis_index("tw") * (2 * gate_ref.shape[0])
     left = lax.broadcasted_iota(jnp.int32, (1, LANES), 1) < HEAD_DIM
     zero = jnp.zeros((), jnp.bfloat16)
-    one = jnp.ones((), jnp.bfloat16)
     text_rows = text_ref.shape[1]
     text_bias = jnp.where(
         lax.broadcasted_iota(jnp.int32, (1, text_rows), 1) < text_count, 0.0, NEG
     )
 
-    def one_pair(turn, slot):
-        here = pl.ds(pl.multiple_of(turn * LANES, LANES), LANES)
-        whole = pl.ds(pl.multiple_of((first_pair + turn) * LANES, LANES), LANES)
+    def lanes_of(turn):
+        start = turn * LANES
+        if not isinstance(start, int):
+            start = pl.multiple_of(start, LANES)
+        return pl.ds(start, LANES)
+
+    def score(turn, slot):
+        here, whole = lanes_of(turn), lanes_of(first_pair + turn)
         for part, into in ((0, key_ref.at[slot]), (1, value_ref.at[slot])):
             into[0:count] = mine_kv_ref[part, :, whole]
             into[count : 2 * count] = peer_ref[1 + part, :, here]
             at = 2 * count
-            for ref, lanes in (
-                (above_mine_ref, whole),
-                (above_peer_ref, here),
-                (below_mine_ref, whole),
-                (below_peer_ref, here),
+            for ref, low, lanes in (
+                (above_mine_ref, 0, whole),
+                (above_peer, 0, here),
+                (below_mine_ref, 0, whole),
+                (below_peer, below_peer.shape[1] - edge, here),
             ):
-                into[at : at + edge] = ref[part, :, lanes]
+                into[at : at + edge] = ref[part, low : low + edge, lanes]
                 at += edge
             into[near:] = text_ref[part, :, whole]
         queries = jnp.concatenate([mine_q_ref[0, :, whole], peer_ref[0, :, here]], 0)
         queries = queries * jnp.asarray(score_scale, jnp.bfloat16)
         queries = jnp.concatenate([jnp.where(left, queries, zero), jnp.where(left, zero, queries)], 0)
-        both = lax.dot_general(
+        return lax.dot_general(
             queries, key_ref[slot], (((1,), (1,)), ((), ())), preferred_element_type=jnp.float32
         )
-        values = value_ref[slot]
-        outs = []
+
+    def mix(turn, slot, both):
+        here = lanes_of(turn)
+        weights, shares = [], []
         for side in (0, 1):
             head = first_head + 2 * (first_pair + turn) + side
             reach_rows = jnp.clip(extent_ref[0, head], 1, HALO) - 1
@@ -399,27 +417,36 @@
             bias = bias_ref[reach_rows * HALO + reach_cols]
             scores = both[2 * count * side : 2 * count * (side + 1)]
             scores = jnp.concatenate([scores[:, :near] + bias, scores[:, near:] + text_bias], 1)
-            top = jnp.max(scores, axis=-1, keepdims=True)
-            weights = jnp.exp(scores - top).astype(jnp.bfloat16)
-            summed = jnp.where(left, values, one) if side == 0 else jnp.where(left, one, values)
-            outs.append(
-                lax.dot_general(
-                    weights, summed, (((1,), (0,)), ((), ())), preferred_element_type=jnp.float32
-                )
-            )
-        total = pltpu.roll(jnp.where(left, outs[1], outs[0]), HEAD_DIM, 1)
-        attended = jnp.where(left, outs[0], outs[1]) / total
+            terms = jnp.exp(scores - jnp.max(scores, axis=-1, keepdims=True))
+            shares.append(1.0 / jnp.sum(terms, axis=-1, keepdims=True))
+            weights.append(terms.astype(jnp.bfloat16))
+        sums = lax.dot_general(
+            jnp.concatenate(weights, 0),
+            value_ref[slot],
+            (((1,), (0,)), ((), ())),
+            preferred_element_type=jnp.float32,
+        )
+        attended = jnp.where(left, sums[: 2 * count] * shares[0], sums[2 * count :] * shares[1])
         gated = jnp.where(ok_ref[...] > 0.0, attended * gate_ref[first_pair + turn], 0.0)
         gated = gated.astype(jnp.bfloat16)
         own_out_ref[:, here] = gated[:count]
         peer_out_ref[:, here] = gated[count:]
 
-    def some_pairs(turn, carry):
-        for slot in range(unroll):
-            one_pair(turn * unroll + slot, slot)
-        return carry
-
-    lax.fori_loop(0, pairs // unroll, some_pairs, 0)
+    def some_pairs(first, size):
+        turns = [(first + slot, slot) for slot in range(size)]
+        scored = [score(*turn) for turn in turns]
+        for turn, both in zip(turns, scored):
+            mix(*turn, both)
+
+    steps = -(-pairs // unroll)
+    low, extra = divmod(pairs, steps)
+    if extra:
+        at = 0
+        for step in range(steps):
+            some_pairs(at, low + (step < extra))
+            at += low + (step < extra)
+    else:
+        lax.fori_loop(0, steps, lambda step, _: some_pairs(step * low, low), None)
 
 
 def place_kernel(*refs, moves):
@@ -438,7 +465,7 @@
         copy.wait()
 
 
-def place(pieces, base, shape, moves, name):
+def place(pieces, base, shape, moves):
     vmem = pl.BlockSpec(memory_space=pltpu.VMEM)
     hbm = pl.BlockSpec(memory_space=pltpu.HBM)
     rest = () if base is None else (base,)
@@ -450,7 +477,6 @@
         scratch_shapes=[pltpu.SemaphoreType.DMA((len(moves),))],
         input_output_aliases={} if base is None else {len(pieces): 0},
         compiler_params=pltpu.CompilerParams(vmem_limit_bytes=VMEM_LIMIT),
-        name=name,
     )(*pieces, *rest)
 
 
@@ -498,6 +524,8 @@
     key_places, query_places, select = places(frames, tile_rows, tile_cols, edge_rows)
     q = jnp.transpose(queries, (0, 2, 1, 3)).reshape(1, count, model_width)
     kv = jnp.transpose(video_kv, (0, 1, 3, 2, 4)).reshape(2, count, model_width)
+    q = pltpu.with_memory_space_constraint(q, pltpu.HBM)
+    kv = pltpu.with_memory_space_constraint(kv, pltpu.HBM)
     total_pairs = half // LANES
     pieces = []
     first = 0
@@ -506,61 +534,77 @@
         pieces.append((first, pairs))
         first += pairs
     head, tail = slice(0, 1), slice(1, 3)
-    arrived = []
-    for at, (first, pairs) in enumerate(pieces):
-        low = first * LANES
-        shapes = [(3, count, pairs * LANES)]
-        moves = [(0, low, 0, head, True), (1, low, 0, tail, True)]
-        last = at == len(pieces) - 1
-        if last:
-            shapes += [(1, count, half), (2, count, half)]
-            moves += [(0, 0, 1, slice(0, 1), False), (1, 0, 2, slice(0, 2), False)]
-        packed = pack(q, kv, shapes, tuple(moves), "pack")
-        arrived.append(lax.ppermute(packed[0], "tw", swap))
-        if last:
-            mine_q, mine_kv = packed[1:]
-    edge_shape = jax.ShapeDtypeStruct((2, edge, half), jnp.bfloat16)
-    bottom, top, bias, gate, query_ok = pl.pallas_call(
+    (first, pairs), (last, rest) = pieces
+    low, width, end = first * LANES, pairs * LANES, rest * LANES
+    moves = ((0, low, 0, head, True), (1, low, 0, tail, True))
+    (sent,) = pack(q, kv, [(3, count, width)], moves)
+    arrived = [lax.ppermute(sent, "tw", swap)]
+    shapes = [(3, count, end), (1, count, half), (2, count, half)]
+    low = last * LANES
+    moves = (
+        (0, 0, 1, slice(0, 1), False),
+        (1, 0, 2, slice(0, 2), False),
+        (0, low, 0, head, True),
+        (1, low, 0, tail, True),
+    )
+    sent, mine_q, mine_kv = pack(q, kv, shapes, moves)
+    bottom, top = pl.pallas_call(
+        own_edges_kernel,
+        out_shape=[jax.ShapeDtypeStruct((2, edge, half + end), jnp.bfloat16)] * 2,
+        in_specs=[vmem] * 3,
+        out_specs=[vmem] * 2,
+        compiler_params=params,
+        name="own_edges",
+    )(select, mine_kv, sent)
+    above_mine = lax.ppermute(bottom, "th", down)
+    below_mine = lax.ppermute(top, "th", up)
+    arrived.append(lax.ppermute(sent, "tw", swap))
+    joined = pl.pallas_call(
+        join_kernel,
+        out_shape=jax.ShapeDtypeStruct((2, 2 * edge, end), jnp.bfloat16),
+        in_specs=[vmem] * 2,
+        out_specs=vmem,
+        compiler_params=params,
+        name="join",
+    )(above_mine, below_mine)
+    joined = lax.ppermute(joined, "tw", swap)
+    bias, gate, query_ok = pl.pallas_call(
         partial(prepare_kernel, tile_cols=tile_cols, tiles_down=tiles_down),
         out_shape=[
-            edge_shape,
-            edge_shape,
             jax.ShapeDtypeStruct((HALO * HALO, 2 * count, near), jnp.float32),
             jax.ShapeDtypeStruct((total_pairs, 1, LANES), jnp.float32),
             jax.ShapeDtypeStruct((2 * count, LANES), jnp.float32),
         ],
-        in_specs=[smem] + [vmem] * 6,
-        out_specs=[vmem] * 5,
+        in_specs=[smem] + [vmem] * 4,
+        out_specs=[vmem] * 3,
         compiler_params=params,
         name="prepare",
     )(
         jnp.transpose(tile_valid.reshape(tiles_down, 2, 2), (1, 2, 0)),
-        select,
         key_places,
         query_places,
         time_embed.reshape(1, -1),
         gate_weight,
-        mine_kv,
-    )
-    above_mine = lax.ppermute(bottom, "th", down)
-    below_mine = lax.ppermute(top, "th", up)
+    )
     text = jnp.pad(text_kv, ((0, 0), (0, text_rows - text_count), (0, 0)))
     extents = window_extent.T
     owned, returned = [], []
-    for (first, pairs), peer in zip(pieces, arrived):
+    for at, ((first, pairs), peer) in enumerate(zip(pieces, arrived)):
         width = pairs * LANES
-        edge_shape = jax.ShapeDtypeStruct((2, edge, width), jnp.bfloat16)
-        bottom, top = pl.pallas_call(
-            edges_kernel,
-            out_shape=[edge_shape] * 2,
-            in_specs=[vmem] * 2 + [pl.BlockSpec(memory_space=pl.ANY)],
-            out_specs=[vmem] * 2,
-            compiler_params=params,
-            name="edges",
-        )(select, peer, text)
-        above_peer = lax.ppermute(bottom, "th", down)
-        below_peer = lax.ppermute(top, "th", up)
-        unroll = math.gcd(pairs, UNROLL)
+        edges = (joined,)
+        if at == 0:
+            bottom, top = pl.pallas_call(
+                edges_kernel,
+                out_shape=[jax.ShapeDtypeStruct((2, edge, width), jnp.bfloat16)] * 2,
+                in_specs=[vmem] * 2 + [pl.BlockSpec(memory_space=pl.ANY)],
+                out_specs=[vmem] * 2,
+                compiler_params=params,
+                name="edges",
+            )(select, peer, text)
+            above_peer = lax.ppermute(bottom, "th", down)
+            below_peer = lax.ppermute(top, "th", up)
+            edges = (above_peer, below_peer)
+        unroll = min(pairs, UNROLL)
         own_out, peer_out = pl.pallas_call(
             partial(
                 attend_kernel,
@@ -571,11 +615,10 @@
                 score_scale=HEAD_DIM ** (-0.5),
             ),
             out_shape=[jax.ShapeDtypeStruct((count, width), jnp.bfloat16)] * 2,
-            in_specs=[smem] + [vmem] * 11,
+            in_specs=[smem] + [vmem] * (9 + len(edges)),
             out_specs=[vmem] * 2,
             scratch_shapes=[pltpu.VMEM((unroll, near + text_rows, LANES), jnp.bfloat16)] * 2,
             compiler_params=params,
-            name="attend",
         )(
             extents,
             mine_q,
@@ -583,12 +626,11 @@
             peer,
             above_mine,
             below_mine,
-            above_peer,
-            below_peer,
             text,
             bias,
             gate,
             query_ok,
+            *edges,
         )
         owned.append(own_out)
         returned.append(lax.ppermute(peer_out, "tw", swap))
@@ -596,9 +638,9 @@
     early = owned + returned[:-1]
     moves = [(i, low, False) for i, low in enumerate(starts)]
     moves += [(len(owned) + i, low, True) for i, low in enumerate(starts[:-1])]
-    result = place(early, None, (count, model_width), tuple(moves), "place")
+    result = place(early, None, (count, model_width), tuple(moves))
     moves = ((0, starts[-1], True),)
-    result = place(returned[-1:], result, (count, model_width), moves, "place_last")
+    result = place(returned[-1:], result, (count, model_width), moves)
     result = result.reshape(frames, tile_cols, tile_rows, model_width)
     return jnp.transpose(result, (0, 2, 1, 3))
 
@@ -613,7 +655,9 @@
         P(),
         P("vid", None, None),
     )
-    body = swapped_body if mesh.shape["tw"] == 2 else general_body
+    swapped = mesh.shape["tw"] == 2
+    body = swapped_body if swapped else general_body
+
     return jax.shard_map(
         body, mesh=mesh, in_specs=placed, out_specs=P("vid", "th", "tw", None), check_vma=False
     )

time: 51.4 us -> 41.5 us (0.81)
  starting transfers between devices: 23.2 us -> 14.6 us
  local copies, waits for them, and re-layouts: 2.62 us -> 0.3 us
  waiting for transfers between devices: 12.3 us -> 13.5 us
    ppermute x2 -> x1, starting transfers between devices: 9.24 us -> 2.05 us  [swapped_body(): above_peer = lax.ppermute(bottom, 'th', down)]
    ppermute x2 -> x3, waiting for transfers between devices: 4.71 us -> 0.01 us  [the longest x1 0.01 us: swapped_body(): arrived = [lax.ppermute(sent, 'tw', swap)]]
    ppermute x1, waiting for transfers between devices: 0.01 us -> 4.69 us  [swapped_body(): below_mine = lax.ppermute(top, 'th', up)]
    ppermute x1, waiting for transfers between devices: 0.01 us -> 2.74 us  [swapped_body(): above_mine = lax.ppermute(bottom, 'th', down)]
    unnamed x21 -> x17, local copies, waits for them, and re-layouts: 2.51 us -> 0.19 us
    pallas_call x2, Pallas kernels: 9.19 us -> 6.96 us  [swapped_body(): pl.pallas_call(partial(attend_kernel, first_pair=first, pairs=pairs, unro...]
    pallas_call x2, Pallas kernels: 0.26 us -> 2.38 us  [pack(): pl.pallas_call(partial(pack_kernel, moves=moves), out_shape=[jax.ShapeDty...]
    ppermute x2 -> x1, waiting for transfers between devices: 5.17 us -> 3.35 us  [swapped_body(): below_peer = lax.ppermute(top, 'th', up)]
  transfers between devices with their start and end apart: 10 -> 9, of which waited for: 4 -> 5; matrix products, arithmetic and copies ran while one was open for 0% -> 1% of each run, Pallas kernels for 23% -> 26%
where the time goes in v2:
time: 41.5 us; the launch traced here: 41.3 us
  starting transfers between devices  14.6 us (35%)
  waiting for transfers between devices  13.5 us (33%)
  Pallas kernels  12.6 us (30%)
    pallas_call x2, Pallas kernels, swapped_body(): pl.pallas_call(partial(attend_kernel, first_pair=first, pairs=pairs, unro...  6.96 us
    ppermute x1, waiting for transfers between devices, swapped_body(): below_mine = lax.ppermute(top, 'th', up)  4.69 us
    ppermute x1, starting transfers between devices, swapped_body(): above_mine = lax.ppermute(bottom, 'th', down)  3.96 us
    ppermute x1, waiting for transfers between devices, swapped_body(): below_peer = lax.ppermute(top, 'th', up)  3.35 us
    ppermute x1, waiting for transfers between devices, swapped_body(): above_mine = lax.ppermute(bottom, 'th', down)  2.74 us
    ppermute x2, waiting for transfers between devices, swapped_body(): returned.append(lax.ppermute(peer_out, 'tw', swap))  2.7 us
    ppermute x1, starting transfers between devices, swapped_body(): below_peer = lax.ppermute(top, 'th', up)  2.41 us
    pallas_call x2, Pallas kernels, pack(): pl.pallas_call(partial(pack_kernel, moves=moves), out_shape=[jax.ShapeDty...  2.38 us
  transfers between devices with their start and end apart: 9, of which 5 were waited for; matrix products, arithmetic and copies ran while one was open for 1% of the time, Pallas kernels for 26%

profile of v2, /device:TPU:1, one launch (start us, length us, event | category | flops | bytes accessed | tf_op | source)
XLA Modules:
  0.0 41.3 jit_solution(9931096619268501462)
XLA Ops:
  0.0 1.1 %shard_map.102 = bf16[3,96,896]{2,1,0:T(8,128)(2,1)S(1)} custom-call(bf16[1,96,3072]{2,1,0:T(8,128)(2,1)} %bitcast.16, bf16[2,96,3072]{2,1,0:T(8,128)(2,1)} %bitcast.14), custom_call_target="tpu_custom_call" | custom-call | tf_op jit(solution)/shard_map/pallas_call | solution.py:247
  1.1 2.1 %collective-permute-start.5 = (bf16[3,96,896]{2,1,0:T(8,128)(2,1)S(1)}, bf16[3,96,896]{2,1,0:T(8,128)(2,1)S(1)}, u32[]{:S(2)}, u32[]{:S(2)}) collective-permute-start(bf16[3,96,896]{2,1,0:T(8,128)(2,1)S(1)} %shard_map.102), channel_id=1, source_target_pairs={{0,1},{1,0},{2,3},{3,2},{4,5},{5,4},{6,7},{7,6},{8,9},{9,8},{10,11... | collective-permute-start | bytes 1548296 | tf_op jit(solution)/shard_map/ppermute | solution.py:541
  3.2 1.3 %shard_map.100 = (bf16[3,96,640]{2,1,0:T(8,128)(2,1)S(1)}, bf16[1,96,1536]{2,1,0:T(8,128)(2,1)S(1)}, bf16[2,96,1536]{2,1,0:T(8,128)(2,1)S(1)}) custom-call(bf16[1,96,3072]{2,1,0:T(8,128)(2,1)} %bitcast.17, bf16[2,96,3072]{2,1,0:T(8,128)(2,1)} %bitcast.15), custom_call_target="tpu_custom_call" | custom-call | tf_op jit(solution)/shard_map/pallas_call | solution.py:247
  4.5 0.4 own_edges.1
  4.9 4.0 %collective-permute-start.1 = (bf16[2,48,2176]{2,1,0:T(8,128)(2,1)S(1)}, bf16[2,48,2176]{2,1,0:T(8,128)(2,1)S(1)}, u32[]{:S(2)}, u32[]{:S(2)}) collective-permute-start(bf16[2,48,2176]{2,1,0:T(8,128)(2,1)S(1)} %get-tuple-element.22), channel_id=1, source_target_pairs={{0,2},{2,4},{4,6},{1,3},{3,5},{5,7},{8,10},{10,12},{12,14},{9,11},... | collective-permute-start | bytes 1253384 | tf_op jit(solution)/shard_map/ppermute | solution.py:559
  8.9 1.9 %collective-permute-start.2 = (bf16[2,48,2176]{2,1,0:T(8,128)(2,1)S(1)}, bf16[2,48,2176]{2,1,0:T(8,128)(2,1)S(1)}, u32[]{:S(2)}, u32[]{:S(2)}) collective-permute-start(bf16[2,48,2176]{2,1,0:T(8,128)(2,1)S(1)} %get-tuple-element.23), channel_id=1, source_target_pairs={{2,0},{4,2},{6,4},{3,1},{5,3},{7,5},{10,8},{12,10},{14,12},{11,9},... | collective-permute-start | bytes 1253384 | tf_op jit(solution)/shard_map/ppermute | solution.py:560
  10.8 0.3 collective-permute-start
  11.1 2.7 %collective-permute-done.1.above_ref.above_mine_ref = bf16[2,48,2176]{2,1,0:T(8,128)(2,1)S(1)} collective-permute-done((bf16[2,48,2176]{2,1,0:T(8,128)(2,1)S(1)}, bf16[2,48,2176]{2,1,0:T(8,128)(2,1)S(1)}, u32[]{:S(2)}, u32[]{:S(2)}) %collective-permute-start.1) | collective-permute-done | bytes 417824 | tf_op jit(solution)/shard_map/ppermute | solution.py:559
  13.8 4.7 %collective-permute-done.2.below_ref.below_mine_ref = bf16[2,48,2176]{2,1,0:T(8,128)(2,1)S(1)} collective-permute-done((bf16[2,48,2176]{2,1,0:T(8,128)(2,1)S(1)}, bf16[2,48,2176]{2,1,0:T(8,128)(2,1)S(1)}, u32[]{:S(2)}, u32[]{:S(2)}) %collective-permute-start.2) | collective-permute-done | bytes 417824 | tf_op jit(solution)/shard_map/ppermute | solution.py:560
  18.6 0.3 collective-permute-start.3
  18.9 0.1 copy.12
  19.0 0.1 pad.4.text_ref.refs_0_
  19.2 0.2 edges.1
  19.4 2.1 %collective-permute-start.6 = (bf16[2,48,896]{2,1,0:T(8,128)(2,1)S(1)}, bf16[2,48,896]{2,1,0:T(8,128)(2,1)S(1)}, u32[]{:S(2)}, u32[]{:S(2)}) collective-permute-start(bf16[2,48,896]{2,1,0:T(8,128)(2,1)S(1)} %get-tuple-element.28), channel_id=1, source_target_pairs={{0,2},{2,4},{4,6},{1,3},{3,5},{5,7},{8,10},{10,12},{12,14},{9,11},... | collective-permute-start | bytes 516104 | tf_op jit(solution)/shard_map/ppermute | solution.py:604
  21.5 2.4 %collective-permute-start.7 = (bf16[2,48,896]{2,1,0:T(8,128)(2,1)S(1)}, bf16[2,48,896]{2,1,0:T(8,128)(2,1)S(1)}, u32[]{:S(2)}, u32[]{:S(2)}) collective-permute-start(bf16[2,48,896]{2,1,0:T(8,128)(2,1)S(1)} %get-tuple-element.29), channel_id=1, source_target_pairs={{2,0},{4,2},{6,4},{3,1},{5,3},{7,5},{10,8},{12,10},{14,12},{11,9},... | collective-permute-start | bytes 516104 | tf_op jit(solution)/shard_map/ppermute | solution.py:605
  24.0 1.2 %prepare.1 = (f32[9,192,384]{2,1,0:T(8,128)S(1)}, f32[12,1,128]{2,1,0:T(1,128)S(1)}, f32[192,128]{1,0:T(8,128)S(1)}) custom-call(s32[2,2,4]{2,1,0:T(2,128)S(1)} %bitcast.13, s32[8,384]{1,0:T(8,128)S(1)} %copy-done.3, s32[192,8]{1,0:T(8,128)S(1)} %copy-done.2, bf16[1,512]{1,0:T(2,128)(2,1)S(1)} %reshape.14.time_ref, bf16[512,1536]{1,0:T(8,128)(2,1)S(1)} %copy-done), custom_call_target="tpu_custom_call" | custom-call | tf_op jit(solution)/shard_map/prepare/pallas_call | solution.py:571
  25.2 3.4 %collective-permute-done.7.refs_1_ = bf16[2,48,896]{2,1,0:T(8,128)(2,1)S(1)} collective-permute-done((bf16[2,48,896]{2,1,0:T(8,128)(2,1)S(1)}, bf16[2,48,896]{2,1,0:T(8,128)(2,1)S(1)}, u32[]{:S(2)}, u32[]{:S(2)}) %collective-permute-start.7) | collective-permute-done | bytes 172064 | tf_op jit(solution)/shard_map/ppermute | solution.py:605
  28.5 4.0 %shard_map.103 = (bf16[96,896]{1,0:T(8,128)(2,1)S(1)}, bf16[96,896]{1,0:T(8,128)(2,1)S(1)}) custom-call(s32[2,48]{1,0:T(2,128)S(1)} %bitcast.11, bf16[1,96,1536]{2,1,0:T(8,128)(2,1)S(1)} %get-tuple-element.19.mine_q_ref, bf16[2,96,1536]{2,1,0:T(8,128)(2,1)S(1)} %get-tuple-element.20.mine_ref.mine_kv_ref, ...), custom_call_target="tpu_custom_call" | custom-call | tf_op jit(solution)/shard_map/pallas_call | solution.py:608
  32.5 1.3 %collective-permute-start.8 = (bf16[96,896]{1,0:T(8,128)(2,1)S(1)}, bf16[96,896]{1,0:T(8,128)(2,1)S(1)}, u32[]{:S(2)}, u32[]{:S(2)}) collective-permute-start(bf16[96,896]{1,0:T(8,128)(2,1)S(1)} %get-tuple-element.32), channel_id=1, source_target_pairs={{0,1},{1,0},{2,3},{3,2},{4,5},{5,4},{6,7},{7,6},{8,9},{9,8},{10,11... | collective-permute-start | bytes 516104 | tf_op jit(solution)/shard_map/ppermute | solution.py:636
  33.8 3.0 %shard_map.101 = (bf16[96,640]{1,0:T(8,128)(2,1)S(1)}, bf16[96,640]{1,0:T(8,128)(2,1)S(1)}) custom-call(s32[2,48]{1,0:T(2,128)S(1)} %bitcast.12, bf16[1,96,1536]{2,1,0:T(8,128)(2,1)S(1)} %get-tuple-element.19.mine_q_ref, bf16[2,96,1536]{2,1,0:T(8,128)(2,1)S(1)} %get-tuple-element.20.mine_ref.mine_kv_ref, ...), custom_call_target="tpu_custom_call" | custom-call | tf_op jit(solution)/shard_map/pallas_call | solution.py:608
  36.8 0.3 collective-permute-start.4
  37.2 0.8 %shard_map.104.refs_1_ = bf16[96,3072]{1,0:T(8,128)(2,1)} custom-call(bf16[96,896]{1,0:T(8,128)(2,1)S(1)} %get-tuple-element.30.refs_0_, bf16[96,640]{1,0:T(8,128)(2,1)S(1)} %get-tuple-element.31.refs_1_, bf16[96,896]{1,0:T(8,128)(2,1)S(1)} %collective-permute-done.8.refs_2_), custom_call_target="tpu_custom_call" | custom-call | tf_op jit(solution)/shard_map/pallas_call | solution.py:472
  38.0 2.6 %collective-permute-done.4.refs_0_ = bf16[96,640]{1,0:T(8,128)(2,1)S(1)} collective-permute-done((bf16[96,640]{1,0:T(8,128)(2,1)S(1)}, bf16[96,640]{1,0:T(8,128)(2,1)S(1)}, u32[]{:S(2)}, u32[]{:S(2)}) %collective-permute-start.4) | collective-permute-done | bytes 122912 | tf_op jit(solution)/shard_map/ppermute | solution.py:636
  40.6 0.7 %shard_map.105 = bf16[96,3072]{1,0:T(8,128)(2,1)} custom-call(bf16[96,640]{1,0:T(8,128)(2,1)S(1)} %collective-permute-done.4.refs_0_, bf16[96,3072]{1,0:T(8,128)(2,1)} %shard_map.104.refs_1_), custom_call_target="tpu_custom_call", output_to_operand_aliasing={{}: (1, {})} | custom-call | tf_op jit(solution)/shard_map/pallas_call | solution.py:472
  (23 shorter events, 0.2 us)
Async XLA Ops:
  0.0 4.5 %copy-start.1 = (bf16[96,96]{1,0:T(8,128)(2,1)S(1)}, bf16[96,96]{1,0:T(8,128)(2,1)}, u32[]{:S(2)}) copy-start(bf16[96,96]{1,0:T(8,128)(2,1)} %constant.9.clone.select_ref) | copy-start | bytes 55300
  1.1 17.8 %copy-start.6 = (bf16[2,226,1536]{2,0,1:T(2,128)(2,1)S(1)}, bf16[2,226,1536]{2,0,1:T(2,128)(2,1)}, u32[]{:S(2)}) copy-start(bf16[2,226,1536]{2,0,1:T(2,128)(2,1)} %param.12) | copy-start | bytes 4165636
  1.1 18.1 %collective-permute-start.5 = (bf16[3,96,896]{2,1,0:T(8,128)(2,1)S(1)}, bf16[3,96,896]{2,1,0:T(8,128)(2,1)S(1)}, u32[]{:S(2)}, u32[]{:S(2)}) collective-permute-start(bf16[3,96,896]{2,1,0:T(8,128)(2,1)S(1)} %shard_map.102), channel_id=1, source_target_pairs={{0,1},{1,0},{2,3},{3,2},{4,5},{5,4},{6,7},{7,6},{8,9},{9,8},{10,11... | collective-permute-start | bytes 1548296 | tf_op jit(solution)/shard_map/ppermute | solution.py:541
  4.9 8.9 %collective-permute-start.1 = (bf16[2,48,2176]{2,1,0:T(8,128)(2,1)S(1)}, bf16[2,48,2176]{2,1,0:T(8,128)(2,1)S(1)}, u32[]{:S(2)}, u32[]{:S(2)}) collective-permute-start(bf16[2,48,2176]{2,1,0:T(8,128)(2,1)S(1)} %get-tuple-element.22), channel_id=1, source_target_pairs={{0,2},{2,4},{4,6},{1,3},{3,5},{5,7},{8,10},{10,12},{12,14},{9,11},... | collective-permute-start | bytes 1253384 | tf_op jit(solution)/shard_map/ppermute | solution.py:559
  8.9 9.7 %collective-permute-start.2 = (bf16[2,48,2176]{2,1,0:T(8,128)(2,1)S(1)}, bf16[2,48,2176]{2,1,0:T(8,128)(2,1)S(1)}, u32[]{:S(2)}, u32[]{:S(2)}) collective-permute-start(bf16[2,48,2176]{2,1,0:T(8,128)(2,1)S(1)} %get-tuple-element.23), channel_id=1, source_target_pairs={{2,0},{4,2},{6,4},{3,1},{5,3},{7,5},{10,8},{12,10},{14,12},{11,9},... | collective-permute-start | bytes 1253384 | tf_op jit(solution)/shard_map/ppermute | solution.py:560
  10.8 23.0 %collective-permute-start = (bf16[3,96,640]{2,1,0:T(8,128)(2,1)S(1)}, bf16[3,96,640]{2,1,0:T(8,128)(2,1)S(1)}, u32[]{:S(2)}, u32[]{:S(2)}) collective-permute-start(bf16[3,96,640]{2,1,0:T(8,128)(2,1)S(1)} %get-tuple-element.21.other_ref), channel_id=1, source_target_pairs={{0,1},{1,0},{2,3},{3,2},{4,5},{5,4},{6,7},{7,6},{8,9},{9,8},{10,11... | collective-permute-start | bytes 1105928 | tf_op jit(solution)/shard_map/ppermute | solution.py:561
  18.6 15.3 %collective-permute-start.3 = (bf16[2,96,640]{2,1,0:T(8,128)(2,1)S(1)}, bf16[2,96,640]{2,1,0:T(8,128)(2,1)S(1)}, u32[]{:S(2)}, u32[]{:S(2)}) collective-permute-start(bf16[2,96,640]{2,1,0:T(8,128)(2,1)S(1)} %join.1), channel_id=1, source_target_pairs={{0,1},{1,0},{2,3},{3,2},{4,5},{5,4},{6,7},{7,6},{8,9},{9,8},{10,11... | collective-permute-start | bytes 737288 | tf_op jit(solution)/shard_map/ppermute | solution.py:570
  19.1 4.8 %copy-start.7 = (bf16[512]{0:T(512)(128)(2,1)S(1)}, bf16[512]{0:T(512)(128)(2,1)}, u32[]{:S(2)}) copy-start(bf16[512]{0:T(512)(128)(2,1)} %param.13) | copy-start | bytes 3076
  19.1 4.8 %copy-start = (bf16[512,1536]{1,0:T(8,128)(2,1)S(1)}, bf16[512,1536]{1,0:T(8,128)(2,1)}, u32[]{:S(2)}) copy-start(bf16[512,1536]{1,0:T(8,128)(2,1)} %weight_ref.1) | copy-start | bytes 4718596
  19.1 4.8 %copy-start.2 = (s32[192,8]{1,0:T(8,128)S(1)}, s32[192,8]{1,0:T(8,128)}, u32[]{:S(2)}) copy-start(s32[192,8]{1,0:T(8,128)} %constant.11.clone.query_ref) | copy-start | bytes 18436
  19.1 4.8 %copy-start.3 = (s32[8,384]{1,0:T(8,128)S(1)}, s32[8,384]{1,0:T(8,128)}, u32[]{:S(2)}) copy-start(s32[8,384]{1,0:T(8,128)} %constant.10.clone.key_ref) | copy-start | bytes 36868
  19.2 4.8 %copy-start.5 = (s32[4,2,2]{0,2,1:T(2,128)S(1)}, s32[4,2,2]{0,2,1:T(2,128)}, u32[]{:S(2)}) copy-start(s32[4,2,2]{0,2,1:T(2,128)} %param.16) | copy-start | bytes 196
  19.2 9.4 %copy-start.4 = (s32[48,2]{0,1:T(2,128)S(1)}, s32[48,2]{0,1:T(2,128)}, u32[]{:S(2)}) copy-start(s32[48,2]{0,1:T(2,128)} %param.15) | copy-start | bytes 1156
  19.4 5.7 %collective-permute-start.6 = (bf16[2,48,896]{2,1,0:T(8,128)(2,1)S(1)}, bf16[2,48,896]{2,1,0:T(8,128)(2,1)S(1)}, u32[]{:S(2)}, u32[]{:S(2)}) collective-permute-start(bf16[2,48,896]{2,1,0:T(8,128)(2,1)S(1)} %get-tuple-element.28), channel_id=1, source_target_pairs={{0,2},{2,4},{4,6},{1,3},{3,5},{5,7},{8,10},{10,12},{12,14},{9,11},... | collective-permute-start | bytes 516104 | tf_op jit(solution)/shard_map/ppermute | solution.py:604
  21.5 7.0 %collective-permute-start.7 = (bf16[2,48,896]{2,1,0:T(8,128)(2,1)S(1)}, bf16[2,48,896]{2,1,0:T(8,128)(2,1)S(1)}, u32[]{:S(2)}, u32[]{:S(2)}) collective-permute-start(bf16[2,48,896]{2,1,0:T(8,128)(2,1)S(1)} %get-tuple-element.29), channel_id=1, source_target_pairs={{2,0},{4,2},{6,4},{3,1},{5,3},{7,5},{10,8},{12,10},{14,12},{11,9},... | collective-permute-start | bytes 516104 | tf_op jit(solution)/shard_map/ppermute | solution.py:605
  32.5 4.7 %collective-permute-start.8 = (bf16[96,896]{1,0:T(8,128)(2,1)S(1)}, bf16[96,896]{1,0:T(8,128)(2,1)S(1)}, u32[]{:S(2)}, u32[]{:S(2)}) collective-permute-start(bf16[96,896]{1,0:T(8,128)(2,1)S(1)} %get-tuple-element.32), channel_id=1, source_target_pairs={{0,1},{1,0},{2,3},{3,2},{4,5},{5,4},{6,7},{7,6},{8,9},{9,8},{10,11... | collective-permute-start | bytes 516104 | tf_op jit(solution)/shard_map/ppermute | solution.py:636
  36.8 3.8 %collective-permute-start.4 = (bf16[96,640]{1,0:T(8,128)(2,1)S(1)}, bf16[96,640]{1,0:T(8,128)(2,1)S(1)}, u32[]{:S(2)}, u32[]{:S(2)}) collective-permute-start(bf16[96,640]{1,0:T(8,128)(2,1)S(1)} %get-tuple-element.27), channel_id=1, source_target_pairs={{0,1},{1,0},{2,3},{3,2},{4,5},{5,4},{6,7},{7,6},{8,9},{9,8},{10,11... | collective-permute-start | bytes 368648 | tf_op jit(solution)/shard_map/ppermute | solution.py:636

commit v3 on v2

--- a/solution.py
+++ b/solution.py
@@ -223,6 +223,7 @@
 LANES = 128
 CHUNKS = (7, 5)
 UNROLL = 4
+TEXT_BLOCK = 6
 VMEM_LIMIT = 16 * 2**20
 
 
@@ -231,12 +232,12 @@
     col_at = lax.axis_index("tw")
     half = q_ref.shape[2] // 2
     copies = []
-    for at, (source, first, out, slot, other) in enumerate(moves):
+    for source, first, out, slot, other in moves:
         to = outs[out].at[slot]
         side = 1 - col_at if other else col_at
         lanes = pl.ds(pl.multiple_of(side * half + first, LANES), to.shape[2])
         ref = q_ref if source == 0 else kv_ref
-        copies.append(pltpu.make_async_copy(ref.at[:, :, lanes], to, sems.at[at]))
+        copies.append(pltpu.make_async_copy(ref.at[:, :, lanes], to, sems.at[len(copies)]))
     for copy in copies:
         copy.start()
     for copy in copies:
@@ -254,43 +255,34 @@
     )(q, kv)
 
 
-def cut_edges(select_ref, keys_values, bottom_ref, top_ref):
-    edge = bottom_ref.shape[1]
+def cut_edges(select, keys_values, *outs):
     for part in (0, 1):
         rows = lax.dot_general(
-            select_ref[...],
+            select,
             keys_values[part],
             (((1,), (0,)), ((), ())),
             preferred_element_type=jnp.float32,
         ).astype(jnp.bfloat16)
-        bottom_ref[part] = rows[:edge]
-        top_ref[part] = rows[edge:]
+        at = 0
+        for out in outs:
+            out[part] = rows[at : at + out.shape[1]]
+            at += out.shape[1]
 
 
 def edges_kernel(select_ref, peer_ref, *refs):
-    cut_edges(select_ref, (peer_ref[1], peer_ref[2]), *refs[-2:])
-
-
-def own_edges_kernel(select_ref, mine_ref, other_ref, bottom_ref, top_ref):
+    select = select_ref[lax.axis_index("th") % 2]
+    cut_edges(select, (peer_ref[1], peer_ref[2]), *refs[-2:])
+
+
+def own_edges_kernel(select_ref, mine_ref, late_ref, near_ref, far_ref, cross_ref):
     half = mine_ref.shape[2]
-    for ref, skip, low, high in (
-        (mine_ref, 0, 0, half),
-        (other_ref, 1, half, bottom_ref.shape[2]),
-    ):
-        cut_edges(
-            select_ref,
-            (ref[skip], ref[skip + 1]),
-            bottom_ref.at[:, :, low:high],
-            top_ref.at[:, :, low:high],
-        )
-
-
-def join_kernel(above_ref, below_ref, out_ref):
-    edge = above_ref.shape[1]
-    skip = above_ref.shape[2] - out_ref.shape[2]
-    for part in (0, 1):
-        out_ref[part, :edge] = above_ref[part, :, skip:]
-        out_ref[part, edge:] = below_ref[part, :, skip:]
+    select = select_ref[lax.axis_index("th") % 2]
+    cut_edges(select, (mine_ref[0], mine_ref[1]), near_ref.at[:, :, :half], far_ref)
+    cut_edges(select, (late_ref[1], late_ref[2]), near_ref.at[:, :, half:], cross_ref)
+
+
+def join_kernel(near_ref, out_ref):
+    out_ref[...] = near_ref[:, :, near_ref.shape[2] - out_ref.shape[2] :]
 
 
 def prepare_kernel(
@@ -303,18 +295,22 @@
     gate_ref,
     ok_ref,
     *,
+    tile_rows,
     tile_cols,
+    edge_rows,
     tiles_down,
 ):
     row_at = lax.axis_index("th")
     col_at = lax.axis_index("tw")
-    key_row, key_local, key_col, key_block = (key_ref[i : i + 1] for i in range(4))
+    key_local, key_col, key_block = (key_ref[i : i + 1] for i in range(3))
     query_row, query_col, query_peer = (query_ref[:, i : i + 1] for i in range(3))
     key_peer = key_block % 2
-    row_limit = jnp.zeros_like(key_row)
-    col_limit = jnp.zeros_like(key_row)
+    row_limit = jnp.zeros_like(key_local)
+    col_limit = jnp.zeros_like(key_local)
+    shift = jnp.zeros_like(key_local)
     query_limits = []
-    for at, step in enumerate((0, -1, 1)):
+    toward = 1 - 2 * (row_at % 2)
+    for at, step in enumerate((0, toward, -toward)):
         tile_row = row_at + step
         inside = (tile_row >= 0) & (tile_row < tiles_down)
         tile_row = jnp.clip(tile_row, 0, tiles_down - 1)
@@ -325,17 +321,22 @@
             block = 2 * at + peer
             row_limit = jnp.where(key_block == block, rows, row_limit)
             col_limit = jnp.where(key_block == block, cols, col_limit)
-            if step == 0:
+            if at == 0:
                 query_limits.append((rows, cols))
+            else:
+                shift = jnp.where(key_block == block, step, shift)
+    key_local = key_local + jnp.where(shift < 0, tile_rows - edge_rows, 0)
+    key_row = key_local + shift * tile_rows
     key_ok = (key_local < row_limit) & (key_col < col_limit)
     key_at = key_col + tile_cols * jnp.where(key_peer > 0, 1 - col_at, col_at)
     query_at = query_col + tile_cols * jnp.where(query_peer > 0, 1 - col_at, col_at)
     row_gap = jnp.abs(query_row - key_row)
+    text = key_block == TEXT_BLOCK
     col_gap = jnp.where(key_ok, jnp.abs(query_at - key_at), 2 * HALO + 1)
     for rows in range(HALO):
         for cols in range(HALO):
             near = (row_gap <= rows + 1) & (col_gap <= cols + 1)
-            bias_ref[rows * HALO + cols] = jnp.where(near, 0.0, NEG)
+            bias_ref[rows * HALO + cols] = jnp.where(near | text, 0.0, NEG)
     row_limit = jnp.where(query_peer > 0, query_limits[1][0], query_limits[0][0])
     col_limit = jnp.where(query_peer > 0, query_limits[1][1], query_limits[0][1])
     query_ok = (query_row < row_limit) & (query_col < col_limit)
@@ -353,8 +354,8 @@
     mine_q_ref,
     mine_kv_ref,
     peer_ref,
-    above_mine_ref,
-    below_mine_ref,
+    near_mine_ref,
+    far_mine_ref,
     text_ref,
     bias_ref,
     gate_ref,
@@ -363,21 +364,15 @@
     first_pair,
     pairs,
     unroll,
-    text_count,
     score_scale,
 ):
-    *edges, own_out_ref, peer_out_ref, key_ref, value_ref = refs
-    above_peer, below_peer = edges[0], edges[-1]
+    near_peer_ref, far_peer_ref, own_out_ref, peer_out_ref, key_ref, value_ref = refs
     count = mine_q_ref.shape[1]
-    edge = above_mine_ref.shape[1]
+    edge = near_mine_ref.shape[1]
     near = 2 * count + 4 * edge
     first_head = lax.axis_index("tw") * (2 * gate_ref.shape[0])
     left = lax.broadcasted_iota(jnp.int32, (1, LANES), 1) < HEAD_DIM
     zero = jnp.zeros((), jnp.bfloat16)
-    text_rows = text_ref.shape[1]
-    text_bias = jnp.where(
-        lax.broadcasted_iota(jnp.int32, (1, text_rows), 1) < text_count, 0.0, NEG
-    )
 
     def lanes_of(turn):
         start = turn * LANES
@@ -391,13 +386,13 @@
             into[0:count] = mine_kv_ref[part, :, whole]
             into[count : 2 * count] = peer_ref[1 + part, :, here]
             at = 2 * count
-            for ref, low, lanes in (
-                (above_mine_ref, 0, whole),
-                (above_peer, 0, here),
-                (below_mine_ref, 0, whole),
-                (below_peer, below_peer.shape[1] - edge, here),
+            for ref, lanes in (
+                (near_mine_ref, whole),
+                (near_peer_ref, here),
+                (far_mine_ref, whole),
+                (far_peer_ref, here),
             ):
-                into[at : at + edge] = ref[part, low : low + edge, lanes]
+                into[at : at + edge] = ref[part, :, lanes]
                 at += edge
             into[near:] = text_ref[part, :, whole]
         queries = jnp.concatenate([mine_q_ref[0, :, whole], peer_ref[0, :, here]], 0)
@@ -415,8 +410,7 @@
             reach_rows = jnp.clip(extent_ref[0, head], 1, HALO) - 1
             reach_cols = jnp.clip(extent_ref[1, head], 1, HALO) - 1
             bias = bias_ref[reach_rows * HALO + reach_cols]
-            scores = both[2 * count * side : 2 * count * (side + 1)]
-            scores = jnp.concatenate([scores[:, :near] + bias, scores[:, near:] + text_bias], 1)
+            scores = both[2 * count * side : 2 * count * (side + 1)] + bias
             terms = jnp.exp(scores - jnp.max(scores, axis=-1, keepdims=True))
             shares.append(1.0 / jnp.sum(terms, axis=-1, keepdims=True))
             weights.append(terms.astype(jnp.bfloat16))
@@ -480,48 +474,54 @@
     )(*pieces, *rest)
 
 
-def places(frames, tile_rows, tile_cols, edge_rows):
-    keys = []
-    for at, (step, low, high) in enumerate(
-        ((0, 0, tile_rows), (-1, tile_rows - edge_rows, tile_rows), (1, 0, edge_rows))
-    ):
-        shape = (frames, tile_cols, high - low)
-        row = np.broadcast_to(np.arange(low, high), shape).reshape(-1)
+def places(frames, tile_rows, tile_cols, edge, text_count, total):
+    groups = frames * tile_cols
+    blocks = []
+    for at, rows in enumerate((tile_rows, HALO, HALO)):
+        shape = (frames, tile_cols, rows)
+        row = np.broadcast_to(np.arange(rows), shape).reshape(-1)
         col = np.broadcast_to(np.arange(tile_cols)[:, None], shape).reshape(-1)
         for peer in (0, 1):
-            keys.append(np.stack([row + step * tile_rows, row, col, 0 * row + 2 * at + peer]))
-    query = np.concatenate(keys[:2], 1)[[0, 2, 3]]
-    keys = np.concatenate(keys, 1)
-    keys = np.concatenate([keys, 0 * keys]).astype(np.int32)
+            blocks.append(np.stack([row, col, 0 * row + 2 * at + peer]))
+            if at:
+                blocks.append(np.full((3, edge - groups * HALO), TEXT_BLOCK + 1))
+    blocks.append(np.full((3, text_count), TEXT_BLOCK))
+    query = np.concatenate([blocks[0], blocks[1]], 1)
+    used = sum(block.shape[1] for block in blocks)
+    blocks.append(np.full((3, total - used), TEXT_BLOCK + 1))
+    keys = np.concatenate([np.concatenate(blocks, 1), np.zeros((5, total))]).astype(np.int32)
     query = np.concatenate([query, np.zeros((5, query.shape[1]))]).T.astype(np.int32)
-    groups = np.arange(frames * tile_cols)[:, None] * tile_rows
-    rows = np.arange(edge_rows)[None, :]
-    chosen = np.concatenate(
-        [(groups + tile_rows - edge_rows + rows).reshape(-1), (groups + rows).reshape(-1)]
-    )
-    select = (chosen[:, None] == np.arange(frames * tile_cols * tile_rows)[None, :]).astype(
-        jnp.bfloat16
-    )
-    return keys, query, select
+    top = (np.arange(groups)[:, None] * tile_rows + np.arange(HALO)).reshape(-1)
+    bottom = top + tile_rows - HALO
+    rest = np.full(edge - groups * HALO, -1)
+    chosen = np.stack(
+        [np.concatenate([bottom, rest, top, rest]), np.concatenate([top, rest, bottom, rest])]
+    )
+    select = chosen[:, :, None] == np.arange(groups * tile_rows)
+    return keys, query, select.astype(jnp.bfloat16)
 
 
 def swapped_body(queries, video_kv, text_kv, time_embed, gate_weight, window_extent, tile_valid):
     frames, tile_rows, tile_cols, model_width = queries.shape
     half = model_width // 2
     count = frames * tile_rows * tile_cols
-    edge_rows = HALO + HALO % 2
-    edge = frames * tile_cols * edge_rows
-    near = 2 * count + 4 * edge
+    edge = -(-frames * tile_cols * HALO // 8) * 8
+    near_keys = 2 * count + 4 * edge
     text_count = text_kv.shape[1]
-    text_rows = -(-text_count // LANES) * LANES
+    total = -(-(near_keys + text_count) // LANES) * LANES
+    text_rows = total - near_keys
     tiles_down = lax.axis_size("th")
     swap = [(0, 1), (1, 0)]
-    down = [(i, i + 1) for i in range(tiles_down - 1)]
-    up = [(i + 1, i) for i in range(tiles_down - 1)]
+    near_pairs = [(i, i ^ 1) for i in range(tiles_down) if i ^ 1 < tiles_down]
+    far_pairs = [(i, ((i + 1) ^ 1) - 1) for i in range(1, tiles_down)]
+    far_pairs = [(i, j) for i, j in far_pairs if j < tiles_down]
+    cross_pairs = [(2 * i + t, 2 * j + 1 - t) for i, j in far_pairs for t in (0, 1)]
     vmem = pl.BlockSpec(memory_space=pltpu.VMEM)
     smem = pl.BlockSpec(memory_space=pltpu.SMEM)
     params = pltpu.CompilerParams(vmem_limit_bytes=VMEM_LIMIT)
-    key_places, query_places, select = places(frames, tile_rows, tile_cols, edge_rows)
+    key_places, query_places, select = places(
+        frames, tile_rows, tile_cols, edge, text_count, total
+    )
     q = jnp.transpose(queries, (0, 2, 1, 3)).reshape(1, count, model_width)
     kv = jnp.transpose(video_kv, (0, 1, 3, 2, 4)).reshape(2, count, model_width)
     q = pltpu.with_memory_space_constraint(q, pltpu.HBM)
@@ -537,8 +537,8 @@
     (first, pairs), (last, rest) = pieces
     low, width, end = first * LANES, pairs * LANES, rest * LANES
     moves = ((0, low, 0, head, True), (1, low, 0, tail, True))
-    (sent,) = pack(q, kv, [(3, count, width)], moves)
-    arrived = [lax.ppermute(sent, "tw", swap)]
+    (early,) = pack(q, kv, [(3, count, width)], moves)
+    arrived = [lax.ppermute(early, "tw", swap)]
     shapes = [(3, count, end), (1, count, half), (2, count, half)]
     low = last * LANES
     moves = (
@@ -548,30 +548,41 @@
         (1, low, 0, tail, True),
     )
     sent, mine_q, mine_kv = pack(q, kv, shapes, moves)
-    bottom, top = pl.pallas_call(
+    near, far, crossing = pl.pallas_call(
         own_edges_kernel,
-        out_shape=[jax.ShapeDtypeStruct((2, edge, half + end), jnp.bfloat16)] * 2,
+        out_shape=[
+            jax.ShapeDtypeStruct((2, edge, half + end), jnp.bfloat16),
+            jax.ShapeDtypeStruct((2, edge, half), jnp.bfloat16),
+            jax.ShapeDtypeStruct((2, edge, end), jnp.bfloat16),
+        ],
         in_specs=[vmem] * 3,
-        out_specs=[vmem] * 2,
+        out_specs=[vmem] * 3,
         compiler_params=params,
         name="own_edges",
     )(select, mine_kv, sent)
-    above_mine = lax.ppermute(bottom, "th", down)
-    below_mine = lax.ppermute(top, "th", up)
+    crossed = lax.ppermute(crossing, ("th", "tw"), cross_pairs)
+    near_mine = lax.ppermute(near, "th", near_pairs)
+    far_mine = lax.ppermute(far, "th", far_pairs)
     arrived.append(lax.ppermute(sent, "tw", swap))
     joined = pl.pallas_call(
         join_kernel,
-        out_shape=jax.ShapeDtypeStruct((2, 2 * edge, end), jnp.bfloat16),
-        in_specs=[vmem] * 2,
+        out_shape=jax.ShapeDtypeStruct((2, edge, end), jnp.bfloat16),
+        in_specs=[vmem],
         out_specs=vmem,
         compiler_params=params,
         name="join",
-    )(above_mine, below_mine)
+    )(near_mine)
     joined = lax.ppermute(joined, "tw", swap)
     bias, gate, query_ok = pl.pallas_call(
-        partial(prepare_kernel, tile_cols=tile_cols, tiles_down=tiles_down),
+        partial(
+            prepare_kernel,
+            tile_rows=tile_rows,
+            tile_cols=tile_cols,
+            edge_rows=HALO,
+            tiles_down=tiles_down,
+        ),
         out_shape=[
-            jax.ShapeDtypeStruct((HALO * HALO, 2 * count, near), jnp.float32),
+            jax.ShapeDtypeStruct((HALO * HALO, 2 * count, total), jnp.float32),
             jax.ShapeDtypeStruct((total_pairs, 1, LANES), jnp.float32),
             jax.ShapeDtypeStruct((2 * count, LANES), jnp.float32),
         ],
@@ -591,9 +602,9 @@
     owned, returned = [], []
     for at, ((first, pairs), peer) in enumerate(zip(pieces, arrived)):
         width = pairs * LANES
-        edges = (joined,)
+        near_peer, far_peer = joined, crossed
         if at == 0:
-            bottom, top = pl.pallas_call(
+            near, far = pl.pallas_call(
                 edges_kernel,
                 out_shape=[jax.ShapeDtypeStruct((2, edge, width), jnp.bfloat16)] * 2,
                 in_specs=[vmem] * 2 + [pl.BlockSpec(memory_space=pl.ANY)],
@@ -601,9 +612,8 @@
                 compiler_params=params,
                 name="edges",
             )(select, peer, text)
-            above_peer = lax.ppermute(bottom, "th", down)
-            below_peer = lax.ppermute(top, "th", up)
-            edges = (above_peer, below_peer)
+            far_peer = lax.ppermute(far, "th", far_pairs)
+            near_peer = lax.ppermute(near, "th", near_pairs)
         unroll = min(pairs, UNROLL)
         own_out, peer_out = pl.pallas_call(
             partial(
@@ -611,26 +621,26 @@
                 first_pair=first,
                 pairs=pairs,
                 unroll=unroll,
-                text_count=text_count,
                 score_scale=HEAD_DIM ** (-0.5),
             ),
             out_shape=[jax.ShapeDtypeStruct((count, width), jnp.bfloat16)] * 2,
-            in_specs=[smem] + [vmem] * (9 + len(edges)),
+            in_specs=[smem] + [vmem] * 11,
             out_specs=[vmem] * 2,
-            scratch_shapes=[pltpu.VMEM((unroll, near + text_rows, LANES), jnp.bfloat16)] * 2,
+            scratch_shapes=[pltpu.VMEM((unroll, total, LANES), jnp.bfloat16)] * 2,
             compiler_params=params,
         )(
             extents,
             mine_q,
             mine_kv,
             peer,
-            above_mine,
-            below_mine,
+            near_mine,
+            far_mine,
             text,
             bias,
             gate,
             query_ok,
-            *edges,
+            near_peer,
+            far_peer,
         )
         owned.append(own_out)
         returned.append(lax.ppermute(peer_out, "tw", swap))

time: 41.5 us -> 39.6 us (0.954)
  waiting for transfers between devices: 13.5 us -> 7.76 us
  starting transfers between devices: 14.6 us -> 17.6 us
  Pallas kernels: 12.6 us -> 13.3 us
    ppermute x5 -> x6, waiting for transfers between devices: 10.8 us -> 4.86 us  [the longest x1 4.85 us: swapped_body(): arrived = [lax.ppermute(early, 'tw', swap)]]
    ppermute x5 -> x6, starting transfers between devices: 12.5 us -> 15.9 us  [the longest x1 3.58 us: swapped_body(): far_mine = lax.ppermute(far, 'th', far_pairs)]
    pallas_call x2, Pallas kernels: 1.19 us -> 2.01 us  [the longest x1 2 us: swapped_body(): pl.pallas_call(partial(prepare_kernel, tile_rows=tile_rows, tile_cols=til...]
  transfers between devices with their start and end apart: 9 -> 10, of which waited for: 5 -> 3; matrix products, arithmetic and copies ran while one was open for 1% -> 1% of each run, Pallas kernels for 26% -> 29%
where the time goes in v3:
time: 39.6 us; the launch traced here: 39.2 us
  starting transfers between devices  17.6 us (44%)
  Pallas kernels  13.3 us (34%)
  waiting for transfers between devices  7.76 us (20%)
    pallas_call x2, Pallas kernels, swapped_body(): pl.pallas_call(partial(attend_kernel, first_pair=first, pairs=pairs, unro...  6.88 us
    ppermute x1, waiting for transfers between devices, swapped_body(): arrived = [lax.ppermute(early, 'tw', swap)]  4.85 us
    ppermute x1, starting transfers between devices, swapped_body(): far_mine = lax.ppermute(far, 'th', far_pairs)  3.58 us
    ppermute x1, starting transfers between devices, swapped_body(): far_peer = lax.ppermute(far, 'th', far_pairs)  3.52 us
    ppermute x1, starting transfers between devices, swapped_body(): crossed = lax.ppermute(crossing, ('th', 'tw'), cross_pairs)  3.49 us
    ppermute x2, waiting for transfers between devices, swapped_body(): returned.append(lax.ppermute(peer_out, 'tw', swap))  2.9 us
    pallas_call x2, Pallas kernels, pack(): pl.pallas_call(partial(pack_kernel, moves=moves), out_shape=[jax.ShapeDty...  2.38 us
    ppermute x1, starting transfers between devices, swapped_body(): near_peer = lax.ppermute(near, 'th', near_pairs)  2.17 us
  transfers between devices with their start and end apart: 10, of which 3 were waited for; matrix products, arithmetic and copies ran while one was open for 1% of the time, Pallas kernels for 29%

profile of v3, /device:TPU:1, one launch (start us, length us, event | category | flops | bytes accessed | tf_op | source)
XLA Modules:
  0.0 39.2 jit_solution(2585014314243340469)
XLA Ops:
  0.0 1.1 %shard_map.102 = bf16[3,96,896]{2,1,0:T(8,128)(2,1)S(1)} custom-call(bf16[1,96,3072]{2,1,0:T(8,128)(2,1)} %bitcast.16, bf16[2,96,3072]{2,1,0:T(8,128)(2,1)} %bitcast.14), custom_call_target="tpu_custom_call" | custom-call | tf_op jit(solution)/shard_map/pallas_call | solution.py:248
  1.1 2.1 %collective-permute-start.6 = (bf16[3,96,896]{2,1,0:T(8,128)(2,1)S(1)}, bf16[3,96,896]{2,1,0:T(8,128)(2,1)S(1)}, u32[]{:S(2)}, u32[]{:S(2)}) collective-permute-start(bf16[3,96,896]{2,1,0:T(8,128)(2,1)S(1)} %shard_map.102), channel_id=1, source_target_pairs={{0,1},{1,0},{2,3},{3,2},{4,5},{5,4},{6,7},{7,6},{8,9},{9,8},{10,11... | collective-permute-start | bytes 1548296 | tf_op jit(solution)/shard_map/ppermute | solution.py:541
  3.2 1.3 %shard_map.100 = (bf16[3,96,640]{2,1,0:T(8,128)(2,1)S(1)}, bf16[1,96,1536]{2,1,0:T(8,128)(2,1)S(1)}, bf16[2,96,1536]{2,1,0:T(8,128)(2,1)S(1)}) custom-call(bf16[1,96,3072]{2,1,0:T(8,128)(2,1)} %bitcast.17, bf16[2,96,3072]{2,1,0:T(8,128)(2,1)} %bitcast.15), custom_call_target="tpu_custom_call" | custom-call | tf_op jit(solution)/shard_map/pallas_call | solution.py:248
  4.5 0.3 own_edges.1
  4.9 1.0 %collective-permute-start.1 = (bf16[2,40,2176]{2,1,0:T(8,128)(2,1)S(1)}, bf16[2,40,2176]{2,1,0:T(8,128)(2,1)S(1)}, u32[]{:S(2)}, u32[]{:S(2)}) collective-permute-start(bf16[2,40,2176]{2,1,0:T(8,128)(2,1)S(1)} %get-tuple-element.23), channel_id=1, source_target_pairs={{0,2},{2,0},{4,6},{6,4},{1,3},{3,1},{5,7},{7,5},{8,10},{10,8},{12,... | collective-permute-start | bytes 1044488 | tf_op jit(solution)/shard_map/ppermute | solution.py:564
  5.9 3.6 %collective-permute-start.2 = (bf16[2,40,1536]{2,1,0:T(8,128)(2,1)S(1)}, bf16[2,40,1536]{2,1,0:T(8,128)(2,1)S(1)}, u32[]{:S(2)}, u32[]{:S(2)}) collective-permute-start(bf16[2,40,1536]{2,1,0:T(8,128)(2,1)S(1)} %get-tuple-element.24), channel_id=1, source_target_pairs={{2,4},{4,2},{3,5},{5,3},{10,12},{12,10},{11,13},{13,11},{18,20},{2... | collective-permute-start | bytes 737288 | tf_op jit(solution)/shard_map/ppermute | solution.py:565
  9.5 0.1 copy.12
  9.7 0.1 pad.4.text_ref.refs_0_
  9.8 0.0 copy-start.2
  9.8 4.8 %collective-permute-done.6.peer_ref = bf16[3,96,896]{2,1,0:T(8,128)(2,1)S(1)} collective-permute-done((bf16[3,96,896]{2,1,0:T(8,128)(2,1)S(1)}, bf16[3,96,896]{2,1,0:T(8,128)(2,1)S(1)}, u32[]{:S(2)}, u32[]{:S(2)}) %collective-permute-start.6) | collective-permute-done | bytes 516128 | tf_op jit(solution)/shard_map/ppermute | solution.py:541
  14.7 0.2 edges.1
  14.9 2.2 %collective-permute-start.7 = (bf16[2,40,896]{2,1,0:T(8,128)(2,1)S(1)}, bf16[2,40,896]{2,1,0:T(8,128)(2,1)S(1)}, u32[]{:S(2)}, u32[]{:S(2)}) collective-permute-start(bf16[2,40,896]{2,1,0:T(8,128)(2,1)S(1)} %get-tuple-element.30), channel_id=1, source_target_pairs={{0,2},{2,0},{4,6},{6,4},{1,3},{3,1},{5,7},{7,5},{8,10},{10,8},{12,... | collective-permute-start | bytes 430088 | tf_op jit(solution)/shard_map/ppermute | solution.py:616
  17.1 3.5 %collective-permute-start.8 = (bf16[2,40,896]{2,1,0:T(8,128)(2,1)S(1)}, bf16[2,40,896]{2,1,0:T(8,128)(2,1)S(1)}, u32[]{:S(2)}, u32[]{:S(2)}) collective-permute-start(bf16[2,40,896]{2,1,0:T(8,128)(2,1)S(1)} %get-tuple-element.31), channel_id=1, source_target_pairs={{2,4},{4,2},{3,5},{5,3},{10,12},{12,10},{11,13},{13,11},{18,20},{2... | collective-permute-start | bytes 430088 | tf_op jit(solution)/shard_map/ppermute | solution.py:615
  20.6 3.5 %collective-permute-start.4 = (bf16[2,40,640]{2,1,0:T(8,128)(2,1)S(1)}, bf16[2,40,640]{2,1,0:T(8,128)(2,1)S(1)}, u32[]{:S(2)}, u32[]{:S(2)}) collective-permute-start(bf16[2,40,640]{2,1,0:T(8,128)(2,1)S(1)} %get-tuple-element.28), channel_id=1, source_target_pairs={{2,5},{3,4},{4,3},{5,2},{10,13},{11,12},{12,11},{13,10},{18,21},{1... | collective-permute-start | bytes 307208 | tf_op jit(solution)/shard_map/ppermute | solution.py:563
  24.2 0.1 collective-permute-start.3
  24.3 2.0 %prepare.1 = (f32[9,192,640]{2,1,0:T(8,128)S(1)}, f32[12,1,128]{2,1,0:T(1,128)S(1)}, f32[192,128]{1,0:T(8,128)S(1)}) custom-call(s32[2,2,4]{2,1,0:T(2,128)S(1)} %bitcast.13, s32[8,640]{1,0:T(8,128)S(1)} %copy-done.3, s32[192,8]{1,0:T(8,128)S(1)} %copy-done.2, bf16[1,512]{1,0:T(2,128)(2,1)S(1)} %reshape.14.time_ref, bf16[512,1536]{1,0:T(8,128)(2,1)S(1)} %copy-done), custom_call_target="tpu_custom_call" | custom-call | tf_op jit(solution)/shard_map/prepare/pallas_call | solution.py:576
  26.3 3.9 %shard_map.103 = (bf16[96,896]{1,0:T(8,128)(2,1)S(1)}, bf16[96,896]{1,0:T(8,128)(2,1)S(1)}) custom-call(s32[2,48]{1,0:T(2,128)S(1)} %bitcast.11, bf16[1,96,1536]{2,1,0:T(8,128)(2,1)S(1)} %get-tuple-element.20.mine_q_ref, bf16[2,96,1536]{2,1,0:T(8,128)(2,1)S(1)} %get-tuple-element.21.mine_ref.mine_kv_ref, ...), custom_call_target="tpu_custom_call" | custom-call | tf_op jit(solution)/shard_map/pallas_call | solution.py:618
  30.3 1.5 %collective-permute-start.9 = (bf16[96,896]{1,0:T(8,128)(2,1)S(1)}, bf16[96,896]{1,0:T(8,128)(2,1)S(1)}, u32[]{:S(2)}, u32[]{:S(2)}) collective-permute-start(bf16[96,896]{1,0:T(8,128)(2,1)S(1)} %get-tuple-element.34), channel_id=1, source_target_pairs={{0,1},{1,0},{2,3},{3,2},{4,5},{5,4},{6,7},{7,6},{8,9},{9,8},{10,11... | collective-permute-start | bytes 516104 | tf_op jit(solution)/shard_map/ppermute | solution.py:646
  31.8 2.9 %shard_map.101 = (bf16[96,640]{1,0:T(8,128)(2,1)S(1)}, bf16[96,640]{1,0:T(8,128)(2,1)S(1)}) custom-call(s32[2,48]{1,0:T(2,128)S(1)} %bitcast.12, bf16[1,96,1536]{2,1,0:T(8,128)(2,1)S(1)} %get-tuple-element.20.mine_q_ref, bf16[2,96,1536]{2,1,0:T(8,128)(2,1)S(1)} %get-tuple-element.21.mine_ref.mine_kv_ref, ...), custom_call_target="tpu_custom_call" | custom-call | tf_op jit(solution)/shard_map/pallas_call | solution.py:618
  34.7 0.1 collective-permute-start.5
  34.8 0.9 %collective-permute-done.9.refs_2_ = bf16[96,896]{1,0:T(8,128)(2,1)S(1)} collective-permute-done((bf16[96,896]{1,0:T(8,128)(2,1)S(1)}, bf16[96,896]{1,0:T(8,128)(2,1)S(1)}, u32[]{:S(2)}, u32[]{:S(2)}) %collective-permute-start.9) | collective-permute-done | bytes 172064 | tf_op jit(solution)/shard_map/ppermute | solution.py:646
  35.8 0.8 %shard_map.104.refs_1_ = bf16[96,3072]{1,0:T(8,128)(2,1)} custom-call(bf16[96,896]{1,0:T(8,128)(2,1)S(1)} %get-tuple-element.32.refs_0_, bf16[96,640]{1,0:T(8,128)(2,1)S(1)} %get-tuple-element.33.refs_1_, bf16[96,896]{1,0:T(8,128)(2,1)S(1)} %collective-permute-done.9.refs_2_), custom_call_target="tpu_custom_call" | custom-call | tf_op jit(solution)/shard_map/pallas_call | solution.py:466
  36.6 2.0 %collective-permute-done.5.refs_0_ = bf16[96,640]{1,0:T(8,128)(2,1)S(1)} collective-permute-done((bf16[96,640]{1,0:T(8,128)(2,1)S(1)}, bf16[96,640]{1,0:T(8,128)(2,1)S(1)}, u32[]{:S(2)}, u32[]{:S(2)}) %collective-permute-start.5) | collective-permute-done | bytes 122912 | tf_op jit(solution)/shard_map/ppermute | solution.py:646
  38.5 0.7 %shard_map.105 = bf16[96,3072]{1,0:T(8,128)(2,1)} custom-call(bf16[96,640]{1,0:T(8,128)(2,1)S(1)} %collective-permute-done.5.refs_0_, bf16[96,3072]{1,0:T(8,128)(2,1)} %shard_map.104.refs_1_), custom_call_target="tpu_custom_call", output_to_operand_aliasing={{}: (1, {})} | custom-call | tf_op jit(solution)/shard_map/pallas_call | solution.py:466
  (25 shorter events, 0.1 us)
Async XLA Ops:
  0.0 4.5 %copy-start.1 = (bf16[2,80,96]{2,1,0:T(8,128)(2,1)S(1)}, bf16[2,80,96]{2,1,0:T(8,128)(2,1)}, u32[]{:S(2)}) copy-start(bf16[2,80,96]{2,1,0:T(8,128)(2,1)} %constant.9.clone.select_ref) | copy-start | bytes 92164
  1.1 8.4 %copy-start.6 = (bf16[2,226,1536]{2,0,1:T(2,128)(2,1)S(1)}, bf16[2,226,1536]{2,0,1:T(2,128)(2,1)}, u32[]{:S(2)}) copy-start(bf16[2,226,1536]{2,0,1:T(2,128)(2,1)} %param.12) | copy-start | bytes 4165636
  1.1 13.6 %collective-permute-start.6 = (bf16[3,96,896]{2,1,0:T(8,128)(2,1)S(1)}, bf16[3,96,896]{2,1,0:T(8,128)(2,1)S(1)}, u32[]{:S(2)}, u32[]{:S(2)}) collective-permute-start(bf16[3,96,896]{2,1,0:T(8,128)(2,1)S(1)} %shard_map.102), channel_id=1, source_target_pairs={{0,1},{1,0},{2,3},{3,2},{4,5},{5,4},{6,7},{7,6},{8,9},{9,8},{10,11... | collective-permute-start | bytes 1548296 | tf_op jit(solution)/shard_map/ppermute | solution.py:541
  4.9 15.8 %collective-permute-start.1 = (bf16[2,40,2176]{2,1,0:T(8,128)(2,1)S(1)}, bf16[2,40,2176]{2,1,0:T(8,128)(2,1)S(1)}, u32[]{:S(2)}, u32[]{:S(2)}) collective-permute-start(bf16[2,40,2176]{2,1,0:T(8,128)(2,1)S(1)} %get-tuple-element.23), channel_id=1, source_target_pairs={{0,2},{2,0},{4,6},{6,4},{1,3},{3,1},{5,7},{7,5},{8,10},{10,8},{12,... | collective-permute-start | bytes 1044488 | tf_op jit(solution)/shard_map/ppermute | solution.py:564
  5.9 25.9 %collective-permute-start = (bf16[3,96,640]{2,1,0:T(8,128)(2,1)S(1)}, bf16[3,96,640]{2,1,0:T(8,128)(2,1)S(1)}, u32[]{:S(2)}, u32[]{:S(2)}) collective-permute-start(bf16[3,96,640]{2,1,0:T(8,128)(2,1)S(1)} %get-tuple-element.22.late_ref), channel_id=1, source_target_pairs={{0,1},{1,0},{2,3},{3,2},{4,5},{5,4},{6,7},{7,6},{8,9},{9,8},{10,11... | collective-permute-start | bytes 1105928 | tf_op jit(solution)/shard_map/ppermute | solution.py:566
  5.9 18.3 %collective-permute-start.2 = (bf16[2,40,1536]{2,1,0:T(8,128)(2,1)S(1)}, bf16[2,40,1536]{2,1,0:T(8,128)(2,1)S(1)}, u32[]{:S(2)}, u32[]{:S(2)}) collective-permute-start(bf16[2,40,1536]{2,1,0:T(8,128)(2,1)S(1)} %get-tuple-element.24), channel_id=1, source_target_pairs={{2,4},{4,2},{3,5},{5,3},{10,12},{12,10},{11,13},{13,11},{18,20},{2... | collective-permute-start | bytes 737288 | tf_op jit(solution)/shard_map/ppermute | solution.py:565
  9.8 14.5 %copy-start.7 = (bf16[512]{0:T(512)(128)(2,1)S(1)}, bf16[512]{0:T(512)(128)(2,1)}, u32[]{:S(2)}) copy-start(bf16[512]{0:T(512)(128)(2,1)} %param.13) | copy-start | bytes 3076
  9.8 14.5 %copy-start = (bf16[512,1536]{1,0:T(8,128)(2,1)S(1)}, bf16[512,1536]{1,0:T(8,128)(2,1)}, u32[]{:S(2)}) copy-start(bf16[512,1536]{1,0:T(8,128)(2,1)} %weight_ref.1) | copy-start | bytes 4718596
  9.8 14.5 %copy-start.2 = (s32[192,8]{1,0:T(8,128)S(1)}, s32[192,8]{1,0:T(8,128)}, u32[]{:S(2)}) copy-start(s32[192,8]{1,0:T(8,128)} %constant.11.clone.query_ref) | copy-start | bytes 18436
  9.8 14.5 %copy-start.3 = (s32[8,640]{1,0:T(8,128)S(1)}, s32[8,640]{1,0:T(8,128)}, u32[]{:S(2)}) copy-start(s32[8,640]{1,0:T(8,128)} %constant.10.clone.key_ref) | copy-start | bytes 61444
  9.8 14.5 %copy-start.5 = (s32[4,2,2]{0,2,1:T(2,128)S(1)}, s32[4,2,2]{0,2,1:T(2,128)}, u32[]{:S(2)}) copy-start(s32[4,2,2]{0,2,1:T(2,128)} %param.16) | copy-start | bytes 196
  14.9 11.4 %copy-start.4 = (s32[48,2]{0,1:T(2,128)S(1)}, s32[48,2]{0,1:T(2,128)}, u32[]{:S(2)}) copy-start(s32[48,2]{0,1:T(2,128)} %param.15) | copy-start | bytes 1156
  14.9 11.4 %collective-permute-start.7 = (bf16[2,40,896]{2,1,0:T(8,128)(2,1)S(1)}, bf16[2,40,896]{2,1,0:T(8,128)(2,1)S(1)}, u32[]{:S(2)}, u32[]{:S(2)}) collective-permute-start(bf16[2,40,896]{2,1,0:T(8,128)(2,1)S(1)} %get-tuple-element.30), channel_id=1, source_target_pairs={{0,2},{2,0},{4,6},{6,4},{1,3},{3,1},{5,7},{7,5},{8,10},{10,8},{12,... | collective-permute-start | bytes 430088 | tf_op jit(solution)/shard_map/ppermute | solution.py:616
  17.1 9.2 %collective-permute-start.8 = (bf16[2,40,896]{2,1,0:T(8,128)(2,1)S(1)}, bf16[2,40,896]{2,1,0:T(8,128)(2,1)S(1)}, u32[]{:S(2)}, u32[]{:S(2)}) collective-permute-start(bf16[2,40,896]{2,1,0:T(8,128)(2,1)S(1)} %get-tuple-element.31), channel_id=1, source_target_pairs={{2,4},{4,2},{3,5},{5,3},{10,12},{12,10},{11,13},{13,11},{18,20},{2... | collective-permute-start | bytes 430088 | tf_op jit(solution)/shard_map/ppermute | solution.py:615
  20.6 11.2 %collective-permute-start.4 = (bf16[2,40,640]{2,1,0:T(8,128)(2,1)S(1)}, bf16[2,40,640]{2,1,0:T(8,128)(2,1)S(1)}, u32[]{:S(2)}, u32[]{:S(2)}) collective-permute-start(bf16[2,40,640]{2,1,0:T(8,128)(2,1)S(1)} %get-tuple-element.28), channel_id=1, source_target_pairs={{2,5},{3,4},{4,3},{5,2},{10,13},{11,12},{12,11},{13,10},{18,21},{1... | collective-permute-start | bytes 307208 | tf_op jit(solution)/shard_map/ppermute | solution.py:563
  24.2 7.6 %collective-permute-start.3 = (bf16[2,40,640]{2,1,0:T(8,128)(2,1)S(1)}, bf16[2,40,640]{2,1,0:T(8,128)(2,1)S(1)}, u32[]{:S(2)}, u32[]{:S(2)}) collective-permute-start(bf16[2,40,640]{2,1,0:T(8,128)(2,1)S(1)} %join.1), channel_id=1, source_target_pairs={{0,1},{1,0},{2,3},{3,2},{4,5},{5,4},{6,7},{7,6},{8,9},{9,8},{10,11... | collective-permute-start | bytes 307208 | tf_op jit(solution)/shard_map/ppermute | solution.py:575
  30.3 5.5 %collective-permute-start.9 = (bf16[96,896]{1,0:T(8,128)(2,1)S(1)}, bf16[96,896]{1,0:T(8,128)(2,1)S(1)}, u32[]{:S(2)}, u32[]{:S(2)}) collective-permute-start(bf16[96,896]{1,0:T(8,128)(2,1)S(1)} %get-tuple-element.34), channel_id=1, source_target_pairs={{0,1},{1,0},{2,3},{3,2},{4,5},{5,4},{6,7},{7,6},{8,9},{9,8},{10,11... | collective-permute-start | bytes 516104 | tf_op jit(solution)/shard_map/ppermute | solution.py:646
  34.7 3.8 %collective-permute-start.5 = (bf16[96,640]{1,0:T(8,128)(2,1)S(1)}, bf16[96,640]{1,0:T(8,128)(2,1)S(1)}, u32[]{:S(2)}, u32[]{:S(2)}) collective-permute-start(bf16[96,640]{1,0:T(8,128)(2,1)S(1)} %get-tuple-element.29), channel_id=1, source_target_pairs={{0,1},{1,0},{2,3},{3,2},{4,5},{5,4},{6,7},{7,6},{8,9},{9,8},{10,11... | collective-permute-start | bytes 368648 | tf_op jit(solution)/shard_map/ppermute | solution.py:646

commit v4 on v3

--- a/solution.py
+++ b/solution.py
@@ -270,15 +270,19 @@
 
 
 def edges_kernel(select_ref, peer_ref, *refs):
-    select = select_ref[lax.axis_index("th") % 2]
-    cut_edges(select, (peer_ref[1], peer_ref[2]), *refs[-2:])
-
-
-def own_edges_kernel(select_ref, mine_ref, late_ref, near_ref, far_ref, cross_ref):
+    near_ref = refs[-1]
+    select = select_ref[lax.axis_index("th") % 2, : near_ref.shape[1]]
+    cut_edges(select, (peer_ref[1], peer_ref[2]), near_ref)
+
+
+def own_edges_kernel(
+    select_ref, mine_ref, early_ref, late_ref, near_ref, far_ref, first_ref, second_ref
+):
     half = mine_ref.shape[2]
     select = select_ref[lax.axis_index("th") % 2]
+    cut_edges(select[far_ref.shape[1] :], (early_ref[1], early_ref[2]), first_ref)
     cut_edges(select, (mine_ref[0], mine_ref[1]), near_ref.at[:, :, :half], far_ref)
-    cut_edges(select, (late_ref[1], late_ref[2]), near_ref.at[:, :, half:], cross_ref)
+    cut_edges(select, (late_ref[1], late_ref[2]), near_ref.at[:, :, half:], second_ref)
 
 
 def join_kernel(near_ref, out_ref):
@@ -548,19 +552,22 @@
         (1, low, 0, tail, True),
     )
     sent, mine_q, mine_kv = pack(q, kv, shapes, moves)
-    near, far, crossing = pl.pallas_call(
+    near, far, *crossing = pl.pallas_call(
         own_edges_kernel,
         out_shape=[
             jax.ShapeDtypeStruct((2, edge, half + end), jnp.bfloat16),
             jax.ShapeDtypeStruct((2, edge, half), jnp.bfloat16),
+            jax.ShapeDtypeStruct((2, edge, width), jnp.bfloat16),
             jax.ShapeDtypeStruct((2, edge, end), jnp.bfloat16),
         ],
-        in_specs=[vmem] * 3,
-        out_specs=[vmem] * 3,
+        in_specs=[vmem] * 4,
+        out_specs=[vmem] * 4,
         compiler_params=params,
         name="own_edges",
-    )(select, mine_kv, sent)
-    crossed = lax.ppermute(crossing, ("th", "tw"), cross_pairs)
+    )(select, mine_kv, early, sent)
+    crossed = []
+    for rows in crossing:
+        crossed.append(lax.ppermute(rows, ("th", "tw"), cross_pairs))
     near_mine = lax.ppermute(near, "th", near_pairs)
     far_mine = lax.ppermute(far, "th", far_pairs)
     arrived.append(lax.ppermute(sent, "tw", swap))
@@ -602,17 +609,16 @@
     owned, returned = [], []
     for at, ((first, pairs), peer) in enumerate(zip(pieces, arrived)):
         width = pairs * LANES
-        near_peer, far_peer = joined, crossed
+        near_peer, far_peer = joined, crossed[at]
         if at == 0:
-            near, far = pl.pallas_call(
+            near = pl.pallas_call(
                 edges_kernel,
-                out_shape=[jax.ShapeDtypeStruct((2, edge, width), jnp.bfloat16)] * 2,
+                out_shape=jax.ShapeDtypeStruct((2, edge, width), jnp.bfloat16),
                 in_specs=[vmem] * 2 + [pl.BlockSpec(memory_space=pl.ANY)],
-                out_specs=[vmem] * 2,
+                out_specs=vmem,
                 compiler_params=params,
                 name="edges",
             )(select, peer, text)
-            far_peer = lax.ppermute(far, "th", far_pairs)
             near_peer = lax.ppermute(near, "th", near_pairs)
         unroll = min(pairs, UNROLL)
         own_out, peer_out = pl.pallas_call(

time: 39.6 us -> 38.4 us (0.970)
  waiting for transfers between devices: 7.76 us -> 4.36 us
  starting transfers between devices: 17.6 us -> 19.9 us
    ppermute x1, waiting for transfers between devices: 4.85 us -> 1.63 us  [swapped_body(): arrived = [lax.ppermute(early, 'tw', swap)]]
    ppermute x1, starting transfers between devices: 2.17 us -> 3.7 us  [swapped_body(): near_peer = lax.ppermute(near, 'th', near_pairs)]
    ppermute x2, starting transfers between devices: 7.01 us -> 7.63 us  [swapped_body(): crossed.append(lax.ppermute(rows, ('th', 'tw'), cross_pairs))]
  transfers between devices with their start and end apart: 10 -> 10, of which waited for: 3 -> 3; matrix products, arithmetic and copies ran while one was open for 1% -> 1% of each run, Pallas kernels for 29% -> 30%
where the time goes in v4:
time: 38.4 us; the launch traced here: 38.2 us
  starting transfers between devices  19.9 us (52%)
  Pallas kernels  13.3 us (35%)
  waiting for transfers between devices  4.36 us (11%)
    ppermute x2, starting transfers between devices, swapped_body(): crossed.append(lax.ppermute(rows, ('th', 'tw'), cross_pairs))  7.63 us
    pallas_call x2, Pallas kernels, swapped_body(): pl.pallas_call(partial(attend_kernel, first_pair=first, pairs=pairs, unro...  6.89 us
    ppermute x1, starting transfers between devices, swapped_body(): near_peer = lax.ppermute(near, 'th', near_pairs)  3.7 us
    ppermute x1, starting transfers between devices, swapped_body(): far_mine = lax.ppermute(far, 'th', far_pairs)  3.59 us
    ppermute x2, waiting for transfers between devices, swapped_body(): returned.append(lax.ppermute(peer_out, 'tw', swap))  2.71 us
    pallas_call x2, Pallas kernels, pack(): pl.pallas_call(partial(pack_kernel, moves=moves), out_shape=[jax.ShapeDty...  2.38 us
    ppermute x1, starting transfers between devices, swapped_body(): arrived = [lax.ppermute(early, 'tw', swap)]  2.12 us
    pallas_call x1, Pallas kernels, swapped_body(): pl.pallas_call(partial(prepare_kernel, tile_rows=tile_rows, tile_cols=til...  1.99 us
  transfers between devices with their start and end apart: 10, of which 3 were waited for; matrix products, arithmetic and copies ran while one was open for 1% of the time, Pallas kernels for 30%

profile of v4, /device:TPU:1, one launch (start us, length us, event | category | flops | bytes accessed | tf_op | source)
XLA Modules:
  0.0 38.2 jit_solution(6866737166514748035)
XLA Ops:
  0.0 1.1 %shard_map.101.early_ref = bf16[3,96,896]{2,1,0:T(8,128)(2,1)S(1)} custom-call(bf16[1,96,3072]{2,1,0:T(8,128)(2,1)} %bitcast.16, bf16[2,96,3072]{2,1,0:T(8,128)(2,1)} %bitcast.14), custom_call_target="tpu_custom_call" | custom-call | tf_op jit(solution)/shard_map/pallas_call | solution.py:248
  1.1 2.1 %collective-permute-start.6 = (bf16[3,96,896]{2,1,0:T(8,128)(2,1)S(1)}, bf16[3,96,896]{2,1,0:T(8,128)(2,1)S(1)}, u32[]{:S(2)}, u32[]{:S(2)}) collective-permute-start(bf16[3,96,896]{2,1,0:T(8,128)(2,1)S(1)} %shard_map.101.early_ref), channel_id=1, source_target_pairs={{0,1},{1,0},{2,3},{3,2},{4,5},{5,4},{6,7},{7,6},{8,9},{9,8},{10,11... | collective-permute-start | bytes 1548296 | tf_op jit(solution)/shard_map/ppermute | solution.py:545
  3.2 1.3 %shard_map.100 = (bf16[3,96,640]{2,1,0:T(8,128)(2,1)S(1)}, bf16[1,96,1536]{2,1,0:T(8,128)(2,1)S(1)}, bf16[2,96,1536]{2,1,0:T(8,128)(2,1)S(1)}) custom-call(bf16[1,96,3072]{2,1,0:T(8,128)(2,1)} %bitcast.17, bf16[2,96,3072]{2,1,0:T(8,128)(2,1)} %bitcast.15), custom_call_target="tpu_custom_call" | custom-call | tf_op jit(solution)/shard_map/pallas_call | solution.py:248
  4.5 0.4 %own_edges.1 = (bf16[2,40,2176]{2,1,0:T(8,128)(2,1)S(1)}, bf16[2,40,1536]{2,1,0:T(8,128)(2,1)S(1)}, bf16[2,40,896]{2,1,0:T(8,128)(2,1)S(1)}, bf16[2,40,640]{2,1,0:T(8,128)(2,1)S(1)}) custom-call(bf16[2,80,96]{2,1,0:T(8,128)(2,1)S(1)} %copy-done.1, bf16[2,96,1536]{2,1,0:T(8,128)(2,1)S(1)} %get-tuple-element.20.mine_ref.mine_kv_ref, ...), custom_call_target="tpu_custom_call" | custom-call | tf_op jit(solution)/shard_map/own_edges/pallas_call | solution.py:555
  4.9 1.0 %collective-permute-start.1 = (bf16[2,40,2176]{2,1,0:T(8,128)(2,1)S(1)}, bf16[2,40,2176]{2,1,0:T(8,128)(2,1)S(1)}, u32[]{:S(2)}, u32[]{:S(2)}) collective-permute-start(bf16[2,40,2176]{2,1,0:T(8,128)(2,1)S(1)} %get-tuple-element.22), channel_id=1, source_target_pairs={{0,2},{2,0},{4,6},{6,4},{1,3},{3,1},{5,7},{7,5},{8,10},{10,8},{12,... | collective-permute-start | bytes 1044488 | tf_op jit(solution)/shard_map/ppermute | solution.py:571
  6.0 3.6 %collective-permute-start.2 = (bf16[2,40,1536]{2,1,0:T(8,128)(2,1)S(1)}, bf16[2,40,1536]{2,1,0:T(8,128)(2,1)S(1)}, u32[]{:S(2)}, u32[]{:S(2)}) collective-permute-start(bf16[2,40,1536]{2,1,0:T(8,128)(2,1)S(1)} %get-tuple-element.23), channel_id=1, source_target_pairs={{2,4},{4,2},{3,5},{5,3},{10,12},{12,10},{11,13},{13,11},{18,20},{2... | collective-permute-start | bytes 737288 | tf_op jit(solution)/shard_map/ppermute | solution.py:572
  9.6 3.1 %collective-permute-start.8 = (bf16[2,40,896]{2,1,0:T(8,128)(2,1)S(1)}, bf16[2,40,896]{2,1,0:T(8,128)(2,1)S(1)}, u32[]{:S(2)}, u32[]{:S(2)}) collective-permute-start(bf16[2,40,896]{2,1,0:T(8,128)(2,1)S(1)} %get-tuple-element.29), channel_id=1, source_target_pairs={{2,5},{3,4},{4,3},{5,2},{10,13},{11,12},{12,11},{13,10},{18,21},{1... | collective-permute-start | bytes 430088 | tf_op jit(solution)/shard_map/ppermute | solution.py:570
  12.7 0.1 copy.12
  12.9 0.1 pad.4.text_ref.refs_0_
  13.0 0.0 copy-start.2
  13.1 1.6 %collective-permute-done.6.peer_ref = bf16[3,96,896]{2,1,0:T(8,128)(2,1)S(1)} collective-permute-done((bf16[3,96,896]{2,1,0:T(8,128)(2,1)S(1)}, bf16[3,96,896]{2,1,0:T(8,128)(2,1)S(1)}, u32[]{:S(2)}, u32[]{:S(2)}) %collective-permute-start.6) | collective-permute-done | bytes 516128 | tf_op jit(solution)/shard_map/ppermute | solution.py:545
  14.7 0.2 edges.1
  14.9 3.7 %collective-permute-start.7 = (bf16[2,40,896]{2,1,0:T(8,128)(2,1)S(1)}, bf16[2,40,896]{2,1,0:T(8,128)(2,1)S(1)}, u32[]{:S(2)}, u32[]{:S(2)}) collective-permute-start(bf16[2,40,896]{2,1,0:T(8,128)(2,1)S(1)} %edges.1), channel_id=1, source_target_pairs={{0,2},{2,0},{4,6},{6,4},{1,3},{3,1},{5,7},{7,5},{8,10},{10,8},{12,... | collective-permute-start | bytes 430088 | tf_op jit(solution)/shard_map/ppermute | solution.py:622
  18.6 4.5 %collective-permute-start.4 = (bf16[2,40,640]{2,1,0:T(8,128)(2,1)S(1)}, bf16[2,40,640]{2,1,0:T(8,128)(2,1)S(1)}, u32[]{:S(2)}, u32[]{:S(2)}) collective-permute-start(bf16[2,40,640]{2,1,0:T(8,128)(2,1)S(1)} %get-tuple-element.27), channel_id=1, source_target_pairs={{2,5},{3,4},{4,3},{5,2},{10,13},{11,12},{12,11},{13,10},{18,21},{1... | collective-permute-start | bytes 307208 | tf_op jit(solution)/shard_map/ppermute | solution.py:570
  23.1 0.3 collective-permute-start.3
  23.5 2.0 %prepare.1 = (f32[9,192,640]{2,1,0:T(8,128)S(1)}, f32[12,1,128]{2,1,0:T(1,128)S(1)}, f32[192,128]{1,0:T(8,128)S(1)}) custom-call(s32[2,2,4]{2,1,0:T(2,128)S(1)} %bitcast.13, s32[8,640]{1,0:T(8,128)S(1)} %copy-done.3, s32[192,8]{1,0:T(8,128)S(1)} %copy-done.2, bf16[1,512]{1,0:T(2,128)(2,1)S(1)} %reshape.14.time_ref, bf16[512,1536]{1,0:T(8,128)(2,1)S(1)} %copy-done), custom_call_target="tpu_custom_call" | custom-call | tf_op jit(solution)/shard_map/prepare/pallas_call | solution.py:583
  25.5 3.9 %shard_map.103 = (bf16[96,896]{1,0:T(8,128)(2,1)S(1)}, bf16[96,896]{1,0:T(8,128)(2,1)S(1)}) custom-call(s32[2,48]{1,0:T(2,128)S(1)} %bitcast.11, bf16[1,96,1536]{2,1,0:T(8,128)(2,1)S(1)} %get-tuple-element.19.mine_q_ref, bf16[2,96,1536]{2,1,0:T(8,128)(2,1)S(1)} %get-tuple-element.20.mine_ref.mine_kv_ref, ...), custom_call_target="tpu_custom_call" | custom-call | tf_op jit(solution)/shard_map/pallas_call | solution.py:624
  29.4 1.3 %collective-permute-start.9 = (bf16[96,896]{1,0:T(8,128)(2,1)S(1)}, bf16[96,896]{1,0:T(8,128)(2,1)S(1)}, u32[]{:S(2)}, u32[]{:S(2)}) collective-permute-start(bf16[96,896]{1,0:T(8,128)(2,1)S(1)} %get-tuple-element.32), channel_id=1, source_target_pairs={{0,1},{1,0},{2,3},{3,2},{4,5},{5,4},{6,7},{7,6},{8,9},{9,8},{10,11... | collective-permute-start | bytes 516104 | tf_op jit(solution)/shard_map/ppermute | solution.py:652
  30.8 2.9 %shard_map.102 = (bf16[96,640]{1,0:T(8,128)(2,1)S(1)}, bf16[96,640]{1,0:T(8,128)(2,1)S(1)}) custom-call(s32[2,48]{1,0:T(2,128)S(1)} %bitcast.12, bf16[1,96,1536]{2,1,0:T(8,128)(2,1)S(1)} %get-tuple-element.19.mine_q_ref, bf16[2,96,1536]{2,1,0:T(8,128)(2,1)S(1)} %get-tuple-element.20.mine_ref.mine_kv_ref, ...), custom_call_target="tpu_custom_call" | custom-call | tf_op jit(solution)/shard_map/pallas_call | solution.py:624
  33.7 0.3 collective-permute-start.5
  34.0 0.1 collective-permute-done.9.refs_2_
  34.1 0.8 %shard_map.104.refs_1_ = bf16[96,3072]{1,0:T(8,128)(2,1)} custom-call(bf16[96,896]{1,0:T(8,128)(2,1)S(1)} %get-tuple-element.30.refs_0_, bf16[96,640]{1,0:T(8,128)(2,1)S(1)} %get-tuple-element.31.refs_1_, bf16[96,896]{1,0:T(8,128)(2,1)S(1)} %collective-permute-done.9.refs_2_), custom_call_target="tpu_custom_call" | custom-call | tf_op jit(solution)/shard_map/pallas_call | solution.py:470
  34.9 2.6 %collective-permute-done.5.refs_0_ = bf16[96,640]{1,0:T(8,128)(2,1)S(1)} collective-permute-done((bf16[96,640]{1,0:T(8,128)(2,1)S(1)}, bf16[96,640]{1,0:T(8,128)(2,1)S(1)}, u32[]{:S(2)}, u32[]{:S(2)}) %collective-permute-start.5) | collective-permute-done | bytes 122912 | tf_op jit(solution)/shard_map/ppermute | solution.py:652
  37.5 0.7 %shard_map.105 = bf16[96,3072]{1,0:T(8,128)(2,1)} custom-call(bf16[96,640]{1,0:T(8,128)(2,1)S(1)} %collective-permute-done.5.refs_0_, bf16[96,3072]{1,0:T(8,128)(2,1)} %shard_map.104.refs_1_), custom_call_target="tpu_custom_call", output_to_operand_aliasing={{}: (1, {})} | custom-call | tf_op jit(solution)/shard_map/pallas_call | solution.py:470
  (25 shorter events, 0.1 us)
Async XLA Ops:
  0.0 4.5 %copy-start.1 = (bf16[2,80,96]{2,1,0:T(8,128)(2,1)S(1)}, bf16[2,80,96]{2,1,0:T(8,128)(2,1)}, u32[]{:S(2)}) copy-start(bf16[2,80,96]{2,1,0:T(8,128)(2,1)} %constant.9.clone.select_ref) | copy-start | bytes 92164
  1.1 11.6 %copy-start.6 = (bf16[2,226,1536]{2,0,1:T(2,128)(2,1)S(1)}, bf16[2,226,1536]{2,0,1:T(2,128)(2,1)}, u32[]{:S(2)}) copy-start(bf16[2,226,1536]{2,0,1:T(2,128)(2,1)} %param.12) | copy-start | bytes 4165636
  1.1 13.6 %collective-permute-start.6 = (bf16[3,96,896]{2,1,0:T(8,128)(2,1)S(1)}, bf16[3,96,896]{2,1,0:T(8,128)(2,1)S(1)}, u32[]{:S(2)}, u32[]{:S(2)}) collective-permute-start(bf16[3,96,896]{2,1,0:T(8,128)(2,1)S(1)} %shard_map.101.early_ref), channel_id=1, source_target_pairs={{0,1},{1,0},{2,3},{3,2},{4,5},{5,4},{6,7},{7,6},{8,9},{9,8},{10,11... | collective-permute-start | bytes 1548296 | tf_op jit(solution)/shard_map/ppermute | solution.py:545
  4.9 13.7 %collective-permute-start.1 = (bf16[2,40,2176]{2,1,0:T(8,128)(2,1)S(1)}, bf16[2,40,2176]{2,1,0:T(8,128)(2,1)S(1)}, u32[]{:S(2)}, u32[]{:S(2)}) collective-permute-start(bf16[2,40,2176]{2,1,0:T(8,128)(2,1)S(1)} %get-tuple-element.22), channel_id=1, source_target_pairs={{0,2},{2,0},{4,6},{6,4},{1,3},{3,1},{5,7},{7,5},{8,10},{10,8},{12,... | collective-permute-start | bytes 1044488 | tf_op jit(solution)/shard_map/ppermute | solution.py:571
  6.0 24.8 %collective-permute-start = (bf16[3,96,640]{2,1,0:T(8,128)(2,1)S(1)}, bf16[3,96,640]{2,1,0:T(8,128)(2,1)S(1)}, u32[]{:S(2)}, u32[]{:S(2)}) collective-permute-start(bf16[3,96,640]{2,1,0:T(8,128)(2,1)S(1)} %get-tuple-element.21.late_ref), channel_id=1, source_target_pairs={{0,1},{1,0},{2,3},{3,2},{4,5},{5,4},{6,7},{7,6},{8,9},{9,8},{10,11... | collective-permute-start | bytes 1105928 | tf_op jit(solution)/shard_map/ppermute | solution.py:573
  6.0 19.5 %collective-permute-start.2 = (bf16[2,40,1536]{2,1,0:T(8,128)(2,1)S(1)}, bf16[2,40,1536]{2,1,0:T(8,128)(2,1)S(1)}, u32[]{:S(2)}, u32[]{:S(2)}) collective-permute-start(bf16[2,40,1536]{2,1,0:T(8,128)(2,1)S(1)} %get-tuple-element.23), channel_id=1, source_target_pairs={{2,4},{4,2},{3,5},{5,3},{10,12},{12,10},{11,13},{13,11},{18,20},{2... | collective-permute-start | bytes 737288 | tf_op jit(solution)/shard_map/ppermute | solution.py:572
  9.6 13.6 %collective-permute-start.8 = (bf16[2,40,896]{2,1,0:T(8,128)(2,1)S(1)}, bf16[2,40,896]{2,1,0:T(8,128)(2,1)S(1)}, u32[]{:S(2)}, u32[]{:S(2)}) collective-permute-start(bf16[2,40,896]{2,1,0:T(8,128)(2,1)S(1)} %get-tuple-element.29), channel_id=1, source_target_pairs={{2,5},{3,4},{4,3},{5,2},{10,13},{11,12},{12,11},{13,10},{18,21},{1... | collective-permute-start | bytes 430088 | tf_op jit(solution)/shard_map/ppermute | solution.py:570
  13.0 10.4 %copy-start.7 = (bf16[512]{0:T(512)(128)(2,1)S(1)}, bf16[512]{0:T(512)(128)(2,1)}, u32[]{:S(2)}) copy-start(bf16[512]{0:T(512)(128)(2,1)} %param.13) | copy-start | bytes 3076
  13.0 10.4 %copy-start = (bf16[512,1536]{1,0:T(8,128)(2,1)S(1)}, bf16[512,1536]{1,0:T(8,128)(2,1)}, u32[]{:S(2)}) copy-start(bf16[512,1536]{1,0:T(8,128)(2,1)} %weight_ref.1) | copy-start | bytes 4718596
  13.0 10.4 %copy-start.2 = (s32[192,8]{1,0:T(8,128)S(1)}, s32[192,8]{1,0:T(8,128)}, u32[]{:S(2)}) copy-start(s32[192,8]{1,0:T(8,128)} %constant.11.clone.query_ref) | copy-start | bytes 18436
  13.0 10.4 %copy-start.3 = (s32[8,640]{1,0:T(8,128)S(1)}, s32[8,640]{1,0:T(8,128)}, u32[]{:S(2)}) copy-start(s32[8,640]{1,0:T(8,128)} %constant.10.clone.key_ref) | copy-start | bytes 61444
  13.0 10.4 %copy-start.5 = (s32[4,2,2]{0,2,1:T(2,128)S(1)}, s32[4,2,2]{0,2,1:T(2,128)}, u32[]{:S(2)}) copy-start(s32[4,2,2]{0,2,1:T(2,128)} %param.16) | copy-start | bytes 196
  14.9 10.6 %copy-start.4 = (s32[48,2]{0,1:T(2,128)S(1)}, s32[48,2]{0,1:T(2,128)}, u32[]{:S(2)}) copy-start(s32[48,2]{0,1:T(2,128)} %param.15) | copy-start | bytes 1156
  14.9 10.6 %collective-permute-start.7 = (bf16[2,40,896]{2,1,0:T(8,128)(2,1)S(1)}, bf16[2,40,896]{2,1,0:T(8,128)(2,1)S(1)}, u32[]{:S(2)}, u32[]{:S(2)}) collective-permute-start(bf16[2,40,896]{2,1,0:T(8,128)(2,1)S(1)} %edges.1), channel_id=1, source_target_pairs={{0,2},{2,0},{4,6},{6,4},{1,3},{3,1},{5,7},{7,5},{8,10},{10,8},{12,... | collective-permute-start | bytes 430088 | tf_op jit(solution)/shard_map/ppermute | solution.py:622
  18.6 12.1 %collective-permute-start.4 = (bf16[2,40,640]{2,1,0:T(8,128)(2,1)S(1)}, bf16[2,40,640]{2,1,0:T(8,128)(2,1)S(1)}, u32[]{:S(2)}, u32[]{:S(2)}) collective-permute-start(bf16[2,40,640]{2,1,0:T(8,128)(2,1)S(1)} %get-tuple-element.27), channel_id=1, source_target_pairs={{2,5},{3,4},{4,3},{5,2},{10,13},{11,12},{12,11},{13,10},{18,21},{1... | collective-permute-start | bytes 307208 | tf_op jit(solution)/shard_map/ppermute | solution.py:570
  23.1 7.6 %collective-permute-start.3 = (bf16[2,40,640]{2,1,0:T(8,128)(2,1)S(1)}, bf16[2,40,640]{2,1,0:T(8,128)(2,1)S(1)}, u32[]{:S(2)}, u32[]{:S(2)}) collective-permute-start(bf16[2,40,640]{2,1,0:T(8,128)(2,1)S(1)} %join.1), channel_id=1, source_target_pairs={{0,1},{1,0},{2,3},{3,2},{4,5},{5,4},{6,7},{7,6},{8,9},{9,8},{10,11... | collective-permute-start | bytes 307208 | tf_op jit(solution)/shard_map/ppermute | solution.py:582
  29.4 4.6 %collective-permute-start.9 = (bf16[96,896]{1,0:T(8,128)(2,1)S(1)}, bf16[96,896]{1,0:T(8,128)(2,1)S(1)}, u32[]{:S(2)}, u32[]{:S(2)}) collective-permute-start(bf16[96,896]{1,0:T(8,128)(2,1)S(1)} %get-tuple-element.32), channel_id=1, source_target_pairs={{0,1},{1,0},{2,3},{3,2},{4,5},{5,4},{6,7},{7,6},{8,9},{9,8},{10,11... | collective-permute-start | bytes 516104 | tf_op jit(solution)/shard_map/ppermute | solution.py:652
  33.7 3.8 %collective-permute-start.5 = (bf16[96,640]{1,0:T(8,128)(2,1)S(1)}, bf16[96,640]{1,0:T(8,128)(2,1)S(1)}, u32[]{:S(2)}, u32[]{:S(2)}) collective-permute-start(bf16[96,640]{1,0:T(8,128)(2,1)S(1)} %get-tuple-element.28), channel_id=1, source_target_pairs={{0,1},{1,0},{2,3},{3,2},{4,5},{5,4},{6,7},{7,6},{8,9},{9,8},{10,11... | collective-permute-start | bytes 368648 | tf_op jit(solution)/shard_map/ppermute | solution.py:652

commit v5 on v4

--- a/solution.py
+++ b/solution.py
@@ -278,15 +278,10 @@
 def own_edges_kernel(
     select_ref, mine_ref, early_ref, late_ref, near_ref, far_ref, first_ref, second_ref
 ):
-    half = mine_ref.shape[2]
     select = select_ref[lax.axis_index("th") % 2]
     cut_edges(select[far_ref.shape[1] :], (early_ref[1], early_ref[2]), first_ref)
-    cut_edges(select, (mine_ref[0], mine_ref[1]), near_ref.at[:, :, :half], far_ref)
-    cut_edges(select, (late_ref[1], late_ref[2]), near_ref.at[:, :, half:], second_ref)
-
-
-def join_kernel(near_ref, out_ref):
-    out_ref[...] = near_ref[:, :, near_ref.shape[2] - out_ref.shape[2] :]
+    cut_edges(select, (mine_ref[0], mine_ref[1]), near_ref, far_ref)
+    cut_edges(select[far_ref.shape[1] :], (late_ref[1], late_ref[2]), second_ref)
 
 
 def prepare_kernel(
@@ -555,7 +550,7 @@
     near, far, *crossing = pl.pallas_call(
         own_edges_kernel,
         out_shape=[
-            jax.ShapeDtypeStruct((2, edge, half + end), jnp.bfloat16),
+            jax.ShapeDtypeStruct((2, edge, half), jnp.bfloat16),
             jax.ShapeDtypeStruct((2, edge, half), jnp.bfloat16),
             jax.ShapeDtypeStruct((2, edge, width), jnp.bfloat16),
             jax.ShapeDtypeStruct((2, edge, end), jnp.bfloat16),
@@ -571,15 +566,6 @@
     near_mine = lax.ppermute(near, "th", near_pairs)
     far_mine = lax.ppermute(far, "th", far_pairs)
     arrived.append(lax.ppermute(sent, "tw", swap))
-    joined = pl.pallas_call(
-        join_kernel,
-        out_shape=jax.ShapeDtypeStruct((2, edge, end), jnp.bfloat16),
-        in_specs=[vmem],
-        out_specs=vmem,
-        compiler_params=params,
-        name="join",
-    )(near_mine)
-    joined = lax.ppermute(joined, "tw", swap)
     bias, gate, query_ok = pl.pallas_call(
         partial(
             prepare_kernel,
@@ -609,17 +595,15 @@
     owned, returned = [], []
     for at, ((first, pairs), peer) in enumerate(zip(pieces, arrived)):
         width = pairs * LANES
-        near_peer, far_peer = joined, crossed[at]
-        if at == 0:
-            near = pl.pallas_call(
-                edges_kernel,
-                out_shape=jax.ShapeDtypeStruct((2, edge, width), jnp.bfloat16),
-                in_specs=[vmem] * 2 + [pl.BlockSpec(memory_space=pl.ANY)],
-                out_specs=vmem,
-                compiler_params=params,
-                name="edges",
-            )(select, peer, text)
-            near_peer = lax.ppermute(near, "th", near_pairs)
+        far_peer = crossed[at]
+        near = pl.pallas_call(
+            edges_kernel,
+            out_shape=jax.ShapeDtypeStruct((2, edge, width), jnp.bfloat16),
+            in_specs=[vmem] * 2 + [pl.BlockSpec(memory_space=pl.ANY)],
+            out_specs=vmem,
+            compiler_params=params,
+        )(select, peer, text)
+        near_peer = lax.ppermute(near, "th", near_pairs)
         unroll = min(pairs, UNROLL)
         own_out, peer_out = pl.pallas_call(
             partial(

time: 38.4 us -> 46.6 us (1.21)
  the two profiles are of different devices: /device:TPU:1 before, /device:TPU:0 now
where the time goes in v5:
time: 46.6 us; the launch traced here: 46.4 us
  waiting for transfers between devices  20.2 us (43%)
  Pallas kernels  13.9 us (30%)
  starting transfers between devices  11.8 us (25%)
    ppermute x1, waiting for transfers between devices, swapped_body(): arrived = [lax.ppermute(early, 'tw', swap)]  10.6 us
    pallas_call x2, Pallas kernels, swapped_body(): pl.pallas_call(partial(attend_kernel, first_pair=first, pairs=pairs, unro...  7.33 us
    ppermute x1, waiting for transfers between devices, swapped_body(): arrived.append(lax.ppermute(sent, 'tw', swap))  6.71 us
    ppermute x2, starting transfers between devices, swapped_body(): near_peer = lax.ppermute(near, 'th', near_pairs)  4.16 us
    ppermute x1, starting transfers between devices, swapped_body(): arrived = [lax.ppermute(early, 'tw', swap)]  3.06 us
    ppermute x2, waiting for transfers between devices, swapped_body(): returned.append(lax.ppermute(peer_out, 'tw', swap))  2.91 us
    pallas_call x2, Pallas kernels, pack(): pl.pallas_call(partial(pack_kernel, moves=moves), out_shape=[jax.ShapeDty...  2.38 us
    ppermute x2, starting transfers between devices, swapped_body(): returned.append(lax.ppermute(peer_out, 'tw', swap))  2.16 us
  transfers between devices with their start and end apart: 10, of which 4 were waited for; matrix products, arithmetic and copies ran while one was open for 1% of the time, Pallas kernels for 26%

profile of v5, /device:TPU:0, one launch (start us, length us, event | category | flops | bytes accessed | tf_op | source)
XLA Modules:
  0.0 46.4 jit_solution(13349642430961584701)
XLA Ops:
  0.0 1.1 %shard_map.101.early_ref = bf16[3,96,896]{2,1,0:T(8,128)(2,1)S(1)} custom-call(bf16[1,96,3072]{2,1,0:T(8,128)(2,1)} %bitcast.16, bf16[2,96,3072]{2,1,0:T(8,128)(2,1)} %bitcast.14), custom_call_target="tpu_custom_call" | custom-call | tf_op jit(solution)/shard_map/pallas_call | solution.py:248
  1.1 3.1 %collective-permute-start.6 = (bf16[3,96,896]{2,1,0:T(8,128)(2,1)S(1)}, bf16[3,96,896]{2,1,0:T(8,128)(2,1)S(1)}, u32[]{:S(2)}, u32[]{:S(2)}) collective-permute-start(bf16[3,96,896]{2,1,0:T(8,128)(2,1)S(1)} %shard_map.101.early_ref), channel_id=1, source_target_pairs={{0,1},{1,0},{2,3},{3,2},{4,5},{5,4},{6,7},{7,6},{8,9},{9,8},{10,11... | collective-permute-start | bytes 1548296 | tf_op jit(solution)/shard_map/ppermute | solution.py:540
  4.2 1.3 %shard_map.100 = (bf16[3,96,640]{2,1,0:T(8,128)(2,1)S(1)}, bf16[1,96,1536]{2,1,0:T(8,128)(2,1)S(1)}, bf16[2,96,1536]{2,1,0:T(8,128)(2,1)S(1)}) custom-call(bf16[1,96,3072]{2,1,0:T(8,128)(2,1)} %bitcast.17, bf16[2,96,3072]{2,1,0:T(8,128)(2,1)} %bitcast.15), custom_call_target="tpu_custom_call" | custom-call | tf_op jit(solution)/shard_map/pallas_call | solution.py:248
  5.5 0.2 collective-permute-start
  5.7 0.4 own_edges.1
  6.1 0.7 %collective-permute-start.2 = (bf16[2,40,1536]{2,1,0:T(8,128)(2,1)S(1)}, bf16[2,40,1536]{2,1,0:T(8,128)(2,1)S(1)}, u32[]{:S(2)}, u32[]{:S(2)}) collective-permute-start(bf16[2,40,1536]{2,1,0:T(8,128)(2,1)S(1)} %get-tuple-element.23), channel_id=1, source_target_pairs={{2,4},{4,2},{3,5},{5,3},{10,12},{12,10},{11,13},{13,11},{18,20},{2... | collective-permute-start | bytes 737288 | tf_op jit(solution)/shard_map/ppermute | solution.py:567
  6.8 0.7 %collective-permute-start.8 = (bf16[2,40,896]{2,1,0:T(8,128)(2,1)S(1)}, bf16[2,40,896]{2,1,0:T(8,128)(2,1)S(1)}, u32[]{:S(2)}, u32[]{:S(2)}) collective-permute-start(bf16[2,40,896]{2,1,0:T(8,128)(2,1)S(1)} %get-tuple-element.29), channel_id=1, source_target_pairs={{2,5},{3,4},{4,3},{5,2},{10,13},{11,12},{12,11},{13,10},{18,21},{1... | collective-permute-start | bytes 430088 | tf_op jit(solution)/shard_map/ppermute | solution.py:565
  7.5 0.1 copy.12
  7.6 0.1 pad.4.refs_0_.text_ref
  7.8 10.6 %collective-permute-done.6.peer_ref = bf16[3,96,896]{2,1,0:T(8,128)(2,1)S(1)} collective-permute-done((bf16[3,96,896]{2,1,0:T(8,128)(2,1)S(1)}, bf16[3,96,896]{2,1,0:T(8,128)(2,1)S(1)}, u32[]{:S(2)}, u32[]{:S(2)}) %collective-permute-start.6) | collective-permute-done | bytes 516128 | tf_op jit(solution)/shard_map/ppermute | solution.py:540
  18.3 0.2 shard_map.104
  18.6 6.7 %collective-permute-done.peer_ref = bf16[3,96,640]{2,1,0:T(8,128)(2,1)S(1)} collective-permute-done((bf16[3,96,640]{2,1,0:T(8,128)(2,1)S(1)}, bf16[3,96,640]{2,1,0:T(8,128)(2,1)S(1)}, u32[]{:S(2)}, u32[]{:S(2)}) %collective-permute-start) | collective-permute-done | bytes 368672 | tf_op jit(solution)/shard_map/ppermute | solution.py:568
  25.4 0.8 %collective-permute-start.4 = (bf16[2,40,640]{2,1,0:T(8,128)(2,1)S(1)}, bf16[2,40,640]{2,1,0:T(8,128)(2,1)S(1)}, u32[]{:S(2)}, u32[]{:S(2)}) collective-permute-start(bf16[2,40,640]{2,1,0:T(8,128)(2,1)S(1)} %get-tuple-element.27), channel_id=1, source_target_pairs={{2,5},{3,4},{4,3},{5,2},{10,13},{11,12},{12,11},{13,10},{18,21},{1... | collective-permute-start | bytes 307208 | tf_op jit(solution)/shard_map/ppermute | solution.py:565
  26.2 0.2 shard_map.102
  26.3 4.1 %collective-permute-start.3 = (bf16[2,40,640]{2,1,0:T(8,128)(2,1)S(1)}, bf16[2,40,640]{2,1,0:T(8,128)(2,1)S(1)}, u32[]{:S(2)}, u32[]{:S(2)}) collective-permute-start(bf16[2,40,640]{2,1,0:T(8,128)(2,1)S(1)} %shard_map.102), channel_id=1, source_target_pairs={{0,2},{2,0},{4,6},{6,4},{1,3},{3,1},{5,7},{7,5},{8,10},{10,8},{12,... | collective-permute-start | bytes 307208 | tf_op jit(solution)/shard_map/ppermute | solution.py:606
  30.5 2.0 %prepare.1 = (f32[9,192,640]{2,1,0:T(8,128)S(1)}, f32[12,1,128]{2,1,0:T(1,128)S(1)}, f32[192,128]{1,0:T(8,128)S(1)}) custom-call(s32[2,2,4]{2,1,0:T(2,128)S(1)} %bitcast.13, s32[8,640]{1,0:T(8,128)S(1)} %copy-done.3, s32[192,8]{1,0:T(8,128)S(1)} %copy-done.2, bf16[1,512]{1,0:T(2,128)(2,1)S(1)} %reshape.14.time_ref, bf16[512,1536]{1,0:T(8,128)(2,1)S(1)} %copy-done), custom_call_target="tpu_custom_call" | custom-call | tf_op jit(solution)/shard_map/prepare/pallas_call | solution.py:569
  32.5 4.2 %shard_map.105 = (bf16[96,896]{1,0:T(8,128)(2,1)S(1)}, bf16[96,896]{1,0:T(8,128)(2,1)S(1)}) custom-call(s32[2,48]{1,0:T(2,128)S(1)} %bitcast.11, bf16[1,96,1536]{2,1,0:T(8,128)(2,1)S(1)} %get-tuple-element.19.mine_q_ref, bf16[2,96,1536]{2,1,0:T(8,128)(2,1)S(1)} %get-tuple-element.20.mine_ref.mine_kv_ref, ...), custom_call_target="tpu_custom_call" | custom-call | tf_op jit(solution)/shard_map/pallas_call | solution.py:608
  36.7 0.6 %collective-permute-start.9 = (bf16[96,896]{1,0:T(8,128)(2,1)S(1)}, bf16[96,896]{1,0:T(8,128)(2,1)S(1)}, u32[]{:S(2)}, u32[]{:S(2)}) collective-permute-start(bf16[96,896]{1,0:T(8,128)(2,1)S(1)} %get-tuple-element.32), channel_id=1, source_target_pairs={{0,1},{1,0},{2,3},{3,2},{4,5},{5,4},{6,7},{7,6},{8,9},{9,8},{10,11... | collective-permute-start | bytes 516104 | tf_op jit(solution)/shard_map/ppermute | solution.py:636
  37.3 3.1 %shard_map.103 = (bf16[96,640]{1,0:T(8,128)(2,1)S(1)}, bf16[96,640]{1,0:T(8,128)(2,1)S(1)}) custom-call(s32[2,48]{1,0:T(2,128)S(1)} %bitcast.12, bf16[1,96,1536]{2,1,0:T(8,128)(2,1)S(1)} %get-tuple-element.19.mine_q_ref, bf16[2,96,1536]{2,1,0:T(8,128)(2,1)S(1)} %get-tuple-element.20.mine_ref.mine_kv_ref, ...), custom_call_target="tpu_custom_call" | custom-call | tf_op jit(solution)/shard_map/pallas_call | solution.py:608
  40.4 1.6 %collective-permute-start.5 = (bf16[96,640]{1,0:T(8,128)(2,1)S(1)}, bf16[96,640]{1,0:T(8,128)(2,1)S(1)}, u32[]{:S(2)}, u32[]{:S(2)}) collective-permute-start(bf16[96,640]{1,0:T(8,128)(2,1)S(1)} %get-tuple-element.28), channel_id=1, source_target_pairs={{0,1},{1,0},{2,3},{3,2},{4,5},{5,4},{6,7},{7,6},{8,9},{9,8},{10,11... | collective-permute-start | bytes 368648 | tf_op jit(solution)/shard_map/ppermute | solution.py:636
  42.0 1.3 %collective-permute-done.9.refs_2_ = bf16[96,896]{1,0:T(8,128)(2,1)S(1)} collective-permute-done((bf16[96,896]{1,0:T(8,128)(2,1)S(1)}, bf16[96,896]{1,0:T(8,128)(2,1)S(1)}, u32[]{:S(2)}, u32[]{:S(2)}) %collective-permute-start.9) | collective-permute-done | bytes 172064 | tf_op jit(solution)/shard_map/ppermute | solution.py:636
  43.4 0.8 %shard_map.106.refs_1_ = bf16[96,3072]{1,0:T(8,128)(2,1)} custom-call(bf16[96,896]{1,0:T(8,128)(2,1)S(1)} %get-tuple-element.30.refs_0_, bf16[96,640]{1,0:T(8,128)(2,1)S(1)} %get-tuple-element.31.refs_1_, bf16[96,896]{1,0:T(8,128)(2,1)S(1)} %collective-permute-done.9.refs_2_), custom_call_target="tpu_custom_call" | custom-call | tf_op jit(solution)/shard_map/pallas_call | solution.py:465
  44.1 1.6 %collective-permute-done.5.refs_0_ = bf16[96,640]{1,0:T(8,128)(2,1)S(1)} collective-permute-done((bf16[96,640]{1,0:T(8,128)(2,1)S(1)}, bf16[96,640]{1,0:T(8,128)(2,1)S(1)}, u32[]{:S(2)}, u32[]{:S(2)}) %collective-permute-start.5) | collective-permute-done | bytes 122912 | tf_op jit(solution)/shard_map/ppermute | solution.py:636
  45.7 0.7 %shard_map.107 = bf16[96,3072]{1,0:T(8,128)(2,1)} custom-call(bf16[96,640]{1,0:T(8,128)(2,1)S(1)} %collective-permute-done.5.refs_0_, bf16[96,3072]{1,0:T(8,128)(2,1)} %shard_map.106.refs_1_), custom_call_target="tpu_custom_call", output_to_operand_aliasing={{}: (1, {})} | custom-call | tf_op jit(solution)/shard_map/pallas_call | solution.py:465
  (25 shorter events, 0.2 us)
Async XLA Ops:
  0.0 5.6 %copy-start.1 = (bf16[2,80,96]{2,1,0:T(8,128)(2,1)S(1)}, bf16[2,80,96]{2,1,0:T(8,128)(2,1)}, u32[]{:S(2)}) copy-start(bf16[2,80,96]{2,1,0:T(8,128)(2,1)} %constant.9.clone.select_ref) | copy-start | bytes 92164
  1.1 6.4 %copy-start.6 = (bf16[2,226,1536]{2,0,1:T(2,128)(2,1)S(1)}, bf16[2,226,1536]{2,0,1:T(2,128)(2,1)}, u32[]{:S(2)}) copy-start(bf16[2,226,1536]{2,0,1:T(2,128)(2,1)} %param.12) | copy-start | bytes 4165636
  1.1 17.2 %collective-permute-start.6 = (bf16[3,96,896]{2,1,0:T(8,128)(2,1)S(1)}, bf16[3,96,896]{2,1,0:T(8,128)(2,1)S(1)}, u32[]{:S(2)}, u32[]{:S(2)}) collective-permute-start(bf16[3,96,896]{2,1,0:T(8,128)(2,1)S(1)} %shard_map.101.early_ref), channel_id=1, source_target_pairs={{0,1},{1,0},{2,3},{3,2},{4,5},{5,4},{6,7},{7,6},{8,9},{9,8},{10,11... | collective-permute-start | bytes 1548296 | tf_op jit(solution)/shard_map/ppermute | solution.py:540
  5.5 19.9 %collective-permute-start = (bf16[3,96,640]{2,1,0:T(8,128)(2,1)S(1)}, bf16[3,96,640]{2,1,0:T(8,128)(2,1)S(1)}, u32[]{:S(2)}, u32[]{:S(2)}) collective-permute-start(bf16[3,96,640]{2,1,0:T(8,128)(2,1)S(1)} %get-tuple-element.21.late_ref), channel_id=1, source_target_pairs={{0,1},{1,0},{2,3},{3,2},{4,5},{5,4},{6,7},{7,6},{8,9},{9,8},{10,11... | collective-permute-start | bytes 1105928 | tf_op jit(solution)/shard_map/ppermute | solution.py:568
  6.0 26.4 %collective-permute-start.1 = (bf16[2,40,1536]{2,1,0:T(8,128)(2,1)S(1)}, bf16[2,40,1536]{2,1,0:T(8,128)(2,1)S(1)}, u32[]{:S(2)}, u32[]{:S(2)}) collective-permute-start(bf16[2,40,1536]{2,1,0:T(8,128)(2,1)S(1)} %get-tuple-element.22), channel_id=1, source_target_pairs={{0,2},{2,0},{4,6},{6,4},{1,3},{3,1},{5,7},{7,5},{8,10},{10,8},{12,... | collective-permute-start | bytes 737288 | tf_op jit(solution)/shard_map/ppermute | solution.py:566
  6.1 26.4 %collective-permute-start.2 = (bf16[2,40,1536]{2,1,0:T(8,128)(2,1)S(1)}, bf16[2,40,1536]{2,1,0:T(8,128)(2,1)S(1)}, u32[]{:S(2)}, u32[]{:S(2)}) collective-permute-start(bf16[2,40,1536]{2,1,0:T(8,128)(2,1)S(1)} %get-tuple-element.23), channel_id=1, source_target_pairs={{2,4},{4,2},{3,5},{5,3},{10,12},{12,10},{11,13},{13,11},{18,20},{2... | collective-permute-start | bytes 737288 | tf_op jit(solution)/shard_map/ppermute | solution.py:567
  6.8 19.5 %collective-permute-start.8 = (bf16[2,40,896]{2,1,0:T(8,128)(2,1)S(1)}, bf16[2,40,896]{2,1,0:T(8,128)(2,1)S(1)}, u32[]{:S(2)}, u32[]{:S(2)}) collective-permute-start(bf16[2,40,896]{2,1,0:T(8,128)(2,1)S(1)} %get-tuple-element.29), channel_id=1, source_target_pairs={{2,5},{3,4},{4,3},{5,2},{10,13},{11,12},{12,11},{13,10},{18,21},{1... | collective-permute-start | bytes 430088 | tf_op jit(solution)/shard_map/ppermute | solution.py:565
  18.5 11.9 %copy-start.7 = (bf16[512]{0:T(512)(128)(2,1)S(1)}, bf16[512]{0:T(512)(128)(2,1)}, u32[]{:S(2)}) copy-start(bf16[512]{0:T(512)(128)(2,1)} %param.13) | copy-start | bytes 3076
  18.5 11.9 %copy-start = (bf16[512,1536]{1,0:T(8,128)(2,1)S(1)}, bf16[512,1536]{1,0:T(8,128)(2,1)}, u32[]{:S(2)}) copy-start(bf16[512,1536]{1,0:T(8,128)(2,1)} %weight_ref.1) | copy-start | bytes 4718596
  18.5 11.9 %copy-start.2 = (s32[192,8]{1,0:T(8,128)S(1)}, s32[192,8]{1,0:T(8,128)}, u32[]{:S(2)}) copy-start(s32[192,8]{1,0:T(8,128)} %constant.11.clone.query_ref) | copy-start | bytes 18436
  18.5 11.9 %copy-start.3 = (s32[8,640]{1,0:T(8,128)S(1)}, s32[8,640]{1,0:T(8,128)}, u32[]{:S(2)}) copy-start(s32[8,640]{1,0:T(8,128)} %constant.10.clone.key_ref) | copy-start | bytes 61444
  18.6 11.9 %copy-start.5 = (s32[4,2,2]{0,2,1:T(2,128)S(1)}, s32[4,2,2]{0,2,1:T(2,128)}, u32[]{:S(2)}) copy-start(s32[4,2,2]{0,2,1:T(2,128)} %param.16) | copy-start | bytes 196
  18.6 13.9 %collective-permute-start.7 = (bf16[2,40,896]{2,1,0:T(8,128)(2,1)S(1)}, bf16[2,40,896]{2,1,0:T(8,128)(2,1)S(1)}, u32[]{:S(2)}, u32[]{:S(2)}) collective-permute-start(bf16[2,40,896]{2,1,0:T(8,128)(2,1)S(1)} %shard_map.104), channel_id=1, source_target_pairs={{0,2},{2,0},{4,6},{6,4},{1,3},{3,1},{5,7},{7,5},{8,10},{10,8},{12,... | collective-permute-start | bytes 430088 | tf_op jit(solution)/shard_map/ppermute | solution.py:606
  25.4 7.1 %copy-start.4 = (s32[48,2]{0,1:T(2,128)S(1)}, s32[48,2]{0,1:T(2,128)}, u32[]{:S(2)}) copy-start(s32[48,2]{0,1:T(2,128)} %param.15) | copy-start | bytes 1156
  25.4 11.9 %collective-permute-start.4 = (bf16[2,40,640]{2,1,0:T(8,128)(2,1)S(1)}, bf16[2,40,640]{2,1,0:T(8,128)(2,1)S(1)}, u32[]{:S(2)}, u32[]{:S(2)}) collective-permute-start(bf16[2,40,640]{2,1,0:T(8,128)(2,1)S(1)} %get-tuple-element.27), channel_id=1, source_target_pairs={{2,5},{3,4},{4,3},{5,2},{10,13},{11,12},{12,11},{13,10},{18,21},{1... | collective-permute-start | bytes 307208 | tf_op jit(solution)/shard_map/ppermute | solution.py:565
  26.3 11.0 %collective-permute-start.3 = (bf16[2,40,640]{2,1,0:T(8,128)(2,1)S(1)}, bf16[2,40,640]{2,1,0:T(8,128)(2,1)S(1)}, u32[]{:S(2)}, u32[]{:S(2)}) collective-permute-start(bf16[2,40,640]{2,1,0:T(8,128)(2,1)S(1)} %shard_map.102), channel_id=1, source_target_pairs={{0,2},{2,0},{4,6},{6,4},{1,3},{3,1},{5,7},{7,5},{8,10},{10,8},{12,... | collective-permute-start | bytes 307208 | tf_op jit(solution)/shard_map/ppermute | solution.py:606
  36.7 6.6 %collective-permute-start.9 = (bf16[96,896]{1,0:T(8,128)(2,1)S(1)}, bf16[96,896]{1,0:T(8,128)(2,1)S(1)}, u32[]{:S(2)}, u32[]{:S(2)}) collective-permute-start(bf16[96,896]{1,0:T(8,128)(2,1)S(1)} %get-tuple-element.32), channel_id=1, source_target_pairs={{0,1},{1,0},{2,3},{3,2},{4,5},{5,4},{6,7},{7,6},{8,9},{9,8},{10,11... | collective-permute-start | bytes 516104 | tf_op jit(solution)/shard_map/ppermute | solution.py:636
  40.4 5.3 %collective-permute-start.5 = (bf16[96,640]{1,0:T(8,128)(2,1)S(1)}, bf16[96,640]{1,0:T(8,128)(2,1)S(1)}, u32[]{:S(2)}, u32[]{:S(2)}) collective-permute-start(bf16[96,640]{1,0:T(8,128)(2,1)S(1)} %get-tuple-element.28), channel_id=1, source_target_pairs={{0,1},{1,0},{2,3},{3,2},{4,5},{5,4},{6,7},{7,6},{8,9},{9,8},{10,11... | collective-permute-start | bytes 368648 | tf_op jit(solution)/shard_map/ppermute | solution.py:636
